TPU v7x, 32 devices: a whole 2x2x4 slice. The times are simulated.
32 devices in a mesh: ctx: 8 (over z, x), wsh: 4 (over y, core).
Axes of the slice: x: 2, y: 2, z: 4, core: 2. Of those that a mesh axis runs over, the one named last changes fastest.
Arguments:
- inputs: bfloat16 [2048, 2, 2048], P(('ctx', 'wsh')), may hold values from -6 to 6
- pair_map: int32 [8], replicated, may hold values from 0 to 7, each once
- norm_gain: float32 [2048], replicated, may hold values from 0.25 to 1.75
- query_weight: bfloat16 [2048, 4096], P('ctx', 'wsh'), may hold values from -0.125 to 0.125
- key_weight: bfloat16 [2048, 512], P('ctx', 'wsh'), may hold values from -0.125 to 0.125
- value_weight: bfloat16 [2048, 512], P('ctx', 'wsh'), may hold values from -0.125 to 0.125
- query_gain: float32 [128], replicated, may hold values from 0.5 to 2
- key_gain: float32 [128], replicated, may hold values from 0.5 to 2
- out_weight: bfloat16 [4096, 2048], P('wsh', 'ctx'), may hold values from -3 to 3
- moe_gain: float32 [2048], replicated, may hold values from 0.25 to 1.75
- router: bfloat16 [2048, 32], replicated
- expert_gate: bfloat16 [32, 2048, 768], P(('ctx', 'wsh')), may hold values from -0.125 to 0.125
- expert_up: bfloat16 [32, 2048, 768], P(('ctx', 'wsh')), may hold values from -0.125 to 0.125
- expert_down: bfloat16 [32, 768, 2048], P(('ctx', 'wsh')), may hold values from -0.21875 to 0.21875
- expert_ids: int32 [2048, 2, 8], P(('ctx', 'wsh')), may hold values from 0 to 31, as said below
- dispatch_slot: int32 [2048, 2, 8], P(('ctx', 'wsh')), may hold values from -1 to 47, as said below
- cotangent: float32 [2048, 2, 2048], P(('ctx', 'wsh')), may hold values from -6 to 6
Outputs:
- outputs: bfloat16 [2048, 2, 2048], P(('ctx', 'wsh'))
- input_grad: float32 [2048, 2, 2048], P(('ctx', 'wsh'))
- norm_gain_grad: float32 [2048], replicated
- query_weight_grad: float32 [2048, 4096], P('ctx', 'wsh')
- key_weight_grad: float32 [2048, 512], P('ctx', 'wsh')
- value_weight_grad: float32 [2048, 512], P('ctx', 'wsh')
- query_gain_grad: float32 [128], replicated
- key_gain_grad: float32 [128], replicated
- out_weight_grad: float32 [4096, 2048], P('wsh', 'ctx')
- moe_gain_grad: float32 [2048], replicated
- router_grad: float32 [2048, 32], replicated
- gate_grad: float32 [32, 2048, 768], P(('ctx', 'wsh'))
- up_grad: float32 [32, 2048, 768], P(('ctx', 'wsh'))
- down_grad: float32 [32, 768, 2048], P(('ctx', 'wsh'))
Inputs may be any that keep to these rules, and one draw needn't show every extreme that they name: `expert_ids`: each token names 8 different experts; in every draw one expert is named by every token. `dispatch_slot`: among the routes of the rows of one device to one expert, in token order, the first 48 hold the slots 0, 1, ... in that order and the others hold -1; in every draw some expert gets 48 routes from the rows of every device.
All inputs are finite; a program needn't handle non-finite values.
Results may differ from a plain program's by a relative error of at most 0.02.
Values may be sent and summed in bfloat16 or wider, within the bound.
A program may use at most 256 MiB of HBM per device.

v0:
```python
import math

import jax
import jax.numpy as jnp
from jax import lax
from jax.sharding import PartitionSpec as P

EPSILON = 1e-06
ROPE_BASE = 1000000.0
MASKED = -1e30


def positions_of(pair_map, seq_len, block_len, group_count):
    row_index = jnp.arange(seq_len, dtype=jnp.int32)
    owner_group = row_index // (2 * block_len)
    inner_row = row_index % (2 * block_len)
    group_table = jnp.arange(group_count, dtype=jnp.int32)
    pair_index = jnp.sum(
        jnp.where(owner_group[:, None] == group_table[None, :], pair_map[None, :], 0), axis=1
    )
    block_index = jnp.where(inner_row < block_len, pair_index, 2 * group_count - 1 - pair_index)
    return block_index * block_len + inner_row % block_len


def rope_tables(positions, head_dim):
    half_dim = head_dim // 2
    frequency = ROPE_BASE ** (-(jnp.arange(half_dim, dtype=jnp.float32) * 2.0) / head_dim)
    angles = positions.astype(jnp.float32)[:, None] * frequency[None, :]
    return (jnp.cos(angles), jnp.sin(angles))


def rotate(tensor, cosine, sine_table):
    half_dim = tensor.shape[-1] // 2
    first_half = tensor[..., :half_dim]
    second_half = tensor[..., half_dim:]
    return jnp.concatenate(
        [
            first_half * cosine - second_half * sine_table,
            second_half * cosine + first_half * sine_table,
        ],
        axis=-1,
    )


def unrotate(gradient, cosine, sine_table):
    half_dim = gradient.shape[-1] // 2
    first_half = gradient[..., :half_dim]
    second_half = gradient[..., half_dim:]
    return jnp.concatenate(
        [
            first_half * cosine + second_half * sine_table,
            second_half * cosine - first_half * sine_table,
        ],
        axis=-1,
    )


def rms_forward(tensor, gain_vector):
    inverse = lax.rsqrt(jnp.mean(tensor * tensor, axis=-1, keepdims=True) + EPSILON)
    return (tensor * inverse * gain_vector, inverse)


def rms_backward(tensor, inverse, gain_vector, gradient):
    weighted = gradient * gain_vector
    inner_mean = jnp.mean(weighted * tensor, axis=-1, keepdims=True)
    tensor_grad = inverse * weighted - tensor * inverse**3 * inner_mean
    gain_grad = jnp.sum((gradient * tensor * inverse).reshape(-1, tensor.shape[-1]), axis=0)
    return (tensor_grad, gain_grad)


def expert_forward(rows_in, gate_w, up_w, down_w):
    gate_pre = jnp.dot(rows_in, gate_w, preferred_element_type=jnp.float32)
    up_pre = jnp.dot(rows_in, up_w, preferred_element_type=jnp.float32)
    activation = (gate_pre * jax.nn.sigmoid(gate_pre) * up_pre).astype(jnp.bfloat16)
    return jnp.dot(activation, down_w, preferred_element_type=jnp.float32).astype(jnp.bfloat16)


def expert_backward(rows_in, route_cot, gate_w, up_w, down_w):
    gate_pre = jnp.dot(rows_in, gate_w, preferred_element_type=jnp.float32)
    up_pre = jnp.dot(rows_in, up_w, preferred_element_type=jnp.float32)
    sigmoid = jax.nn.sigmoid(gate_pre)
    swish = gate_pre * sigmoid
    activation = (swish * up_pre).astype(jnp.bfloat16)
    down_grad = jnp.einsum("rf,rd->fd", activation, route_cot, preferred_element_type=jnp.float32)
    act_cot = jnp.einsum("rd,fd->rf", route_cot, down_w, preferred_element_type=jnp.float32)
    gate_cot = (act_cot * up_pre * sigmoid * (1.0 + gate_pre * (1.0 - sigmoid))).astype(
        jnp.bfloat16
    )
    up_cot = (act_cot * swish).astype(jnp.bfloat16)
    gate_grad = jnp.einsum("rd,rf->df", rows_in, gate_cot, preferred_element_type=jnp.float32)
    up_grad = jnp.einsum("rd,rf->df", rows_in, up_cot, preferred_element_type=jnp.float32)
    row_cot = jnp.einsum("rf,df->rd", gate_cot, gate_w, preferred_element_type=jnp.float32)
    row_cot = row_cot + jnp.einsum("rf,df->rd", up_cot, up_w, preferred_element_type=jnp.float32)
    return (row_cot.astype(jnp.bfloat16), gate_grad, up_grad, down_grad)


def score_block(query_rot, key_piece, scaling):
    return (
        jnp.einsum("qsagd,ksad->sagqk", query_rot, key_piece, preferred_element_type=jnp.float32)
        * scaling
    )


def attend_keys(query_rot, query_pos, key_all, value_all, key_pos, scaling):
    length = key_all.shape[0]
    key_block = math.gcd(length, 512)
    block_count = length // key_block
    query_rows, seq_count, kv_count, group, head_dim = query_rot.shape
    start_carry = (
        jnp.full((seq_count, kv_count, group, query_rows), MASKED, jnp.float32),
        jnp.zeros((seq_count, kv_count, group, query_rows), jnp.float32),
        jnp.zeros((seq_count, kv_count, group, query_rows, head_dim), jnp.float32),
    )

    def step(block_id, carry):
        row_top, row_total, accum = carry
        start = block_id * key_block
        key_piece = lax.dynamic_slice_in_dim(key_all, start, key_block, 0)
        value_piece = lax.dynamic_slice_in_dim(value_all, start, key_block, 0)
        piece_pos = lax.dynamic_slice_in_dim(key_pos, start, key_block, 0)
        scores = score_block(query_rot, key_piece, scaling)
        allowed = piece_pos[None, :] <= query_pos[:, None]
        new_top = jnp.maximum(row_top, jnp.max(jnp.where(allowed, scores, MASKED), axis=-1))
        expo = jnp.where(allowed, jnp.exp(scores - new_top[..., None]), 0.0)
        decay = jnp.exp(row_top - new_top)
        row_total = row_total * decay + jnp.sum(expo, axis=-1)
        accum = accum * decay[..., None] + jnp.einsum(
            "sagqk,ksad->sagqd",
            expo.astype(jnp.bfloat16),
            value_piece,
            preferred_element_type=jnp.float32,
        )
        return (new_top, row_total, accum)

    return lax.fori_loop(0, block_count, step, start_carry)


def attend_grads(
    query_rot, query_pos, key_all, value_all, key_pos, attn_cot, delta, log_total, scaling
):
    length = key_all.shape[0]
    key_block = math.gcd(length, 512)
    block_count = length // key_block
    query_rows, seq_count, kv_count, group, head_dim = query_rot.shape

    def step(query_cot, block_id):
        start = block_id * key_block
        key_piece = lax.dynamic_slice_in_dim(key_all, start, key_block, 0)
        value_piece = lax.dynamic_slice_in_dim(value_all, start, key_block, 0)
        piece_pos = lax.dynamic_slice_in_dim(key_pos, start, key_block, 0)
        scores = score_block(query_rot, key_piece, scaling)
        allowed = piece_pos[None, :] <= query_pos[:, None]
        weights_back = jnp.where(allowed, jnp.exp(scores - log_total[..., None]), 0.0)
        prob_cot = jnp.einsum(
            "qsagd,ksad->sagqk", attn_cot, value_piece, preferred_element_type=jnp.float32
        )
        score_cot = weights_back * (prob_cot - delta[..., None])
        value_cot = jnp.einsum(
            "sagqk,qsagd->ksad",
            weights_back.astype(jnp.bfloat16),
            attn_cot,
            preferred_element_type=jnp.float32,
        )
        score_low = score_cot.astype(jnp.bfloat16)
        query_cot = (
            query_cot
            + jnp.einsum(
                "sagqk,ksad->qsagd", score_low, key_piece, preferred_element_type=jnp.float32
            )
            * scaling
        )
        key_cot = (
            jnp.einsum(
                "sagqk,qsagd->ksad", score_low, query_rot, preferred_element_type=jnp.float32
            )
            * scaling
        )
        return (query_cot, (key_cot, value_cot))

    start_carry = jnp.zeros((query_rows, seq_count, kv_count, group, head_dim), jnp.float32)
    query_cot, (key_cot, value_cot) = lax.scan(
        step, start_carry, jnp.arange(block_count, dtype=jnp.int32)
    )
    return (
        query_cot,
        key_cot.reshape(length, seq_count, kv_count * head_dim),
        value_cot.reshape(length, seq_count, kv_count * head_dim),
    )


def local(
    inputs,
    pair_map,
    norm_gain,
    query_weight,
    key_weight,
    value_weight,
    query_gain,
    key_gain,
    out_weight,
    moe_gain,
    router,
    expert_gate,
    expert_up,
    expert_down,
    expert_ids,
    dispatch_slot,
    cotangent,
):
    rows_dev, seq_count, width = inputs.shape
    ctx_count = lax.axis_size("ctx")
    wsh_count = lax.axis_size("wsh")
    device_count = ctx_count * wsh_count
    head_dim = query_gain.shape[0]
    group_rows = rows_dev * wsh_count
    block_len = group_rows // 2
    seq_len = group_rows * ctx_count
    top_count = expert_ids.shape[-1]
    expert_count = router.shape[1]
    capacity = max(2, 3 * top_count * block_len // (2 * device_count))
    scaling = head_dim ** (-0.5)
    positions = positions_of(pair_map, seq_len, block_len, pair_map.shape[0])
    query_pos = lax.dynamic_slice_in_dim(
        positions, lax.axis_index("ctx") * group_rows, group_rows, 0
    )
    cosine, sine_table = rope_tables(query_pos, head_dim)
    cosine = cosine[:, None, None, :]
    sine_table = sine_table[:, None, None, :]
    query_full, key_full, value_full, out_full = (
        lax.all_gather(query_weight, "ctx", axis=0, tiled=True),
        lax.all_gather(key_weight, "ctx", axis=0, tiled=True),
        lax.all_gather(value_weight, "ctx", axis=0, tiled=True),
        lax.all_gather(out_weight, "ctx", axis=1, tiled=True),
    )
    heads_loc = query_full.shape[1] // head_dim
    kv_loc = key_full.shape[1] // head_dim
    group = heads_loc // kv_loc
    inputs_f = inputs.astype(jnp.float32)
    normed_f, inverse_one = rms_forward(inputs_f, norm_gain)
    normed = normed_f.astype(jnp.bfloat16)
    normed_group = lax.all_gather(normed, "wsh", axis=0, tiled=True)
    normed_flat = normed_group.reshape(group_rows * seq_count, width)
    queries = jnp.dot(normed_flat, query_full, preferred_element_type=jnp.float32).reshape(
        group_rows, seq_count, heads_loc, head_dim
    )
    keys_raw = jnp.dot(normed_flat, key_full, preferred_element_type=jnp.float32).reshape(
        group_rows, seq_count, kv_loc, head_dim
    )
    value_rows = (
        jnp.dot(normed_flat, value_full, preferred_element_type=jnp.float32)
        .astype(jnp.bfloat16)
        .reshape(group_rows, seq_count, kv_loc * head_dim)
    )
    query_normed, query_inverse = rms_forward(queries, query_gain)
    key_normed, key_inverse = rms_forward(keys_raw, key_gain)
    query_rot = (
        rotate(query_normed, cosine, sine_table)
        .astype(jnp.bfloat16)
        .reshape(group_rows, seq_count, kv_loc, group, head_dim)
    )
    key_rot = (
        rotate(key_normed, cosine, sine_table)
        .astype(jnp.bfloat16)
        .reshape(group_rows, seq_count, kv_loc * head_dim)
    )
    key_all, value_all = (
        lax.all_gather(key_rot, "ctx", axis=0, tiled=True),
        lax.all_gather(value_rows, "ctx", axis=0, tiled=True),
    )
    key_all = key_all.reshape(seq_len, seq_count, kv_loc, head_dim)
    value_all = value_all.reshape(seq_len, seq_count, kv_loc, head_dim)
    row_top, row_total, accum = attend_keys(
        query_rot, query_pos, key_all, value_all, positions, scaling
    )
    log_total = row_top + jnp.log(row_total)
    attention = (accum / row_total[..., None]).astype(jnp.bfloat16)
    attention_rows = attention.transpose(3, 0, 1, 2, 4).reshape(
        group_rows, seq_count, heads_loc * head_dim
    )
    count = rows_dev * lax.axis_size("wsh")
    residual = inputs_f + lax.psum_scatter(
        jnp.dot(
            attention_rows.reshape(count * seq_count, -1),
            out_full,
            preferred_element_type=jnp.float32,
        ).reshape(count, seq_count, width),
        "wsh",
        scatter_dimension=0,
        tiled=True,
    )
    tokens = rows_dev * seq_count
    moe_normed_f, inverse_two = rms_forward(residual, moe_gain)
    moe_flat = moe_normed_f.astype(jnp.bfloat16).reshape(tokens, width)
    logits = jnp.dot(moe_flat, router, preferred_element_type=jnp.float32)
    route_ids = expert_ids.reshape(tokens, top_count)
    slots = dispatch_slot.reshape(tokens, top_count)
    expert_onehot = (
        route_ids[:, :, None] == jnp.arange(expert_count, dtype=jnp.int32)[None, None, :]
    )
    chosen = jnp.sum(jnp.where(expert_onehot, logits[:, None, :], 0.0), axis=-1)
    chosen_top = jnp.max(chosen, axis=-1, keepdims=True)
    chosen_exp = jnp.exp(chosen - chosen_top)
    route_weight = chosen_exp / jnp.sum(chosen_exp, axis=-1, keepdims=True)
    kept_route = slots >= 0
    placement = jnp.where(
        kept_route, route_ids * capacity + slots, expert_count * capacity
    ).reshape(-1)
    safe_place = jnp.where(kept_route, route_ids * capacity + slots, 0).reshape(-1)
    route_rows = jnp.broadcast_to(moe_flat[:, None, :], (tokens, top_count, width)).reshape(
        -1, width
    )
    send_rows = (
        jnp.zeros((expert_count * capacity, width), jnp.bfloat16)
        .at[placement]
        .set(route_rows, mode="drop")
    )
    send_rows = send_rows.reshape(device_count, capacity, width)
    gate_local, up_local, down_local = (expert_gate[0], expert_up[0], expert_down[0])
    received = lax.all_to_all(send_rows, ("ctx", "wsh"), split_axis=0, concat_axis=0, tiled=True)
    produced = expert_forward(
        received.reshape(-1, width), gate_local, up_local, down_local
    ).reshape(received.shape)
    dispatched = produced
    produced = dispatched
    returned = lax.all_to_all(produced, ("ctx", "wsh"), split_axis=0, concat_axis=0, tiled=True)
    route_out = returned.reshape(-1, width)[safe_place].reshape(tokens, top_count, width)
    route_float = jnp.where(kept_route[..., None], route_out.astype(jnp.float32), 0.0)
    moe_sum = jnp.sum(route_weight[..., None] * route_float, axis=1)
    outputs = (
        (residual.reshape(tokens, width) + moe_sum)
        .reshape(rows_dev, seq_count, width)
        .astype(jnp.bfloat16)
    )
    cot_flat = cotangent.reshape(tokens, width)
    weight_cot = jnp.sum(cot_flat[:, None, :] * route_float, axis=-1)
    chosen_cot = route_weight * (
        weight_cot - jnp.sum(route_weight * weight_cot, axis=-1, keepdims=True)
    )
    logit_cot = jnp.sum(jnp.where(expert_onehot, chosen_cot[:, :, None], 0.0), axis=1).astype(
        jnp.bfloat16
    )
    router_grad = jnp.einsum("td,te->de", moe_flat, logit_cot, preferred_element_type=jnp.float32)
    normed_two_cot = jnp.einsum("te,de->td", logit_cot, router, preferred_element_type=jnp.float32)
    route_cot = (
        (route_weight[..., None] * cot_flat[:, None, :]).astype(jnp.bfloat16).reshape(-1, width)
    )
    cot_send = (
        jnp.zeros((expert_count * capacity, width), jnp.bfloat16)
        .at[placement]
        .set(route_cot, mode="drop")
    )
    cot_send = cot_send.reshape(device_count, capacity, width)
    cot_rows, input_rows = (
        lax.all_to_all(cot_send, ("ctx", "wsh"), split_axis=0, concat_axis=0, tiled=True),
        lax.all_to_all(send_rows, ("ctx", "wsh"), split_axis=0, concat_axis=0, tiled=True),
    )
    row_cot, gate_grad, up_grad, down_grad = expert_backward(
        input_rows.reshape(-1, width), cot_rows.reshape(-1, width), gate_local, up_local, down_local
    )
    rows_back = lax.all_to_all(
        row_cot.reshape(device_count, capacity, width),
        ("ctx", "wsh"),
        split_axis=0,
        concat_axis=0,
        tiled=True,
    )
    back_routes = rows_back.reshape(-1, width)[safe_place].reshape(tokens, top_count, width)
    normed_two_cot = normed_two_cot + jnp.sum(
        jnp.where(kept_route[..., None], back_routes.astype(jnp.float32), 0.0), axis=1
    )
    residual_norm_cot, moe_gain_grad = rms_backward(
        residual, inverse_two, moe_gain, normed_two_cot.reshape(rows_dev, seq_count, width)
    )
    residual_cot = cotangent + residual_norm_cot
    residual_low = residual_cot.astype(jnp.bfloat16)
    residual_group = lax.all_gather(residual_low, "wsh", axis=0, tiled=True)
    residual_flat = residual_group.reshape(group_rows * seq_count, width)
    attention_flat = attention_rows.reshape(group_rows * seq_count, -1)
    out_weight_grad = jnp.einsum(
        "tc,td->cd", attention_flat, residual_flat, preferred_element_type=jnp.float32
    )
    attention_cot = jnp.einsum(
        "td,cd->tc", residual_flat, out_full, preferred_element_type=jnp.float32
    ).astype(jnp.bfloat16)
    attention_cot = attention_cot.reshape(group_rows, seq_count, kv_loc, group, head_dim)
    attention_q = attention_rows.reshape(group_rows, seq_count, kv_loc, group, head_dim)
    delta = jnp.sum(
        attention_cot.astype(jnp.float32) * attention_q.astype(jnp.float32), axis=-1
    ).transpose(1, 2, 3, 0)
    query_rot_cot, key_cot_all, value_cot_all = attend_grads(
        query_rot,
        query_pos,
        key_all,
        value_all,
        positions,
        attention_cot,
        delta,
        log_total,
        scaling,
    )
    key_cot_own, value_cot_own = (
        lax.psum_scatter(key_cot_all, "ctx", scatter_dimension=0, tiled=True),
        lax.psum_scatter(value_cot_all, "ctx", scatter_dimension=0, tiled=True),
    )
    query_cot, query_gain_grad = rms_backward(
        queries,
        query_inverse,
        query_gain,
        unrotate(
            query_rot_cot.reshape(group_rows, seq_count, heads_loc, head_dim), cosine, sine_table
        ),
    )
    key_cot, key_gain_grad = rms_backward(
        keys_raw,
        key_inverse,
        key_gain,
        unrotate(key_cot_own.reshape(group_rows, seq_count, kv_loc, head_dim), cosine, sine_table),
    )
    query_low = query_cot.astype(jnp.bfloat16).reshape(group_rows, seq_count, heads_loc * head_dim)
    key_low = key_cot.astype(jnp.bfloat16).reshape(group_rows, seq_count, kv_loc * head_dim)
    value_low = value_cot_own.astype(jnp.bfloat16)
    query_weight_grad = jnp.einsum(
        "tc,tq->cq",
        normed_flat,
        query_low.reshape(group_rows * seq_count, -1),
        preferred_element_type=jnp.float32,
    )
    key_weight_grad = jnp.einsum(
        "tc,tq->cq",
        normed_flat,
        key_low.reshape(group_rows * seq_count, -1),
        preferred_element_type=jnp.float32,
    )
    value_weight_grad = jnp.einsum(
        "tc,tq->cq",
        normed_flat,
        value_low.reshape(group_rows * seq_count, -1),
        preferred_element_type=jnp.float32,
    )
    count = rows_dev * lax.axis_size("wsh")
    query_piece = query_low.reshape(count * seq_count, -1)
    key_piece = key_low.reshape(count * seq_count, -1)
    value_piece = value_low.reshape(count * seq_count, -1)
    summed = jnp.einsum("tq,cq->tc", query_piece, query_full, preferred_element_type=jnp.float32)
    summed = summed + jnp.einsum(
        "tq,cq->tc", key_piece, key_full, preferred_element_type=jnp.float32
    )
    summed = summed + jnp.einsum(
        "tq,cq->tc", value_piece, value_full, preferred_element_type=jnp.float32
    )
    normed_cot = lax.psum_scatter(
        summed.reshape(count, seq_count, width).astype(jnp.bfloat16),
        "wsh",
        scatter_dimension=0,
        tiled=True,
    ).astype(jnp.float32)
    input_norm_cot, norm_gain_grad = rms_backward(inputs_f, inverse_one, norm_gain, normed_cot)
    input_grad = residual_cot + input_norm_cot
    query_weight_grad, key_weight_grad, value_weight_grad, out_weight_grad = (
        lax.psum_scatter(
            query_weight_grad.astype(jnp.bfloat16), "ctx", scatter_dimension=0, tiled=True
        ).astype(jnp.float32),
        lax.psum_scatter(
            key_weight_grad.astype(jnp.bfloat16), "ctx", scatter_dimension=0, tiled=True
        ).astype(jnp.float32),
        lax.psum_scatter(
            value_weight_grad.astype(jnp.bfloat16), "ctx", scatter_dimension=0, tiled=True
        ).astype(jnp.float32),
        lax.psum_scatter(
            out_weight_grad.astype(jnp.bfloat16), "ctx", scatter_dimension=1, tiled=True
        ).astype(jnp.float32),
    )
    norm_gain_grad, query_gain_grad, key_gain_grad, moe_gain_grad, router_grad = lax.psum(
        (norm_gain_grad, query_gain_grad, key_gain_grad, moe_gain_grad, router_grad), ("ctx", "wsh")
    )
    return (
        outputs,
        input_grad,
        norm_gain_grad,
        query_weight_grad,
        key_weight_grad,
        value_weight_grad,
        query_gain_grad,
        key_gain_grad,
        out_weight_grad,
        moe_gain_grad,
        router_grad,
        gate_grad[None],
        up_grad[None],
        down_grad[None],
    )


def solution(mesh):
    return jax.shard_map(
        local,
        mesh=mesh,
        in_specs=(
            P(("ctx", "wsh"), None, None),
            P(),
            P(),
            P("ctx", "wsh"),
            P("ctx", "wsh"),
            P("ctx", "wsh"),
            P(),
            P(),
            P("wsh", "ctx"),
            P(),
            P(),
            P(("ctx", "wsh"), None, None),
            P(("ctx", "wsh"), None, None),
            P(("ctx", "wsh"), None, None),
            P(("ctx", "wsh"), None, None),
            P(("ctx", "wsh"), None, None),
            P(("ctx", "wsh"), None, None),
        ),
        out_specs=(
            P(("ctx", "wsh"), None, None),
            P(("ctx", "wsh"), None, None),
            P(),
            P("ctx", "wsh"),
            P("ctx", "wsh"),
            P("ctx", "wsh"),
            P(),
            P(),
            P("wsh", "ctx"),
            P(),
            P(),
            P(("ctx", "wsh"), None, None),
            P(("ctx", "wsh"), None, None),
            P(("ctx", "wsh"), None, None),
        ),
        check_vma=False,
    )
```

profile of v0, /device:TPU:0, one launch (start us, length us, event | category | flops | bytes accessed | tf_op | source)
XLA Modules:
  0.0 1749.2 jit_solution(18030187476264747940)
XLA Ops:
  14.7 35.4 %all_gather.25 = bf16[2048,128]{1,0:T(8,128)(2,1)} all-gather(bf16[256,128]{1,0:T(8,128)(2,1)} %param.25), channel_id=1, replica_groups=mesh['ctx'=8,'wsh'=4] {'ctx'}, dimensions={0}, use_global_device_ids=true | all-gather | bytes 589824 | tf_op jit(solution)/shard_map/all_gather | solution.py:231
  67.6 33.8 %all_gather.28 = bf16[2048,128]{1,0:T(8,128)(2,1)S(1)} all-gather(bf16[256,128]{1,0:T(8,128)(2,1)} %param.26), channel_id=1, replica_groups=mesh['ctx'=8,'wsh'=4] {'ctx'}, dimensions={0}, use_global_device_ids=true | all-gather | bytes 589824 | tf_op jit(solution)/shard_map/all_gather | solution.py:232
  106.1 12.7 all-gather.11.cloned.1.call-done
  118.9 6.4 copy.137
  136.0 25.3 %all-gather.9.cloned.1.call-done = bf16[2048,2,128]{2,0,1:T(8,128)(2,1)} async-done(((bf16[256,2,128]{2,0,1:T(8,128)(2,1)}), bf16[2048,2,128]{2,0,1:T(8,128)(2,1)}) %all-gather.9.cloned.1.call-update) | async-done | bytes 1048592 | tf_op jit(solution)/shard_map/all_gather | solution.py:267
  161.3 41.6 %all-gather.13.cloned.1.call-done = bf16[2048,2,128]{2,0,1:T(8,128)(2,1)} async-done(((bf16[256,2,128]{2,0,1:T(8,128)(2,1)}), bf16[2048,2,128]{2,0,1:T(8,128)(2,1)}) %all-gather.13.cloned.1.call-update) | async-done | bytes 1048592 | tf_op jit(solution)/shard_map/all_gather | solution.py:268
  202.9 64.1 %while.33 = (s32[]{:T(128)}, f32[2,1,8,256]{3,2,0,1:T(8,128)S(1)}, f32[2,1,8,256]{3,2,0,1:T(8,128)S(1)}, f32[2,1,8,256,128]{4,3,2,0,1:T(8,128)}, s32[2048]{0:T(1...) while((s32[]{:T(128)}, f32[2,1,8,256]{3,2,0,1:T(8,128)S(1)}, ...), condition=%wide.region_7.8_spmd.clone, body=%wide.region_4.7_spmd.clone.sunk | while | flops 1098539008 | bytes 65281244 | solution.py:135
  203.1 5.9 fusion.192
  209.1 7.8 bitcast_add_fusion.7
  218.9 5.9 fusion.192
  224.9 8.1 bitcast_add_fusion.7
  235.0 5.9 fusion.192
  240.9 8.2 bitcast_add_fusion.7
  251.2 5.9 fusion.192
  257.1 8.1 bitcast_add_fusion.7
  278.2 6.9 fusion.68
  286.1 41.9 %reduce-scatter.9.cloned.1.call-done = f32[64,2,2048]{2,0,1:T(8,128)} async-done(((f32[256,2,2048]{2,0,1:T(8,128)}), f32[64,2,2048]{2,0,1:T(8,128)}) %reduce-scatter.9.cloned.1.call-update) | async-done | bytes 1048592 | tf_op jit(solution)/shard_map/reduce_scatter | solution.py:281
  334.2 10.7 scatter_custom_fusion
  354.5 11.1 scatter_custom_fusion.1
  365.6 124.2 %all-to-all-done = bf16[32,48,2048]{2,1,0:T(8,128)(2,1)} async-done(((bf16[32,48,2048]{2,1,0:T(8,128)(2,1)}), bf16[32,48,2048]{2,1,0:T(8,128)(2,1)}, u32[]{:S(2)}, u32[]{:S(2)}) %all-to-all-start) | async-done | bytes 6291488 | tf_op jit(solution)/shard_map/all_to_all | solution.py:319
  489.7 6.1 all-to-all-start.2
  495.8 9.6 fusion.76
  505.4 8.5 fusion.80
  514.0 121.8 %all-to-all-done.2 = bf16[32,48,2048]{2,1,0:T(8,128)(2,1)} async-done(((bf16[32,48,2048]{2,1,0:T(8,128)(2,1)}), bf16[32,48,2048]{2,1,0:T(8,128)(2,1)}, u32[]{:S(2)}, u32[]{:S(2)}) %all-to-all-start.2) | async-done | bytes 6291488 | tf_op jit(solution)/shard_map/all_to_all | solution.py:354
  635.8 12.2 multiply_convert_fusion
  648.0 8.2 fusion.78
  656.3 10.0 add_convert_fusion
  666.2 5.8 all-to-all-start.3
  672.1 8.6 convolution_convert_fusion
  680.7 131.4 %all-to-all-done.3 = bf16[32,48,2048]{2,1,0:T(8,128)(2,1)} async-done(((bf16[32,48,2048]{2,1,0:T(8,128)(2,1)}), bf16[32,48,2048]{2,1,0:T(8,128)(2,1)}, u32[]{:S(2)}, u32[]{:S(2)}) %all-to-all-start.3) | async-done | bytes 6291488 | tf_op jit(solution)/shard_map/all_to_all | solution.py:360
  818.4 12.9 gather_fusion.1
  831.3 126.6 %all-to-all-done.1 = bf16[32,48,2048]{2,1,0:T(8,128)(2,1)} async-done(((bf16[32,48,2048]{2,1,0:T(8,128)(2,1)}), bf16[32,48,2048]{2,1,0:T(8,128)(2,1)}, u32[]{:S(2)}, u32[]{:S(2)}) %all-to-all-start.1) | async-done | bytes 6291488 | tf_op jit(solution)/shard_map/all_to_all | solution.py:325
  957.9 12.5 gather_fusion
  970.4 11.5 fusion.61
  993.0 23.6 %all-gather.17.cloned.1.call-done = bf16[256,2,2048]{2,0,1:T(8,128)(2,1)} async-done(((bf16[64,2,2048]{2,0,1:T(8,128)(2,1)}), bf16[256,2,2048]{2,0,1:T(8,128)(2,1)}) %all-gather.17.cloned.1.call-update) | async-done | bytes 2097168 | tf_op jit(solution)/shard_map/all_gather | solution.py:376
  1039.6 83.1 %while.34 = (s32[]{:T(128)}, f32[256,2,1,8,128]{0,4,3,1,2:T(8,128)S(1)}, f32[4,512,2,1,128]{4,1,0,2,3:T(8,128)}, f32[4,512,2,1,128]{4,1,0,2,3:T(8,128)}, s32[4]{...) while((s32[]{:T(128)}, ...), condition=%wide.region_23.24_spmd.clone, body=%wide.region_22.23_spmd.clone.sunk | while | flops 2707161088 | bytes 140698000 | solution.py:181
  1126.0 65.2 %reduce-scatter.11.cloned.1.call-done = f32[256,2,128]{2,0,1:T(8,128)} async-done(((f32[2048,2,128]{2,0,1:T(8,128)}), f32[256,2,128]{2,0,1:T(8,128)}) %reduce-scatter.11.cloned.1.call-update) | async-done | bytes 262160 | tf_op jit(solution)/shard_map/reduce_scatter | solution.py:402
  1203.0 59.2 %reduce-scatter.13.cloned.1.call-done = f32[256,2,128]{2,0,1:T(8,128)} async-done(((f32[2048,2,128]{2,0,1:T(8,128)}), f32[256,2,128]{2,0,1:T(8,128)}) %reduce-scatter.13.cloned.1.call-update) | async-done | bytes 262160 | tf_op jit(solution)/shard_map/reduce_scatter | solution.py:403
  1286.4 6.3 convolution_convert_fusion.1
  1300.0 10.0 convolution_bitcast_fusion.1
  1310.0 10.0 convolution_bitcast_fusion.2
  1320.0 10.0 convolution_bitcast_fusion.3
  1333.8 58.4 %reduce-scatter.21.cloned.1.call-done = bf16[256,128]{1,0:T(8,128)(2,1)} async-done(((bf16[2048,128]{1,0:T(8,128)(2,1)}), bf16[256,128]{1,0:T(8,128)(2,1)}) %reduce-scatter.21.cloned.1.call-update) | async-done | bytes 65552 | tf_op jit(solution)/shard_map/reduce_scatter | solution.py:466
  1393.7 31.1 %reduce-scatter.15.cloned.1.call-done = bf16[64,2,2048]{2,0,1:T(8,128)(2,1)} async-done(((bf16[256,2,2048]{2,0,1:T(8,128)(2,1)}), bf16[64,2,2048]{2,0,1:T(8,128)(2,1)}) %reduce-scatter.15.cloned.1.call-update) | async-done | bytes 524304 | tf_op jit(solution)/shard_map/reduce_scatter | solution.py:451
  1430.2 86.9 %reduce-scatter.23.cloned.1.call-done = bf16[1024,256]{1,0:T(8,128)(2,1)} async-done(((bf16[1024,2048]{1,0:T(8,128)(2,1)}), bf16[1024,256]{1,0:T(8,128)(2,1)}) %reduce-scatter.23.cloned.1.call-update) | async-done | bytes 524304 | tf_op jit(solution)/shard_map/reduce_scatter | solution.py:469
  1519.2 89.4 %reduce-scatter.17.cloned.1.call-done = bf16[256,1024]{1,0:T(8,128)(2,1)} async-done(((bf16[2048,1024]{1,0:T(8,128)(2,1)}), bf16[256,1024]{1,0:T(8,128)(2,1)}) %reduce-scatter.17.cloned.1.call-update) | async-done | bytes 524304 | tf_op jit(solution)/shard_map/reduce_scatter | solution.py:460
  1610.7 40.7 %all-reduce = (f32[2048]{0:T(1024)}, f32[128]{0:T(128)}, f32[128]{0:T(128)}, f32[2048]{0:T(1024)}) all-reduce(f32[2048]{0:T(1024)S(1)} %get-tuple-element.467, f32[128]{0:T(128)S(1)} %get-tuple-element.463, f32[128]{0:T(128)S(1)} %get-tuple-element.469, f32[2048]{0:T(1024)S(1)} %get-tuple-element.465), channel_id=1, replica_groups=mesh['ctx'=8,'wsh'=4] {'ctx','wsh'}, use_global_device_ids=true, to_apply=%region_31.32 | all-reduce | flops 4352 | bytes 34816 | tf_op jit(solution)/shard_map/psum | solution.py:473
  1651.4 89.4 %all-reduce.3.cloned.1.call-done = f32[2048,32]{0,1:T(8,128)} async-done(((f32[2048,32]{0,1:T(8,128)}), f32[2048,32]{0,1:T(8,128)}) %all-reduce.3.cloned.1.call-update) | async-done | bytes 262160 | tf_op jit(solution)/shard_map/psum | solution.py:473
  (360 shorter events, 259.3 us)
Async XLA Ops:
  7.2 628.6 %copy-start = (bf16[1,768,2048]{2,1,0:T(8,128)(2,1)S(1)}, bf16[1,768,2048]{2,1,0:T(8,128)(2,1)}, u32[]{:S(2)}) copy-start(bf16[1,768,2048]{2,1,0:T(8,128)(2,1)} %param.34) | copy-start | bytes 9437188
  7.2 43.0 %all-gather.7.cloned.1.call-start = ((), (), s32[]{:S(2)}) async-start(), calls=%async_computation.12 | async-start | bytes 2621440 | tf_op jit(solution)/shard_map/all_gather | solution.py:241
  11.9 107.0 %all-gather.11.cloned.1.call-start = ((), (), s32[]{:S(2)}) async-start(), calls=%async_computation.14 | async-start | bytes 4718592 | tf_op jit(solution)/shard_map/all_gather | solution.py:230
  12.6 148.7 %all-gather.9.cloned.1.call-start = ((), (), s32[]{:S(2)}) async-start(), calls=%async_computation.13 | async-start | bytes 1179648 | tf_op jit(solution)/shard_map/all_gather | solution.py:267
  13.9 41.4 %copy-start.26 = (f32[256,64]{0,1:T(8,128)}, f32[256,64]{0,1:T(8,128)S(1)}, u32[]{:S(2)}) copy-start(f32[256,64]{0,1:T(8,128)S(1)} %get-tuple-element.548) | copy-start | bytes 196612
  13.9 41.4 %copy-start.29 = (f32[256,64]{0,1:T(8,128)}, f32[256,64]{0,1:T(8,128)S(1)}, u32[]{:S(2)}) copy-start(f32[256,64]{0,1:T(8,128)S(1)} %get-tuple-element.549) | copy-start | bytes 196612
  14.0 51.7 %copy-start.25 = (f32[256,64]{1,0:T(8,128)}, f32[256,64]{1,0:T(8,128)S(1)}, u32[]{:S(2)}) copy-start(f32[256,64]{1,0:T(8,128)S(1)} %copy.135) | copy-start | bytes 196612
  61.9 63.4 %copy-start.20 = (f32[512,128]{1,0:T(8,128)}, f32[512,128]{1,0:T(8,128)S(1)}, u32[]{:S(2)}) copy-start(f32[512,128]{1,0:T(8,128)S(1)} %get-tuple-element.555) | copy-start | bytes 786436
  62.5 62.8 %copy-start.40 = (f32[512]{0:T(512)}, f32[512]{0:T(512)S(1)}, u32[]{:S(2)}) copy-start(f32[512]{0:T(512)S(1)} %get-tuple-element.547) | copy-start | bytes 6148
  67.6 135.3 %all-gather.13.cloned.1.call-start = ((), (), s32[]{:S(2)}) async-start(), calls=%async_computation.15 | async-start | bytes 1179648 | tf_op jit(solution)/shard_map/all_gather | solution.py:268
  105.2 173.0 %all-gather.15.cloned.1.call-start = ((), (), s32[]{:S(2)}) async-start(), calls=%async_computation.16 | async-start | bytes 4718592 | tf_op jit(solution)/shard_map/all_gather | solution.py:233
  105.8 222.2 %reduce-scatter.9.cloned.1.call-start = ((), (), s32[]{:S(2)}) async-start(), calls=%async_computation.17 | async-start | bytes 5242880 | tf_op jit(solution)/shard_map/reduce_scatter | solution.py:281
  224.9 8.1 copy-start.2
  240.9 8.3 copy-start.2
  285.1 45.6 %copy-start.37 = (f32[2048]{0:T(1024)S(1)}, f32[2048]{0:T(1024)}, u32[]{:S(2)}) copy-start(f32[2048]{0:T(1024)} %param.30) | copy-start | bytes 24580
  344.9 144.9 %all-to-all-start = ((bf16[32,48,2048]{2,1,0:T(8,128)(2,1)}), bf16[32,48,2048]{2,1,0:T(8,128)(2,1)}, u32[]{:S(2)}, u32[]{:S(2)}) async-start(bf16[32,48,2048]{2,1,0:T(8,128)(2,1)} %bitcast.382), calls=%async_computation.1 | async-start | bytes 12582912 | tf_op jit(solution)/shard_map/all_to_all | solution.py:319
  489.7 146.0 %all-to-all-start.2 = ((bf16[32,48,2048]{2,1,0:T(8,128)(2,1)}), bf16[32,48,2048]{2,1,0:T(8,128)(2,1)}, u32[]{:S(2)}, u32[]{:S(2)}) async-start(bf16[32,48,2048]{2,1,0:T(8,128)(2,1)} %bitcast.383), calls=%async_computation.3 | async-start | bytes 12582912 | tf_op jit(solution)/shard_map/all_to_all | solution.py:354
  495.8 9.6 copy-start.51
  635.8 12.2 copy-start.52
  648.0 8.3 copy-start.55
  648.0 8.3 copy-start.57
  648.0 8.3 copy-start.53
  666.2 145.8 %all-to-all-start.3 = ((bf16[32,48,2048]{2,1,0:T(8,128)(2,1)}), bf16[32,48,2048]{2,1,0:T(8,128)(2,1)}, u32[]{:S(2)}, u32[]{:S(2)}) async-start(bf16[32,48,2048]{2,1,0:T(8,128)(2,1)} %bitcast.390), calls=%async_computation.4 | async-start | bytes 12582912 | tf_op jit(solution)/shard_map/all_to_all | solution.py:360
  812.1 145.8 %all-to-all-start.1 = ((bf16[32,48,2048]{2,1,0:T(8,128)(2,1)}), bf16[32,48,2048]{2,1,0:T(8,128)(2,1)}, u32[]{:S(2)}, u32[]{:S(2)}) async-start(bf16[32,48,2048]{2,1,0:T(8,128)(2,1)} %bitcast.389), calls=%async_computation.2 | async-start | bytes 12582912 | tf_op jit(solution)/shard_map/all_to_all | solution.py:325
  817.9 198.7 %all-gather.17.cloned.1.call-start = ((), (), s32[]{:S(2)}) async-start(), calls=%async_computation.18 | async-start | bytes 2621440 | tf_op jit(solution)/shard_map/all_gather | solution.py:376
  957.9 12.5 copy-start.13
  992.8 198.5 %reduce-scatter.11.cloned.1.call-start = ((), (), s32[]{:S(2)}) async-start(), calls=%async_computation.19 | async-start | bytes 2359296 | tf_op jit(solution)/shard_map/reduce_scatter | solution.py:402
  1122.7 139.5 %reduce-scatter.13.cloned.1.call-start = ((), (), s32[]{:S(2)}) async-start(), calls=%async_computation.20 | async-start | bytes 2359296 | tf_op jit(solution)/shard_map/reduce_scatter | solution.py:403
  1122.7 70.2 %copy-start.21 = (f32[512,128]{1,0:T(8,128)S(1)}, f32[512,128]{1,0:T(8,128)}, u32[]{:S(2)}) copy-start(f32[512,128]{1,0:T(8,128)} %copy-done.20) | copy-start | bytes 786436
  1122.7 70.2 %copy-start.41 = (f32[512]{0:T(512)S(1)}, f32[512]{0:T(512)}, u32[]{:S(2)}) copy-start(f32[512]{0:T(512)} %copy-done.40) | copy-start | bytes 6148
  1122.7 70.2 %copy-start.47 = (f32[128]{0:T(128)S(1)}, f32[128]{0:T(128)}, u32[]{:S(2)}) copy-start(f32[128]{0:T(128)} %param.28) | copy-start | bytes 1540
  1123.4 69.8 %copy-start.46 = (f32[512]{0:T(512)S(1)}, f32[512]{0:T(512)}, u32[]{:S(2)}) copy-start(f32[512]{0:T(512)} %get-tuple-element.546) | copy-start | bytes 6148
  1123.4 208.9 %reduce-scatter.19.cloned.1.call-start = ((), (), s32[]{:S(2)}) async-start(), calls=%async_computation.23 | async-start | bytes 589824 | tf_op jit(solution)/shard_map/reduce_scatter | solution.py:463
  1126.0 68.2 %copy-start.7 = (bf16[512,2048]{1,0:T(8,128)(2,1)S(1)}, bf16[512,2048]{1,0:T(8,128)(2,1)}, u32[]{:S(2)}) copy-start(bf16[512,2048]{1,0:T(8,128)(2,1)} %reshape.707) | copy-start | bytes 6291460
  1195.9 196.3 %reduce-scatter.21.cloned.1.call-start = ((), (), s32[]{:S(2)}) async-start(), calls=%async_computation.24 | async-start | bytes 589824 | tf_op jit(solution)/shard_map/reduce_scatter | solution.py:466
  1266.4 158.4 %reduce-scatter.15.cloned.1.call-start = ((), (), s32[]{:S(2)}) async-start(), calls=%async_computation.21 | async-start | bytes 2621440 | tf_op jit(solution)/shard_map/reduce_scatter | solution.py:451
  1282.7 234.4 %reduce-scatter.23.cloned.1.call-start = ((), (), s32[]{:S(2)}) async-start(), calls=%async_computation.25 | async-start | bytes 4718592 | tf_op jit(solution)/shard_map/reduce_scatter | solution.py:469
  1292.7 315.9 %reduce-scatter.17.cloned.1.call-start = ((), (), s32[]{:S(2)}) async-start(), calls=%async_computation.22 | async-start | bytes 4718592 | tf_op jit(solution)/shard_map/reduce_scatter | solution.py:460
  1298.4 442.5 %all-reduce.3.cloned.1.call-start = ((), (), s32[]{:S(2)}) async-start(), calls=%async_computation.26 | async-start | bytes 524288 | tf_op jit(solution)/shard_map/psum | solution.py:473
  1300.0 10.0 copy-start.58
  1310.0 10.0 copy-start.56
  1320.0 10.0 copy-start.22
  1320.0 11.4 copy-start.15
  1320.0 104.8 %copy-start.12 = (bf16[64,2,2048]{2,1,0:T(2,128)(2,1)S(1)}, bf16[64,2,2048]{2,1,0:T(2,128)(2,1)}, u32[]{:S(2)}) copy-start(bf16[64,2,2048]{2,1,0:T(2,128)(2,1)} %param.21) | copy-start | bytes 1572868
  1320.0 104.8 %copy-start.38 = (f32[2048]{0:T(1024)S(1)}, f32[2048]{0:T(1024)}, u32[]{:S(2)}) copy-start(f32[2048]{0:T(1024)} %param.23) | copy-start | bytes 24580
  1320.0 104.8 %copy-start.45 = (f32[64,2]{0,1:T(2,128)S(1)}, f32[64,2]{0,1:T(2,128)}, u32[]{:S(2)}) copy-start(f32[64,2]{0,1:T(2,128)} %copy-done.44) | copy-start | bytes 1540
  1320.0 106.3 %copy-start.50 = (f32[64,2]{0,1:T(2,128)S(1)}, f32[64,2]{0,1:T(2,128)}, u32[]{:S(2)}) copy-start(f32[64,2]{0,1:T(2,128)} %get-tuple-element.550) | copy-start | bytes 1540
  1426.3 316.2 %copy-start.1 = (bf16[1,768,2048]{2,1,0:T(8,128)(2,1)S(1)}, bf16[1,768,2048]{2,1,0:T(8,128)(2,1)}, u32[]{:S(2)}) copy-start(bf16[1,768,2048]{2,1,0:T(8,128)(2,1)} %param.34) | copy-start | bytes 9437188
  (48 other events, 176.9 us)
Sparse Core Ops, SparseCore 0:
  12.0 25.2 all-gather.6
  39.4 79.3 all-gather.10
  121.6 39.6 all-gather.8
  163.9 38.9 all-gather.12
  204.8 73.3 all-gather.14
  285.2 42.7 reduce-scatter.8
  992.9 23.6 all-gather.16
  1122.8 68.3 reduce-scatter.10
  1194.8 67.3 reduce-scatter.12
  1265.4 61.7 reduce-scatter.18
  1330.5 61.6 reduce-scatter.20
  1394.6 30.1 reduce-scatter.14
  1428.4 88.6 reduce-scatter.22
  1520.6 87.9 reduce-scatter.16
  1614.5 126.2 all-reduce.2
where the time goes:
time: 1760 us; the launch traced here: 1750 us
  waiting for transfers between devices  1140 us (65%)
  matrix products  254 us (14%)
  local copies, waits for them, and re-layouts  132 us (8%)
  blocking collectives  110 us (6%)
  other arithmetic  75.3 us (4%)
  starting transfers between devices  24.3 us (1%)
    all_to_all x1, waiting for transfers between devices, local(): lax.all_to_all(row_cot.reshape(device_count, capacity, width), ('ctx', 'w...  131 us
    all_to_all x1, waiting for transfers between devices, local(): lax.all_to_all(produced, ('ctx', 'wsh'), split_axis=0, concat_axis=0, til...  127 us
    all_to_all x1, waiting for transfers between devices, local(): lax.all_to_all(send_rows, ('ctx', 'wsh'), split_axis=0, concat_axis=0, ti...  124 us
    all_to_all x1, waiting for transfers between devices, local(): lax.all_to_all(cot_send, ('ctx', 'wsh'), split_axis=0, concat_axis=0, til...  122 us
    psum x1, waiting for transfers between devices, local(): lax.psum((norm_gain_grad, query_gain_grad, key_gain_grad, moe_gain_grad,...  89.4 us
    reduce_scatter x1, waiting for transfers between devices, local(): lax.psum_scatter(query_weight_grad.astype(jnp.bfloat16), 'ctx', scatter_d...  89.4 us
    reduce_scatter x1, waiting for transfers between devices, local(): lax.psum_scatter(out_weight_grad.astype(jnp.bfloat16), 'ctx', scatter_dim...  86.9 us
    reduce_scatter x1, waiting for transfers between devices, local(): lax.psum_scatter(key_cot_all, 'ctx', scatter_dimension=0, tiled=True)  65.2 us
  transfers between devices with their start and end apart: 19, of which 17 were waited for; matrix products, arithmetic and copies ran while one was open for 15% of the time, Pallas kernels for 0%

commit v1 on v0

v1 whole, which is shorter than its diff:
```python
import functools
import math

import jax
import jax.numpy as jnp
from jax import lax
from jax.experimental import pallas as pl
from jax.experimental.pallas import tpu as pltpu
from jax.sharding import PartitionSpec as P

EPSILON = 1e-06
ROPE_BASE = 1000000.0
MASKED = -1e30


def positions_of(pair_map, seq_len, block_len, group_count):
    row_index = jnp.arange(seq_len, dtype=jnp.int32)
    owner_group = row_index // (2 * block_len)
    inner_row = row_index % (2 * block_len)
    group_table = jnp.arange(group_count, dtype=jnp.int32)
    pair_index = jnp.sum(
        jnp.where(owner_group[:, None] == group_table[None, :], pair_map[None, :], 0), axis=1
    )
    block_index = jnp.where(inner_row < block_len, pair_index, 2 * group_count - 1 - pair_index)
    return block_index * block_len + inner_row % block_len


def rope_tables(positions, head_dim):
    half_dim = head_dim // 2
    frequency = ROPE_BASE ** (-(jnp.arange(half_dim, dtype=jnp.float32) * 2.0) / head_dim)
    angles = positions.astype(jnp.float32)[:, None] * frequency[None, :]
    return (jnp.cos(angles), jnp.sin(angles))


def rotate(tensor, cosine, sine_table):
    half_dim = tensor.shape[-1] // 2
    first_half = tensor[..., :half_dim]
    second_half = tensor[..., half_dim:]
    return jnp.concatenate(
        [
            first_half * cosine - second_half * sine_table,
            second_half * cosine + first_half * sine_table,
        ],
        axis=-1,
    )


def unrotate(gradient, cosine, sine_table):
    half_dim = gradient.shape[-1] // 2
    first_half = gradient[..., :half_dim]
    second_half = gradient[..., half_dim:]
    return jnp.concatenate(
        [
            first_half * cosine + second_half * sine_table,
            second_half * cosine - first_half * sine_table,
        ],
        axis=-1,
    )


def rms_forward(tensor, gain_vector):
    inverse = lax.rsqrt(jnp.mean(tensor * tensor, axis=-1, keepdims=True) + EPSILON)
    return (tensor * inverse * gain_vector, inverse)


def rms_backward(tensor, inverse, gain_vector, gradient):
    weighted = gradient * gain_vector
    inner_mean = jnp.mean(weighted * tensor, axis=-1, keepdims=True)
    tensor_grad = inverse * weighted - tensor * inverse**3 * inner_mean
    gain_grad = jnp.sum((gradient * tensor * inverse).reshape(-1, tensor.shape[-1]), axis=0)
    return (tensor_grad, gain_grad)


MESH_ID = pl.DeviceIdType.MESH


class Place:
    def __init__(self, nz, ux, uy, uc):
        ci, wi = lax.axis_index("ctx"), lax.axis_index("wsh")
        self.nz, self.ux, self.uy, self.uc = nz, ux, uy, uc
        self.z, self.x, self.y, self.c = ci // 2, ci % 2, wi // 2, wi % 2

    def dev(self, z, x, y, c):
        return (z * 2 + x, y * 2 + c)

    def blk(self, z, x, y, c):
        if self.ux and self.uc:
            return (z * 2 + x) * 4 + y * 2 + c
        if self.ux:
            return z * 2 + x
        return y * 2 + c

    def greet(self):
        z, x, y, c, nz = self.z, self.x, self.y, self.c, self.nz
        barrier = pltpu.get_barrier_semaphore()
        count = 0
        if nz > 1:
            for step in (-1, 1):
                ok = jnp.logical_and(z + step >= 0, z + step < nz)

                @pl.when(ok)
                def _():
                    pl.semaphore_signal(
                        barrier, inc=1, device_id=self.dev(z + step, x, y, c), device_id_type=MESH_ID
                    )

                count = count + ok.astype(jnp.int32)
        for use, place in (
            (self.ux, (z, 1 - x, y, c)),
            (self.uy, (z, x, 1 - y, c)),
            (self.uc, (z, x, y, 1 - c)),
        ):
            if use:
                pl.semaphore_signal(
                    barrier, inc=1, device_id=self.dev(*place), device_id_type=MESH_ID
                )
                count = count + 1
        pl.semaphore_wait(barrier, count)

    def line_steps(self):
        steps = [(0, 0, self.z, None)]
        for d in range(1, self.nz):
            steps.append((d, 0, self.z - d, self.z - d >= 0))
            steps.append((d, 1, self.z + d, self.z + d < self.nz))
        return steps


def when(cond, fn):
    if cond is None:
        fn()
    else:
        pl.when(cond)(fn)


def ag_kernel(nz, ux, uy, uc, x_ref, o_ref, ssem, rsem, lsem):
    pc = Place(nz, ux, uy, uc)
    z, x, y, c = pc.z, pc.x, pc.y, pc.c
    rows = x_ref.shape[0]
    half = rows // 2
    pc.greet()
    to_x, to_y, to_c = pc.dev(z, 1 - x, y, c), pc.dev(z, x, 1 - y, c), pc.dev(z, x, y, 1 - c)

    def part(b, p):
        if p == 0:
            return o_ref.at[b]
        return o_ref.at[b, pl.ds((p - 1) * half, half)]

    def sid(d, side, kind):
        return (d * 2 + side) * 10 + kind

    def copy(b, p, sidx, ridx, device, src=None):
        return pltpu.make_async_remote_copy(
            src_ref=part(b, p) if src is None else src,
            dst_ref=part(b, p),
            send_sem=ssem.at[sidx],
            recv_sem=rsem.at[ridx],
            device_id=device,
            device_id_type=MESH_ID,
        )

    own = pltpu.make_async_copy(x_ref, o_ref.at[pc.blk(z, x, y, c)], lsem)
    own.start()

    def hops(d, side, s):
        out = []
        if nz > 1:
            b = pc.blk(s, x, y, c)
            src = x_ref if d == 0 else None
            if d == 0 or side == 0:
                if d + 1 < nz:
                    out.append(
                        (z + 1 < nz, copy(b, 0, sid(d, 0, 0), sid(d + 1, 0, 0), pc.dev(z + 1, x, y, c), src))
                    )
            if d == 0 or side == 1:
                if d + 1 < nz:
                    out.append(
                        (z >= 1, copy(b, 0, sid(d, 1, 0), sid(d + 1, 1, 0), pc.dev(z - 1, x, y, c), src))
                    )
        return out

    def spread(d, side, s):
        b = pc.blk(s, x, y, c)
        src = x_ref if d == 0 else None
        out = []
        if ux:
            out.append(copy(b, 0, sid(d, side, 1), sid(d, side, 1), to_x, src))
        if uy:
            out.append(copy(b, 0, sid(d, side, 2), sid(d, side, 2), to_y, src))
        if uc:
            out.append(copy(b, 0, sid(d, side, 5), sid(d, side, 5), to_c, src))
        return out

    def passed(d, side, s):
        out = []
        if ux:
            b = pc.blk(s, 1 - x, y, c)
            arrive = copy(b, 0, sid(d, side, 1), sid(d, side, 1), to_x)
            go = []
            if uy:
                go.append(copy(b, 1, sid(d, side, 3), sid(d, side, 3), to_y))
            if uc:
                go.append(copy(b, 0, sid(d, side, 6), sid(d, side, 6), to_c))
            out.append((arrive, go))
        if uy:
            b = pc.blk(s, x, 1 - y, c)
            arrive = copy(b, 0, sid(d, side, 2), sid(d, side, 2), to_y)
            go = []
            if ux:
                go.append(copy(b, 2, sid(d, side, 4), sid(d, side, 4), to_x))
            if uc:
                go.append(copy(b, 0, sid(d, side, 7), sid(d, side, 7), to_c))
            out.append((arrive, go))
        return out

    def across(d, side, s):
        out = []
        if ux and uy:
            b = pc.blk(s, 1 - x, 1 - y, c)
            arrive = copy(b, 1, sid(d, side, 3), sid(d, side, 3), to_y)
            go = [copy(b, 1, sid(d, side, 8), sid(d, side, 8), to_c)] if uc else []
            out.append((arrive, go))
            arrive = copy(b, 2, sid(d, side, 4), sid(d, side, 4), to_x)
            go = [copy(b, 2, sid(d, side, 9), sid(d, side, 9), to_c)] if uc else []
            out.append((arrive, go))
        return out

    def partner(d, side, s):
        out = []
        if uc:
            out.append(copy(pc.blk(s, x, y, 1 - c), 0, 0, sid(d, side, 5), to_c))
            if ux:
                out.append(copy(pc.blk(s, 1 - x, y, 1 - c), 0, 0, sid(d, side, 6), to_c))
            if uy:
                out.append(copy(pc.blk(s, x, 1 - y, 1 - c), 0, 0, sid(d, side, 7), to_c))
            if ux and uy:
                b = pc.blk(s, 1 - x, 1 - y, 1 - c)
                out.append(copy(b, 1, 0, sid(d, side, 8), to_c))
                out.append(copy(b, 2, 0, sid(d, side, 9), to_c))
        return out

    steps = pc.line_steps()

    def do_line(step):
        d, side, s, ok = step

        def fn():
            if d > 0:
                copy(pc.blk(s, x, y, c), 0, 0, sid(d, side, 0), to_x).wait_recv()
            for cond, cp in hops(d, side, s):
                when(cond, cp.start)
            for cp in spread(d, side, s):
                cp.start()

        when(ok, fn)

    def do_pass(step, which):
        d, side, s, ok = step

        def fn():
            for arrive, go in which(d, side, s):
                arrive.wait_recv()
                for cp in go:
                    cp.start()

        when(ok, fn)

    groups = [[st for st in steps if st[0] == d] for d in range(nz)]
    for t in range(nz + 2):
        if t < nz:
            for st in groups[t]:
                do_line(st)
        if 0 <= t - 1 < nz:
            for st in groups[t - 1]:
                do_pass(st, passed)
        if 0 <= t - 2 < nz:
            for st in groups[t - 2]:
                do_pass(st, across)

    for st in steps:
        d, side, s, ok = st

        def fn():
            for cp in partner(d, side, s):
                cp.wait_recv()
            for cond, cp in hops(d, side, s):
                when(cond, cp.wait_send)
            for cp in spread(d, side, s):
                cp.wait_send()
            for which in (passed, across):
                for _, go in which(d, side, s):
                    for cp in go:
                        cp.wait_send()

        when(ok, fn)
    own.wait()


def all_gather(shard, nz, ux, uy, uc, collective_id, name):
    group = (nz * 2 if ux else 1) * (4 if uc else 1)
    nsem = nz * 20
    return pl.pallas_call(
        functools.partial(ag_kernel, nz, ux, uy, uc),
        out_shape=jax.ShapeDtypeStruct((group,) + shard.shape, shard.dtype),
        in_specs=[pl.BlockSpec(memory_space=pl.ANY)],
        out_specs=pl.BlockSpec(memory_space=pl.ANY),
        scratch_shapes=[
            pltpu.SemaphoreType.DMA((nsem,)),
            pltpu.SemaphoreType.DMA((nsem,)),
            pltpu.SemaphoreType.DMA,
        ],
        compiler_params=pltpu.CompilerParams(collective_id=collective_id, has_side_effects=True),
        name=name,
    )(shard)


def rs_kernel(nz, ux, uy, uc, p_ref, o_ref, acc, rc, rx, ry, ra, rb, rz, ssem, rsem, lsem):
    pc = Place(nz, ux, uy, uc)
    z, x, y, c = pc.z, pc.x, pc.y, pc.c
    rows, cols = o_ref.shape
    half = rows // 2
    chunk = math.gcd(half, 32)
    f32 = jnp.float32
    pc.greet()
    to_x, to_y, to_c = pc.dev(z, 1 - x, y, c), pc.dev(z, x, 1 - y, c), pc.dev(z, x, y, 1 - c)
    rels = [(0, x, y)]
    if ux:
        rels.append((1, 1 - x, y))
    if uy:
        rels.append((2, x, 1 - y))
    if ux and uy:
        rels.append((3, 1 - x, 1 - y))
    KINDS = 12

    def slot(s):
        return s if nz > 1 else 0

    def sid(s, kind):
        return slot(s) * KINDS + kind

    def hf(ref, h):
        return ref.at[pl.ds(h * half, half)]

    def rcopy(src, dst, s, kind, device):
        return pltpu.make_async_remote_copy(
            src_ref=src,
            dst_ref=dst,
            send_sem=ssem.at[sid(s, kind)],
            recv_sem=rsem.at[sid(s, kind)],
            device_id=device,
            device_id_type=MESH_ID,
        )

    def load(s, rel, px, py):
        return pltpu.make_async_copy(
            p_ref.at[pc.blk(s, px, py, c)], acc.at[slot(s) * 4 + rel], lsem.at[slot(s) * 4 + rel]
        )

    def give(s, rel, px, py):
        return rcopy(
            p_ref.at[pc.blk(s, px, py, 1 - c)], rc.at[slot(s) * 4 + rel], s, rel, to_c
        )

    def fold(dst, lo, n, srcs):
        def body(i, _):
            r = pl.multiple_of(i * chunk, chunk)
            total = dst[pl.ds(lo + r, chunk), :].astype(f32)
            for ref, at in srcs:
                total = total + ref[pl.ds(at + r, chunk), :].astype(f32)
            dst[pl.ds(lo + r, chunk), :] = total.astype(dst.dtype)
            return 0

        lax.fori_loop(0, n // chunk, body, 0)

    def over_a(s):
        return rcopy(hf(acc.at[slot(s) * 4 + 3], 0), ra.at[slot(s)], s, 4, to_y)

    def over_b(s):
        return rcopy(hf(acc.at[slot(s) * 4 + 3], 1), rb.at[slot(s)], s, 5, to_x)

    def x_half(s, h):
        return rcopy(hf(acc.at[slot(s) * 4 + 1], h), hf(rx.at[slot(s)], h), s, 6 + h, to_x)

    def y_half(s, h):
        return rcopy(hf(acc.at[slot(s) * 4 + 2], h), hf(ry.at[slot(s)], h), s, 8 + h, to_y)

    def z_send(s, up):
        return rcopy(
            acc.at[slot(s) * 4],
            rz.at[slot(s)] if up is None else rz.at[slot(s)],
            s,
            10,
            pc.dev(z + (1 if up else -1), x, y, c),
        )

    def z_last(s, up):
        return pltpu.make_async_remote_copy(
            src_ref=acc.at[slot(s) * 4],
            dst_ref=rz.at[slot(s)] if up else rz.at[nz],
            send_sem=ssem.at[sid(s, 10)],
            recv_sem=rsem.at[sid(s, 10)] if up else rsem.at[sid(s, 11)],
            device_id=pc.dev(z + (1 if up else -1), x, y, c),
            device_id_type=MESH_ID,
        )

    steps = list(reversed(pc.line_steps()))

    for d, side, s, ok in steps:

        def fn():
            for rel, px, py in reversed(rels):
                load(s, rel, px, py).start()
                if uc:
                    give(s, rel, px, py).start()

        when(ok, fn)

    def first(step):
        d, side, s, ok = step

        def fn():
            for rel, px, py in reversed(rels):
                load(s, rel, px, py).wait()
                if uc:
                    give(s, rel, px, py).wait_recv()
                    fold(acc.at[slot(s) * 4 + rel], 0, rows, [(rc.at[slot(s) * 4 + rel], 0)])
                if rel == 3:
                    over_a(s).start()
                    over_b(s).start()
                if rel == 2:
                    y_half(s, 0).start()
                    if not ux:
                        y_half(s, 1).start()
                if rel == 1:
                    x_half(s, 1).start()
                    if not uy:
                        x_half(s, 0).start()

        when(ok, fn)

    def second(step):
        d, side, s, ok = step

        def fn():
            if ux and uy:
                over_a(s).wait_recv()
                fold(acc.at[slot(s) * 4 + 1], 0, half, [(ra.at[slot(s)], 0)])
                x_half(s, 0).start()
                over_b(s).wait_recv()
                fold(acc.at[slot(s) * 4 + 2], half, half, [(rb.at[slot(s)], 0)])
                y_half(s, 1).start()

        when(ok, fn)

    def third(step):
        d, side, s, ok = step

        def fn():
            srcs = []
            if ux:
                x_half(s, 0).wait_recv()
                x_half(s, 1).wait_recv()
                srcs.append((rx.at[slot(s)], 0))
            if uy:
                y_half(s, 0).wait_recv()
                y_half(s, 1).wait_recv()
                srcs.append((ry.at[slot(s)], 0))
            if d > 0:
                more = (z + 1 < nz) if side == 0 else (z >= 1)

                @pl.when(more)
                def _():
                    z_send(s, side == 1).wait_recv()
                    fold(acc.at[slot(s) * 4], 0, rows, srcs + [(rz.at[slot(s)], 0)])

                if srcs:

                    @pl.when(jnp.logical_not(more))
                    def _():
                        fold(acc.at[slot(s) * 4], 0, rows, srcs)

                if d == 1:
                    z_last(s, side == 1).start()
                else:
                    z_send(s, side == 1).start()
            else:

                def body(use_lo, use_hi):
                    terms = list(srcs)
                    if use_lo:
                        z_last(s, True).wait_recv()
                        terms.append((rz.at[slot(s)], 0))
                    if use_hi:
                        z_last(s, False).wait_recv()
                        terms.append((rz.at[nz], 0))

                    def step_(i, _):
                        r = pl.multiple_of(i * chunk, chunk)
                        total = acc[slot(s) * 4, pl.ds(r, chunk), :].astype(f32)
                        for ref, at in terms:
                            total = total + ref[pl.ds(at + r, chunk), :].astype(f32)
                        o_ref[pl.ds(r, chunk), :] = total.astype(o_ref.dtype)
                        return 0

                    lax.fori_loop(0, rows // chunk, step_, 0)

                if nz == 1:
                    body(False, False)
                else:
                    lo, hi = z >= 1, z + 1 < nz
                    pl.when(jnp.logical_and(lo, hi))(lambda: body(True, True))
                    pl.when(jnp.logical_and(lo, jnp.logical_not(hi)))(lambda: body(True, False))
                    pl.when(jnp.logical_and(jnp.logical_not(lo), hi))(lambda: body(False, True))

        when(ok, fn)

    groups = [[st for st in steps if st[0] == d] for d in reversed(range(nz))]
    for t in range(nz + 2):
        if t < nz:
            for st in groups[t]:
                first(st)
        if 0 <= t - 1 < nz:
            for st in groups[t - 1]:
                second(st)
        if 0 <= t - 2 < nz:
            for st in groups[t - 2]:
                third(st)

    for d, side, s, ok in steps:

        def fn():
            for rel, px, py in rels:
                if uc:
                    give(s, rel, px, py).wait_send()
            if ux and uy:
                over_a(s).wait_send()
                over_b(s).wait_send()
            if ux:
                x_half(s, 0).wait_send()
                x_half(s, 1).wait_send()
            if uy:
                y_half(s, 0).wait_send()
                y_half(s, 1).wait_send()
            if d > 0:
                z_send(s, side == 1).wait_send()

        when(ok, fn)


def reduce_scatter(parts, nz, ux, uy, uc, out_dtype, collective_id, name):
    group, rows, cols = parts.shape
    dt = parts.dtype
    lines = nz
    buf = lambda n, r: pltpu.VMEM((n, r, cols), dt)
    return pl.pallas_call(
        functools.partial(rs_kernel, nz, ux, uy, uc),
        out_shape=jax.ShapeDtypeStruct((rows, cols), out_dtype),
        in_specs=[pl.BlockSpec(memory_space=pl.ANY)],
        out_specs=pl.BlockSpec(memory_space=pltpu.VMEM),
        scratch_shapes=[
            buf(lines * 4, rows),
            buf(lines * 4 if uc else 1, rows if uc else 16),
            buf(lines if ux else 1, rows if ux else 16),
            buf(lines if uy else 1, rows if uy else 16),
            buf(lines if ux and uy else 1, rows // 2 if ux and uy else 16),
            buf(lines if ux and uy else 1, rows // 2 if ux and uy else 16),
            buf(lines + 1 if nz > 1 else 1, rows if nz > 1 else 16),
            pltpu.SemaphoreType.DMA((lines * 12,)),
            pltpu.SemaphoreType.DMA((lines * 12,)),
            pltpu.SemaphoreType.DMA((lines * 4,)),
        ],
        compiler_params=pltpu.CompilerParams(
            collective_id=collective_id, has_side_effects=True, vmem_limit_bytes=60 * 1024 * 1024
        ),
        name=name,
    )(parts)


def score_block(query_rot, key_piece, scaling):
    return (
        jnp.einsum("qsagd,ksad->sagqk", query_rot, key_piece, preferred_element_type=jnp.float32)
        * scaling
    )


def attend_keys(query_rot, query_pos, key_all, value_all, key_pos, scaling):
    length = key_all.shape[0]
    key_block = math.gcd(length, 512)
    block_count = length // key_block
    query_rows, seq_count, kv_count, group, head_dim = query_rot.shape
    start_carry = (
        jnp.full((seq_count, kv_count, group, query_rows), MASKED, jnp.float32),
        jnp.zeros((seq_count, kv_count, group, query_rows), jnp.float32),
        jnp.zeros((seq_count, kv_count, group, query_rows, head_dim), jnp.float32),
    )

    def step(block_id, carry):
        row_top, row_total, accum = carry
        start = block_id * key_block
        key_piece = lax.dynamic_slice_in_dim(key_all, start, key_block, 0)
        value_piece = lax.dynamic_slice_in_dim(value_all, start, key_block, 0)
        piece_pos = lax.dynamic_slice_in_dim(key_pos, start, key_block, 0)
        scores = score_block(query_rot, key_piece, scaling)
        allowed = piece_pos[None, :] <= query_pos[:, None]
        new_top = jnp.maximum(row_top, jnp.max(jnp.where(allowed, scores, MASKED), axis=-1))
        expo = jnp.where(allowed, jnp.exp(scores - new_top[..., None]), 0.0)
        decay = jnp.exp(row_top - new_top)
        row_total = row_total * decay + jnp.sum(expo, axis=-1)
        accum = accum * decay[..., None] + jnp.einsum(
            "sagqk,ksad->sagqd",
            expo.astype(jnp.bfloat16),
            value_piece,
            preferred_element_type=jnp.float32,
        )
        return (new_top, row_total, accum)

    return lax.fori_loop(0, block_count, step, start_carry)


def attend_grads(
    query_rot, query_pos, key_all, value_all, key_pos, attn_cot, delta, log_total, scaling
):
    length = key_all.shape[0]
    key_block = math.gcd(length, 512)
    block_count = length // key_block
    query_rows, seq_count, kv_count, group, head_dim = query_rot.shape

    def step(query_cot, block_id):
        start = block_id * key_block
        key_piece = lax.dynamic_slice_in_dim(key_all, start, key_block, 0)
        value_piece = lax.dynamic_slice_in_dim(value_all, start, key_block, 0)
        piece_pos = lax.dynamic_slice_in_dim(key_pos, start, key_block, 0)
        scores = score_block(query_rot, key_piece, scaling)
        allowed = piece_pos[None, :] <= query_pos[:, None]
        weights_back = jnp.where(allowed, jnp.exp(scores - log_total[..., None]), 0.0)
        prob_cot = jnp.einsum(
            "qsagd,ksad->sagqk", attn_cot, value_piece, preferred_element_type=jnp.float32
        )
        score_cot = weights_back * (prob_cot - delta[..., None])
        value_cot = jnp.einsum(
            "sagqk,qsagd->ksad",
            weights_back.astype(jnp.bfloat16),
            attn_cot,
            preferred_element_type=jnp.float32,
        )
        score_low = score_cot.astype(jnp.bfloat16)
        query_cot = (
            query_cot
            + jnp.einsum(
                "sagqk,ksad->qsagd", score_low, key_piece, preferred_element_type=jnp.float32
            )
            * scaling
        )
        key_cot = (
            jnp.einsum(
                "sagqk,qsagd->ksad", score_low, query_rot, preferred_element_type=jnp.float32
            )
            * scaling
        )
        return (query_cot, (key_cot, value_cot))

    start_carry = jnp.zeros((query_rows, seq_count, kv_count, group, head_dim), jnp.float32)
    query_cot, (key_cot, value_cot) = lax.scan(
        step, start_carry, jnp.arange(block_count, dtype=jnp.int32)
    )
    return (
        query_cot,
        key_cot.reshape(length, seq_count, kv_count * head_dim),
        value_cot.reshape(length, seq_count, kv_count * head_dim),
    )


def gather_ctx(shard, name, ident):
    if lax.axis_size("ctx") == 8 and lax.axis_size("wsh") == 4:
        return all_gather(shard, 4, True, False, False, ident, name)
    return lax.all_gather(shard, "ctx", axis=0)


def gather_wsh(shard, name, ident):
    if lax.axis_size("ctx") == 8 and lax.axis_size("wsh") == 4:
        return all_gather(shard, 1, False, True, True, ident, name)
    return lax.all_gather(shard, "wsh", axis=0)


def gather_all(shard, name, ident):
    if lax.axis_size("ctx") == 8 and lax.axis_size("wsh") == 4:
        return all_gather(shard, 4, True, True, True, ident, name)
    return lax.all_gather(shard, ("ctx", "wsh"), axis=0)


def scatter_ctx(parts, name, ident):
    if lax.axis_size("ctx") == 8 and lax.axis_size("wsh") == 4:
        return reduce_scatter(parts, 4, True, False, False, jnp.float32, ident, name)
    return lax.psum_scatter(parts, "ctx", scatter_dimension=0, tiled=False).astype(jnp.float32)


def scatter_wsh(parts, name, ident):
    if lax.axis_size("ctx") == 8 and lax.axis_size("wsh") == 4:
        return reduce_scatter(parts, 1, False, True, True, jnp.float32, ident, name)
    return lax.psum_scatter(parts, "wsh", scatter_dimension=0, tiled=False).astype(jnp.float32)


def scatter_all(parts, name, ident):
    if lax.axis_size("ctx") == 8 and lax.axis_size("wsh") == 4:
        return reduce_scatter(parts, 4, True, True, True, jnp.float32, ident, name)
    return lax.psum_scatter(
        parts, ("ctx", "wsh"), scatter_dimension=0, tiled=False
    ).astype(jnp.float32)


def exchange(pieces):
    return lax.all_to_all(pieces, ("ctx", "wsh"), split_axis=0, concat_axis=0, tiled=True)


def to_everyone(value, device_count):
    return exchange(jnp.broadcast_to(value[None], (device_count,) + value.shape))


def local(
    inputs,
    pair_map,
    norm_gain,
    query_weight,
    key_weight,
    value_weight,
    query_gain,
    key_gain,
    out_weight,
    moe_gain,
    router,
    expert_gate,
    expert_up,
    expert_down,
    expert_ids,
    dispatch_slot,
    cotangent,
):
    f32, bf16 = jnp.float32, jnp.bfloat16
    rows_dev, seq_count, width = inputs.shape
    ctx_count = lax.axis_size("ctx")
    wsh_count = lax.axis_size("wsh")
    device_count = ctx_count * wsh_count
    head_dim = query_gain.shape[0]
    group_rows = rows_dev * wsh_count
    block_len = group_rows // 2
    seq_len = group_rows * ctx_count
    tokens = rows_dev * seq_count
    group_tokens = tokens * wsh_count
    top_count = expert_ids.shape[-1]
    expert_count = router.shape[1]
    capacity = max(2, 3 * top_count * block_len // (2 * device_count))
    scaling = head_dim ** (-0.5)
    positions = positions_of(pair_map, seq_len, block_len, pair_map.shape[0])
    query_pos = lax.dynamic_slice_in_dim(
        positions, lax.axis_index("ctx") * group_rows, group_rows, 0
    )
    cosine, sine_table = rope_tables(query_pos, head_dim)
    cosine = cosine[:, None, None, :]
    sine_table = sine_table[:, None, None, :]

    inputs_f = inputs.astype(f32)
    normed_f, inverse_one = rms_forward(inputs_f, norm_gain)
    normed = normed_f.astype(bf16)
    normed_flat = gather_wsh(normed.reshape(tokens, width), "ag_normed", 1).reshape(
        group_tokens, width
    )
    q_cols, kv_cols = query_weight.shape[1], key_weight.shape[1]
    qkv_shard = jnp.concatenate([query_weight, key_weight, value_weight], axis=1)
    qkv_full = gather_ctx(qkv_shard, "ag_qkv", 2).reshape(width, q_cols + 2 * kv_cols)
    out_shard = out_weight.T
    out_full = lax.all_gather(out_shard, "ctx", axis=0, tiled=True)
    cot_flat = cotangent.reshape(tokens, width)
    cot_all = lax.all_gather(cot_flat.astype(bf16), ("ctx", "wsh"), axis=0)
    heads_loc = q_cols // head_dim
    kv_loc = kv_cols // head_dim
    group = heads_loc // kv_loc
    projected = jnp.dot(normed_flat, qkv_full, preferred_element_type=f32)
    queries = projected[:, :q_cols].reshape(group_rows, seq_count, heads_loc, head_dim)
    keys_raw = projected[:, q_cols : q_cols + kv_cols].reshape(
        group_rows, seq_count, kv_loc, head_dim
    )
    value_rows = projected[:, q_cols + kv_cols :].astype(bf16)
    query_normed, query_inverse = rms_forward(queries, query_gain)
    key_normed, key_inverse = rms_forward(keys_raw, key_gain)
    query_rot = (
        rotate(query_normed, cosine, sine_table)
        .astype(bf16)
        .reshape(group_rows, seq_count, kv_loc, group, head_dim)
    )
    key_rot = rotate(key_normed, cosine, sine_table).astype(bf16)
    kv_width = seq_count * kv_cols
    kv_own = jnp.concatenate(
        [key_rot.reshape(group_rows, kv_width), value_rows.reshape(group_rows, kv_width)], axis=1
    )
    kv_all = gather_ctx(kv_own, "ag_kv", 3).reshape(seq_len, 2 * kv_width)
    key_all = kv_all[:, :kv_width].reshape(seq_len, seq_count, kv_loc, head_dim)
    value_all = kv_all[:, kv_width:].reshape(seq_len, seq_count, kv_loc, head_dim)

    row_top, row_total, accum = attend_keys(
        query_rot, query_pos, key_all, value_all, positions, scaling
    )
    log_total = row_top + jnp.log(row_total)
    attention = (accum / row_total[..., None]).astype(bf16)
    attention_flat = attention.transpose(3, 0, 1, 2, 4).reshape(
        group_tokens, heads_loc * head_dim
    )
    mixed = jnp.einsum("tc,dc->td", attention_flat, out_full, preferred_element_type=f32)
    residual = inputs_f.reshape(tokens, width) + scatter_wsh(
        mixed.astype(bf16).reshape(wsh_count, tokens, width), "rs_mixed", 4
    )

    moe_normed_f, inverse_two = rms_forward(residual, moe_gain)
    moe_flat = moe_normed_f.astype(bf16)
    moe_all = gather_all(moe_flat, "ag_moe", 5)
    logits = jnp.dot(moe_flat, router, preferred_element_type=f32)
    route_ids = expert_ids.reshape(tokens, top_count)
    slots = dispatch_slot.reshape(tokens, top_count)
    expert_onehot = (
        route_ids[:, :, None] == jnp.arange(expert_count, dtype=jnp.int32)[None, None, :]
    )
    named = jnp.any(expert_onehot, axis=1)
    slot_dense = jnp.sum(jnp.where(expert_onehot, slots[:, :, None] + 1, 0), axis=1) - 1
    chosen_top = jnp.max(jnp.where(named, logits, MASKED), axis=-1, keepdims=True)
    chosen_exp = jnp.where(named, jnp.exp(jnp.where(named, logits - chosen_top, 0.0)), 0.0)
    weight_dense = chosen_exp / jnp.sum(chosen_exp, axis=-1, keepdims=True)
    routing = exchange(jnp.stack([slot_dense.astype(f32).T, weight_dense.T], axis=1))
    slot_mine = routing[:, 0, :].astype(jnp.int32)
    weight_mine = routing[:, 1, :]
    picks = slot_mine[:, None, :] == jnp.arange(capacity, dtype=jnp.int32)[None, :, None]
    picks_low = picks.astype(bf16)
    slot_weight = jnp.sum(jnp.where(picks, weight_mine[:, None, :], 0.0), axis=-1)

    def take(everyone):
        return (
            jnp.einsum("dct,dtw->dcw", picks_low, everyone, preferred_element_type=f32)
            .astype(bf16)
            .reshape(device_count * capacity, width)
        )

    def put(rows):
        return jnp.einsum(
            "dct,dcw->dtw",
            picks_low,
            rows.reshape(device_count, capacity, width),
            preferred_element_type=f32,
        ).astype(bf16)

    gate_w, up_w, down_w = (expert_gate[0], expert_up[0], expert_down[0])
    rows_in = take(moe_all)
    cot_rows = take(cot_all).astype(f32)
    weight_rows = slot_weight.reshape(device_count * capacity, 1)
    route_cot = (weight_rows * cot_rows).astype(bf16)
    gate_pre = jnp.dot(rows_in, gate_w, preferred_element_type=f32)
    up_pre = jnp.dot(rows_in, up_w, preferred_element_type=f32)
    sigmoid = jax.nn.sigmoid(gate_pre)
    swish = gate_pre * sigmoid
    activation = (swish * up_pre).astype(bf16)
    produced = jnp.dot(activation, down_w, preferred_element_type=f32).astype(bf16).astype(f32)
    out_parts = put((weight_rows * produced).astype(bf16))
    slot_cot = jnp.sum(cot_rows * produced, axis=-1).reshape(device_count, capacity)
    cot_mine = jnp.sum(jnp.where(picks, slot_cot[:, :, None], 0.0), axis=1)
    weight_cot = exchange(cot_mine).T
    down_grad = jnp.einsum("rf,rd->fd", activation, route_cot, preferred_element_type=f32)
    act_cot = jnp.einsum("rd,fd->rf", route_cot, down_w, preferred_element_type=f32)
    gate_cot = (act_cot * up_pre * sigmoid * (1.0 + gate_pre * (1.0 - sigmoid))).astype(bf16)
    up_cot = (act_cot * swish).astype(bf16)
    gate_grad = jnp.einsum("rd,rf->df", rows_in, gate_cot, preferred_element_type=f32)
    up_grad = jnp.einsum("rd,rf->df", rows_in, up_cot, preferred_element_type=f32)
    row_cot = jnp.einsum("rf,df->rd", gate_cot, gate_w, preferred_element_type=f32)
    row_cot = row_cot + jnp.einsum("rf,df->rd", up_cot, up_w, preferred_element_type=f32)
    row_sum = scatter_all(put(row_cot.astype(bf16)), "rs_rows", 6)
    moe_sum = scatter_all(out_parts, "rs_outputs", 7)
    outputs = (residual + moe_sum).reshape(rows_dev, seq_count, width).astype(bf16)

    chosen_cot = weight_dense * (
        weight_cot - jnp.sum(weight_dense * weight_cot, axis=-1, keepdims=True)
    )
    logit_cot = chosen_cot.astype(bf16)
    if device_count > 32:
        router_grad = lax.psum(
            jnp.einsum("td,te->de", moe_flat, logit_cot, preferred_element_type=f32),
            ("ctx", "wsh"),
        )
    else:
        router_grad = jnp.einsum(
            "td,te->de",
            moe_all.reshape(device_count * tokens, width),
            to_everyone(logit_cot, device_count).reshape(device_count * tokens, expert_count),
            preferred_element_type=f32,
        )
    normed_two_cot = (
        jnp.einsum("te,de->td", logit_cot, router, preferred_element_type=f32) + row_sum
    )
    residual_norm_cot, moe_gain_grad = rms_backward(
        residual, inverse_two, moe_gain, normed_two_cot
    )
    residual_cot = cot_flat + residual_norm_cot
    residual_low = residual_cot.astype(bf16)
    residual_flat = gather_wsh(residual_low, "ag_residual", 8).reshape(group_tokens, width)

    out_grad = jnp.einsum(
        "td,tc->dc", residual_flat, attention_flat, preferred_element_type=f32
    ).astype(bf16)
    out_weight_grad = (
        lax.psum_scatter(out_grad, "ctx", scatter_dimension=0, tiled=True).astype(f32).T
    )
    attention_cot = jnp.einsum(
        "td,dc->tc", residual_flat, out_full, preferred_element_type=f32
    ).astype(bf16)
    attention_cot = attention_cot.reshape(group_rows, seq_count, kv_loc, group, head_dim)
    attention_q = attention_flat.reshape(group_rows, seq_count, kv_loc, group, head_dim)
    delta = jnp.sum(attention_cot.astype(f32) * attention_q.astype(f32), axis=-1).transpose(
        1, 2, 3, 0
    )
    query_rot_cot, key_cot_all, value_cot_all = attend_grads(
        query_rot,
        query_pos,
        key_all,
        value_all,
        positions,
        attention_cot,
        delta,
        log_total,
        scaling,
    )
    kv_cot_all = jnp.concatenate(
        [key_cot_all.reshape(seq_len, kv_width), value_cot_all.reshape(seq_len, kv_width)], axis=1
    ).astype(bf16)
    kv_cot = scatter_ctx(kv_cot_all.reshape(ctx_count, group_rows, 2 * kv_width), "rs_kv", 9)
    key_cot_own = kv_cot[:, :kv_width]
    value_cot_own = kv_cot[:, kv_width:]
    query_cot, query_gain_grad = rms_backward(
        queries,
        query_inverse,
        query_gain,
        unrotate(
            query_rot_cot.reshape(group_rows, seq_count, heads_loc, head_dim), cosine, sine_table
        ),
    )
    key_cot, key_gain_grad = rms_backward(
        keys_raw,
        key_inverse,
        key_gain,
        unrotate(key_cot_own.reshape(group_rows, seq_count, kv_loc, head_dim), cosine, sine_table),
    )
    query_low = query_cot.astype(bf16).reshape(group_tokens, q_cols)
    key_low = key_cot.astype(bf16).reshape(group_tokens, kv_cols)
    value_low = value_cot_own.astype(bf16).reshape(group_tokens, kv_cols)
    low = jnp.concatenate([query_low, key_low, value_low], axis=1)
    summed = jnp.einsum("tq,cq->tc", low, qkv_full, preferred_element_type=f32)
    normed_cot = scatter_wsh(
        summed.astype(bf16).reshape(wsh_count, tokens, width), "rs_normed", 10
    )
    qkv_grad = jnp.einsum("tc,tq->cq", normed_flat, low, preferred_element_type=f32).astype(bf16)
    qkv_grad = scatter_ctx(
        qkv_grad.reshape(ctx_count, width // ctx_count, q_cols + 2 * kv_cols), "rs_qkv", 11
    )
    inputs_flat = inputs_f.reshape(tokens, width)
    input_norm_cot, norm_gain_grad = rms_backward(
        inputs_flat, inverse_one.reshape(tokens, 1), norm_gain, normed_cot
    )
    input_grad = (residual_cot + input_norm_cot).reshape(rows_dev, seq_count, width)
    gains = jnp.concatenate([norm_gain_grad, moe_gain_grad, query_gain_grad, key_gain_grad])
    gains = jnp.sum(to_everyone(gains, device_count), axis=0)
    return (
        outputs,
        input_grad,
        gains[:width],
        qkv_grad[:, :q_cols],
        qkv_grad[:, q_cols : q_cols + kv_cols],
        qkv_grad[:, q_cols + kv_cols :],
        gains[2 * width : 2 * width + head_dim],
        gains[2 * width + head_dim :],
        out_weight_grad,
        gains[width : 2 * width],
        router_grad,
        gate_grad[None],
        up_grad[None],
        down_grad[None],
    )


def solution(mesh):
    return jax.shard_map(
        local,
        mesh=mesh,
        in_specs=(
            P(("ctx", "wsh"), None, None),
            P(),
            P(),
            P("ctx", "wsh"),
            P("ctx", "wsh"),
            P("ctx", "wsh"),
            P(),
            P(),
            P("wsh", "ctx"),
            P(),
            P(),
            P(("ctx", "wsh"), None, None),
            P(("ctx", "wsh"), None, None),
            P(("ctx", "wsh"), None, None),
            P(("ctx", "wsh"), None, None),
            P(("ctx", "wsh"), None, None),
            P(("ctx", "wsh"), None, None),
        ),
        out_specs=(
            P(("ctx", "wsh"), None, None),
            P(("ctx", "wsh"), None, None),
            P(),
            P("ctx", "wsh"),
            P("ctx", "wsh"),
            P("ctx", "wsh"),
            P(),
            P(),
            P("wsh", "ctx"),
            P(),
            P(),
            P(("ctx", "wsh"), None, None),
            P(("ctx", "wsh"), None, None),
            P(("ctx", "wsh"), None, None),
        ),
        check_vma=False,
    )
```

time: 1760 us -> 1040 us (0.59)
  waiting for transfers between devices: 1140 us -> 5.55 us
  Pallas kernels: 0 us -> 581 us
  blocking collectives: 110 us -> 0 us
  local copies, waits for them, and re-layouts: 132 us -> 103 us
  matrix products: 254 us -> 229 us
    pallas_call x0 -> x11, Pallas kernels: none -> 581 us  [the longest x6 308 us: reduce_scatter(): pl.pallas_call(functools.partial(rs_kernel, nz, ux, uy, uc), out_shape=ja...]
    all_to_all x4, waiting for transfers between devices: 504 us -> 4.83 us  [exchange(): lax.all_to_all(pieces, ('ctx', 'wsh'), split_axis=0, concat_axis=0, tiled...]
    reduce_scatter x8 -> x1, waiting for transfers between devices: 432 us -> 0.01 us  [local(): lax.psum_scatter(out_grad, 'ctx', scatter_dimension=0, tiled=True)]
    all_gather x6 -> x2, waiting for transfers between devices: 108 us -> 0.01 us  [the longest x1 0.01 us: local(): out_full = lax.all_gather(out_shard, 'ctx', axis=0, tiled=True)]
    psum x1 -> x0, waiting for transfers between devices: 89.4 us -> none  [local(): lax.psum((norm_gain_grad, query_gain_grad, key_gain_grad, moe_gain_grad,...]
    all_gather x2 -> x0, blocking collectives: 69.2 us -> none  [the longest x1 35.4 us: local(): lax.all_gather(key_weight, 'ctx', axis=0, tiled=True)]
    psum x1 -> x0, blocking collectives: 40.7 us -> none  [local(): lax.psum((norm_gain_grad, query_gain_grad, key_gain_grad, moe_gain_grad,...]
    gather x2 -> x0, local copies, waits for them, and re-layouts: 25.4 us -> none  [the longest x1 12.9 us: local(): rows_back.reshape(-1, width)[safe_place].reshape(tokens, top_count, width)]
  transfers between devices with their start and end apart: 19 -> 7, of which waited for: 17 -> 1; matrix products, arithmetic and copies ran while one was open for 15% -> 32% of each run, Pallas kernels for 0% -> 55%
where the time goes in v1:
time: 1040 us; the launch traced here: 1030 us
  Pallas kernels  581 us (56%)
  matrix products  229 us (22%)
  local copies, waits for them, and re-layouts  103 us (10%)
  other arithmetic  76 us (7%)
  starting transfers between devices  16.6 us (2%)
  between operations  15.4 us (1%)
    pallas_call x6, Pallas kernels, reduce_scatter(): pl.pallas_call(functools.partial(rs_kernel, nz, ux, uy, uc), out_shape=ja...  308 us
    pallas_call x5, Pallas kernels, all_gather(): pl.pallas_call(functools.partial(ag_kernel, nz, ux, uy, uc), out_shape=ja...  272 us
    unnamed x203, local copies, waits for them, and re-layouts  30.6 us
    dot_general x2, matrix products, put(): jnp.einsum('dct,dcw->dtw', picks_low, rows.reshape(device_count, capacity...  26.3 us
  transfers between devices with their start and end apart: 7, of which 1 were waited for; matrix products, arithmetic and copies ran while one was open for 32% of the time, Pallas kernels for 55%

profile of v1, /device:TPU:0, one launch (start us, length us, event | category | flops | bytes accessed | tf_op | source)
XLA Modules:
  0.0 1030.0 jit_solution(9755577219092288752)
XLA Ops:
  25.1 20.3 %ag_normed.1 = bf16[4,128,2048]{2,1,0:T(8,128)(2,1)} custom-call(bf16[128,2048]{1,0:T(8,128)(2,1)} %reshape.567.x_ref), custom_call_target="tpu_custom_call" | custom-call | tf_op jit(solution)/shard_map/ag_normed/pallas_call | solution.py:301
  47.4 105.3 %ag_qkv.1 = bf16[8,256,1280]{2,1,0:T(8,128)(2,1)} custom-call(bf16[256,1280]{1,0:T(8,128)(2,1)} %pad_maximum_fusion.4.x_ref), custom_call_target="tpu_custom_call" | custom-call | tf_op jit(solution)/shard_map/ag_qkv/pallas_call | solution.py:301
  152.8 6.0 fusion.115
  169.5 51.1 %ag_kv.1 = bf16[8,256,512]{2,1,0:T(8,128)(2,1)} custom-call(bf16[256,512]{1,0:T(8,128)(2,1)} %pad_maximum_fusion.7.x_ref), custom_call_target="tpu_custom_call" | custom-call | tf_op jit(solution)/shard_map/ag_kv/pallas_call | solution.py:301
  249.2 40.2 %while.33 = (s32[]{:T(128)}, f32[2,1,8,256]{3,2,0,1:T(8,128)S(1)}, f32[2,1,8,256]{3,2,0,1:T(8,128)S(1)}, f32[2,1,8,256,128]{4,3,2,0,1:T(8,128)}, s32[2048]{0:T(1...) while((s32[]{:T(128)}, f32[2,1,8,256]{3,2,0,1:T(8,128)S(1)}, ...), condition=%wide.region_7.8_spmd.clone, body=%wide.region_4.7_spmd.clone.sunk | while | flops 1098539008 | bytes 48504064 | solution.py:616
  253.8 4.1 bitcast_add_fusion.7
  263.9 4.1 bitcast_add_fusion.7
  273.9 4.1 bitcast_add_fusion.7
  284.0 4.1 bitcast_add_fusion.7
  294.4 6.2 convolution_convert_fusion.7
  300.6 18.2 %rs_mixed.1 = f32[128,2048]{1,0:T(8,128)} custom-call(bf16[4,128,2048]{2,1,0:T(8,128)(2,1)} %bitcast.445), custom_call_target="tpu_custom_call" | custom-call | tf_op jit(solution)/shard_map/rs_mixed/pallas_call | solution.py:554
  324.2 5.2 all-to-all-start
  334.8 77.0 %ag_moe.1 = bf16[32,128,2048]{2,1,0:T(8,128)(2,1)} custom-call(bf16[128,2048]{1,0:T(8,128)(2,1)} %copy-done.23), custom_call_target="tpu_custom_call" | custom-call | tf_op jit(solution)/shard_map/ag_moe/pallas_call | solution.py:301
  411.8 8.2 convolution_convert_fusion.5
  420.1 5.2 fusion.70
  427.5 7.5 multiply_convert_fusion.2
  435.1 8.2 convolution_convert_fusion.4
  443.3 7.1 fusion.58
  451.5 4.0 fusion.59
  455.6 10.2 multiply_convert_fusion
  465.8 7.6 convolution_bitcast_fusion.3
  473.4 8.0 fusion.68
  481.4 3.7 all-to-all-start.1
  485.2 9.3 fusion.60
  494.5 7.0 convolution_bitcast_fusion.1
  501.5 10.0 convolution_bitcast_fusion.2
  511.5 7.5 add_convert_fusion
  519.1 13.1 %convolution_convert_fusion.p_ref = bf16[32,128,2048]{2,1,0:T(8,128)(2,1)} fusion(bf16[32,48,2048]{2,1,0:T(8,128)(2,1)} %bitcast.428, s32[32,128]{1,0:T(8,128)S(1)} %bitcast.449), kind=kOutput, calls=%fused_computation.65 | convolution fusion | flops 813891584 | bytes 23085056 | tf_op jit(solution)/shard_map/dct,dcw->dtw/dot_general | solution.py:840
  532.2 13.2 %convolution_convert_fusion.1.p_ref = bf16[32,128,2048]{2,1,0:T(8,128)(2,1)} fusion(bf16[32,48,2048]{2,1,0:T(8,128)(2,1)} %bitcast.407, s32[32,128]{1,0:T(8,128)S(1)} %bitcast.450), kind=kOutput, calls=%fused_computation.66 | convolution fusion | flops 813891584 | bytes 23085056 | tf_op jit(solution)/shard_map/dct,dcw->dtw/dot_general | solution.py:840
  545.3 84.6 %rs_rows.1 = f32[128,2048]{1,0:T(8,128)} custom-call(bf16[32,128,2048]{2,1,0:T(8,128)(2,1)} %convolution_convert_fusion.p_ref), custom_call_target="tpu_custom_call" | custom-call | tf_op jit(solution)/shard_map/rs_rows/pallas_call | solution.py:554
  630.0 83.3 %rs_outputs.1 = f32[128,2048]{1,0:T(8,128)} custom-call(bf16[32,128,2048]{2,1,0:T(8,128)(2,1)} %convolution_convert_fusion.1.p_ref), custom_call_target="tpu_custom_call" | custom-call | tf_op jit(solution)/shard_map/rs_outputs/pallas_call | solution.py:554
  716.7 18.6 %ag_residual.1 = bf16[4,128,2048]{2,1,0:T(8,128)(2,1)} custom-call(bf16[128,2048]{1,0:T(8,128)(2,1)} %get-tuple-element.623.x_ref), custom_call_target="tpu_custom_call" | custom-call | tf_op jit(solution)/shard_map/ag_residual/pallas_call | solution.py:301
  735.2 5.2 fusion.77
  745.0 4.4 convolution_convert_fusion.6
  751.4 56.5 %while.34 = (s32[]{:T(128)}, f32[256,2,1,8,128]{0,4,3,1,2:T(8,128)S(1)}, bf16[4,512,2,1,128]{4,1,2,3,0:T(8,128)(2,1)}, bf16[4,512,2,1,128]{4,1,2,3,0:T(8,128)(2,...) while((s32[]{:T(128)}, ...), condition=%wide.region_20.21_spmd.clone, body=%wide.region_19.20_spmd.clone.sunk | while | flops 2707161088 | bytes 69393800 | solution.py:662
  757.5 4.0 fusion.183
  771.6 4.0 fusion.183
  785.8 4.0 fusion.183
  799.9 4.0 fusion.183
  818.6 39.3 %rs_kv.1 = f32[256,512]{1,0:T(8,128)} custom-call(bf16[8,256,512]{2,1,0:T(8,128)(2,1)} %pad_maximum_fusion.1.p_ref), custom_call_target="tpu_custom_call" | custom-call | tf_op jit(solution)/shard_map/rs_kv/pallas_call | solution.py:554
  860.3 3.5 all-to-all-start.3
  883.1 4.1 convolution_convert_fusion.8
  887.3 17.8 %rs_normed.1 = f32[128,2048]{1,0:T(8,128)} custom-call(bf16[4,128,2048]{2,1,0:T(8,128)(2,1)} %bitcast.444), custom_call_target="tpu_custom_call" | custom-call | tf_op jit(solution)/shard_map/rs_normed/pallas_call | solution.py:554
  909.4 4.7 convolution_convert_fusion.2
  924.4 65.2 %rs_qkv.1 = f32[256,1280]{1,0:T(8,128)} custom-call(bf16[8,256,1280]{2,1,0:T(8,128)(2,1)} %bitcast.433), custom_call_target="tpu_custom_call" | custom-call | tf_op jit(solution)/shard_map/rs_qkv/pallas_call | solution.py:554
  995.7 4.1 all-to-all-start.2
  1001.6 9.7 convolution_bitcast_fusion.4
  1011.2 4.8 all-to-all-done.2
  (445 shorter events, 210.2 us)
Async XLA Ops:
  7.2 436.1 %copy-start = (bf16[1,768,2048]{2,1,0:T(8,128)(2,1)S(1)}, bf16[1,768,2048]{2,1,0:T(8,128)(2,1)}, u32[]{:S(2)}) copy-start(bf16[1,768,2048]{2,1,0:T(8,128)(2,1)} %param.34) | copy-start | bytes 9437188
  7.2 10.1 copy-start.76
  7.2 10.8 %copy-start.75 = (s32[64,2,8]{0,2,1:T(8,128)S(1)}, s32[64,2,8]{0,2,1:T(8,128)}, u32[]{:S(2)}) copy-start(s32[64,2,8]{0,2,1:T(8,128)} %param.35) | copy-start | bytes 12292
  7.2 11.0 %copy-start.86 = (s32[8]{0:T(128)S(1)}, s32[8]{0:T(128)}, u32[]{:S(2)}) copy-start(s32[8]{0:T(128)} %param.22) | copy-start | bytes 100
  7.2 287.2 %all-gather.3.cloned.1.call-start = ((), (), s32[]{:S(2)}) async-start(), calls=%async_computation.5 | async-start | bytes 4718592 | tf_op jit(solution)/shard_map/all_gather | solution.py:770
  8.0 427.1 %all-gather.5.cloned.1.call-start = ((), (), s32[]{:S(2)}) async-start(), calls=%async_computation.6 | async-start | bytes 17301504 | tf_op jit(solution)/shard_map/all_gather | solution.py:772
  19.4 226.1 %copy-start.38 = (f32[256,64]{0,1:T(8,128)}, f32[256,64]{0,1:T(8,128)S(1)}, u32[]{:S(2)}) copy-start(f32[256,64]{0,1:T(8,128)S(1)} %get-tuple-element.664) | copy-start | bytes 196612
  19.5 147.5 %copy-start.33 = (f32[256,64]{1,0:T(8,128)}, f32[256,64]{1,0:T(8,128)S(1)}, u32[]{:S(2)}) copy-start(f32[256,64]{1,0:T(8,128)S(1)} %copy.209) | copy-start | bytes 196612
  20.5 146.5 %copy-start.35 = (f32[256,64]{1,0:T(8,128)}, f32[256,64]{1,0:T(8,128)S(1)}, u32[]{:S(2)}) copy-start(f32[256,64]{1,0:T(8,128)S(1)} %copy.210) | copy-start | bytes 196612
  152.8 12.9 %copy-start.81 = (f32[128]{0:T(128)S(1)}, f32[128]{0:T(128)}, u32[]{:S(2)}) copy-start(f32[128]{0:T(128)} %param.28) | copy-start | bytes 1540
  164.8 58.8 %copy-start.66 = (f32[512]{0:T(512)}, f32[512]{0:T(512)S(1)}, u32[]{:S(2)}) copy-start(f32[512]{0:T(512)S(1)} %get-tuple-element.663) | copy-start | bytes 6148
  289.4 11.3 %copy-start.36 = (f32[2,1,8,256]{3,2,0,1:T(8,128)}, f32[2,1,8,256]{3,2,0,1:T(8,128)S(1)}, u32[]{:S(2)}) copy-start(f32[2,1,8,256]{3,2,0,1:T(8,128)S(1)} %get-tuple-element.240) | copy-start | bytes 49156
  289.4 11.3 %copy-start.59 = (s32[256]{0:T(256)}, s32[256]{0:T(256)S(1)}, u32[]{:S(2)}) copy-start(s32[256]{0:T(256)S(1)} %get-tuple-element.923) | copy-start | bytes 3076
  289.4 11.3 %copy-start.61 = (s32[2048]{0:T(1024)}, s32[2048]{0:T(1024)S(1)}, u32[]{:S(2)}) copy-start(s32[2048]{0:T(1024)S(1)} %get-tuple-element.924) | copy-start | bytes 24580
  293.2 29.7 %copy-start.56 = (pred[128,32]{0,1:T(8,128)(4,1)}, pred[128,32]{0,1:T(8,128)(4,1)S(1)}, u32[]{:S(2)}) copy-start(pred[128,32]{0,1:T(8,128)(4,1)S(1)} %fusion.89) | copy-start | bytes 12292
  300.6 21.0 %copy-start.62 = (f32[2048]{0:T(1024)S(1)}, f32[2048]{0:T(1024)}, u32[]{:S(2)}) copy-start(f32[2048]{0:T(1024)} %param.30) | copy-start | bytes 24580
  318.8 10.5 %copy-start.82 = (f32[128]{0:T(128)S(1)}, f32[128]{0:T(128)}, u32[]{:S(2)}) copy-start(f32[128]{0:T(128)} %rsqrt.67) | copy-start | bytes 1540
  322.9 88.9 %copy-start.71 = (f32[128]{0:T(128)}, f32[128]{0:T(128)S(1)}, u32[]{:S(2)}) copy-start(f32[128]{0:T(128)S(1)} %get-tuple-element.668) | copy-start | bytes 1540
  323.5 88.3 %copy-start.73 = (f32[128]{0:T(128)}, f32[128]{0:T(128)S(1)}, u32[]{:S(2)}) copy-start(f32[128]{0:T(128)S(1)} %fusion.95) | copy-start | bytes 1540
  324.2 87.6 %all-to-all-start = ((f32[32,2,128]{2,1,0:T(2,128)}), f32[32,2,128]{2,1,0:T(2,128)S(1)}, u32[]{:S(2)}, u32[]{:S(2)}) async-start(f32[32,2,128]{2,1,0:T(2,128)} %copy.223), calls=%async_computation | async-start | bytes 65536 | tf_op jit(solution)/shard_map/all_to_all | solution.py:711
  333.0 78.8 %copy-start.29 = (f32[256,2,8]{2,1,0:T(2,128)}, f32[256,2,8]{2,1,0:T(2,128)S(1)}, u32[]{:S(2)}) copy-start(f32[256,2,8]{2,1,0:T(2,128)S(1)} %copy.261) | copy-start | bytes 49156
  451.5 14.2 %slice-start = ((s8[6291456]{0:T(1024)(128)(4,1)}), s8[2097152]{0:T(1024)(128)(4,1)S(1)}, s32[]{:S(2)}) async-start(s8[6291456]{0:T(1024)(128)(4,1)} %bitcast.413), calls=%async_computation.8 | async-start | bytes 4194304
  455.6 10.2 slice-start.1
  481.4 231.9 %all-to-all-start.1 = ((f32[32,1,128]{2,1,0:T(1,128)}), f32[32,1,128]{2,1,0:T(1,128)S(1)}, u32[]{:S(2)}, u32[]{:S(2)}) async-start(f32[32,1,128]{2,1,0:T(1,128)} %bitcast.27), calls=%async_computation.1 | async-start | bytes 32768 | tf_op jit(solution)/shard_map/all_to_all | solution.py:711
  485.1 533.4 %reduce-scatter.2.cloned.1.call-start = ((), (), s32[]{:S(2)}) async-start(), calls=%async_computation.7 | async-start | bytes 4718592 | tf_op jit(solution)/shard_map/reduce_scatter | solution.py:904
  494.5 17.0 %slice-start.5 = ((s8[12582912]{0:T(1024)(128)(4,1)}), s8[4194304]{0:T(1024)(128)(4,1)S(1)}, s32[]{:S(2)}) async-start(s8[12582912]{0:T(1024)(128)(4,1)} %bitcast.468), calls=%async_computation.13 | async-start | bytes 8388608
  494.5 17.0 %slice-start.6 = ((s8[12582912]{0:T(1024)(128)(4,1)}), s8[4194304]{0:T(1024)(128)(4,1)S(1)}, s32[]{:S(2)}) async-start(s8[12582912]{0:T(1024)(128)(4,1)} %bitcast.468), calls=%async_computation.14 | async-start | bytes 8388608
  629.9 83.5 %copy-start.55 = (f32[128,32]{0,1:T(8,128)S(1)}, f32[128,32]{0,1:T(8,128)}, u32[]{:S(2)}) copy-start(f32[128,32]{0,1:T(8,128)} %copy-done.54) | copy-start | bytes 49156
  630.0 83.5 %copy-start.57 = (pred[128,32]{0,1:T(8,128)(4,1)S(1)}, pred[128,32]{0,1:T(8,128)(4,1)}, u32[]{:S(2)}) copy-start(pred[128,32]{0,1:T(8,128)(4,1)} %copy-done.56) | copy-start | bytes 12292
  630.0 83.5 %copy-start.72 = (f32[128]{0:T(128)S(1)}, f32[128]{0:T(128)}, u32[]{:S(2)}) copy-start(f32[128]{0:T(128)} %copy-done.71) | copy-start | bytes 1540
  630.0 83.5 %copy-start.74 = (f32[128]{0:T(128)S(1)}, f32[128]{0:T(128)}, u32[]{:S(2)}) copy-start(f32[128]{0:T(128)} %copy-done.73) | copy-start | bytes 1540
  630.0 83.5 %copy-start.8 = (f32[128,2048]{1,0:T(8,128)S(1)}, f32[128,2048]{1,0:T(8,128)}, u32[]{:S(2)}) copy-start(f32[128,2048]{1,0:T(8,128)} %copy-done.7) | copy-start | bytes 3145732
  630.0 83.5 %copy-start.25 = (f32[128,2048]{1,0:T(8,128)S(1)}, f32[128,2048]{1,0:T(8,128)}, u32[]{:S(2)}) copy-start(f32[128,2048]{1,0:T(8,128)} %rs_rows.1) | copy-start | bytes 3145732
  630.0 83.5 %copy-start.52 = (bf16[2048,32]{0,1:T(8,128)(2,1)S(1)}, bf16[2048,32]{0,1:T(8,128)(2,1)}, u32[]{:S(2)}) copy-start(bf16[2048,32]{0,1:T(8,128)(2,1)} %param.31) | copy-start | bytes 393220
  630.0 83.5 %copy-start.63 = (f32[2048]{0:T(1024)S(1)}, f32[2048]{0:T(1024)}, u32[]{:S(2)}) copy-start(f32[2048]{0:T(1024)} %param.30) | copy-start | bytes 24580
  630.0 83.5 %copy-start.78 = (f32[128]{0:T(128)S(1)}, f32[128]{0:T(128)}, u32[]{:S(2)}) copy-start(f32[128]{0:T(128)} %copy-done.77) | copy-start | bytes 1540
  818.6 45.2 %copy-start.39 = (f32[256,64]{0,1:T(8,128)S(1)}, f32[256,64]{0,1:T(8,128)}, u32[]{:S(2)}) copy-start(f32[256,64]{0,1:T(8,128)} %copy-done.38) | copy-start | bytes 196612
  818.6 45.2 %copy-start.41 = (f32[256,64]{0,1:T(8,128)S(1)}, f32[256,64]{0,1:T(8,128)}, u32[]{:S(2)}) copy-start(f32[256,64]{0,1:T(8,128)} %get-tuple-element.665) | copy-start | bytes 196612
  860.3 134.3 %all-to-all-start.3 = ((bf16[32,128,32]{1,2,0:T(8,128)(2,1)}), bf16[32,128,32]{1,2,0:T(8,128)(2,1)}, u32[]{:S(2)}, u32[]{:S(2)}) async-start(bf16[32,128,32]{1,2,0:T(8,128)(2,1)} %broadcast_in_dim.193), calls=%async_computation.4 | async-start | bytes 524288 | tf_op jit(solution)/shard_map/all_to_all | solution.py:711
  887.3 17.8 %copy-start.6 = (f32[128,2048]{1,0:T(8,128)S(1)}, f32[128,2048]{1,0:T(8,128)}, u32[]{:S(2)}) copy-start(f32[128,2048]{1,0:T(8,128)} %reshape.566) | copy-start | bytes 3145732
  887.3 17.8 %copy-start.64 = (f32[2048]{0:T(1024)S(1)}, f32[2048]{0:T(1024)}, u32[]{:S(2)}) copy-start(f32[2048]{0:T(1024)} %param.23) | copy-start | bytes 24580
  887.3 17.8 %copy-start.83 = (f32[128]{0:T(128)S(1)}, f32[128]{0:T(128)}, u32[]{:S(2)}) copy-start(f32[128]{0:T(128)} %rsqrt.67) | copy-start | bytes 1540
  887.3 19.5 %copy-start.26 = (f32[128,2048]{1,0:T(8,128)S(1)}, f32[128,2048]{1,0:T(8,128)}, u32[]{:S(2)}) copy-start(f32[128,2048]{1,0:T(8,128)} %get-tuple-element.624) | copy-start | bytes 3145732
  887.3 19.5 %copy-start.84 = (f32[128]{0:T(128)S(1)}, f32[128]{0:T(128)}, u32[]{:S(2)}) copy-start(f32[128]{0:T(128)} %multiply_multiply_fusion.4) | copy-start | bytes 1540
  924.4 67.7 %copy-start.18 = (f32[256,2,8,64]{3,2,1,0:T(8,128)S(1)}, f32[256,2,8,64]{3,2,1,0:T(8,128)}, u32[]{:S(2)}) copy-start(f32[256,2,8,64]{3,2,1,0:T(8,128)} %copy.236) | copy-start | bytes 3145732
  924.4 67.7 %copy-start.65 = (f32[4096]{0:T(1024)S(1)}, f32[4096]{0:T(1024)}, u32[]{:S(2)}) copy-start(f32[4096]{0:T(1024)} %rsqrt.68) | copy-start | bytes 49156
  995.7 20.3 %all-to-all-start.2 = ((f32[32,1,4352]{2,1,0:T(1,128)}), f32[32,1,4352]{2,1,0:T(1,128)}, u32[]{:S(2)}, u32[]{:S(2)}) async-start(f32[32,1,4352]{2,1,0:T(1,128)} %broadcast_in_dim.192), calls=%async_computation.2 | async-start | bytes 1114112 | tf_op jit(solution)/shard_map/all_to_all | solution.py:711
  1001.6 21.7 %copy-start.1 = (bf16[1,768,2048]{2,1,0:T(8,128)(2,1)S(1)}, bf16[1,768,2048]{2,1,0:T(8,128)(2,1)}, u32[]{:S(2)}) copy-start(bf16[1,768,2048]{2,1,0:T(8,128)(2,1)} %param.34) | copy-start | bytes 9437188
  (83 other events, 312.7 us)
Sparse Core Ops, SparseCore 0:
  10.1 101.9 all-gather.2
  115.5 127.6 all-gather.4
  749.6 87.5 reduce-scatter.1

commit v2 on v1

--- a/solution.py
+++ b/solution.py
@@ -7,6 +7,7 @@
 from jax.experimental import pallas as pl
 from jax.experimental.pallas import tpu as pltpu
 from jax.sharding import PartitionSpec as P
+
 
 EPSILON = 1e-06
 ROPE_BASE = 1000000.0
@@ -30,32 +31,6 @@
     frequency = ROPE_BASE ** (-(jnp.arange(half_dim, dtype=jnp.float32) * 2.0) / head_dim)
     angles = positions.astype(jnp.float32)[:, None] * frequency[None, :]
     return (jnp.cos(angles), jnp.sin(angles))
-
-
-def rotate(tensor, cosine, sine_table):
-    half_dim = tensor.shape[-1] // 2
-    first_half = tensor[..., :half_dim]
-    second_half = tensor[..., half_dim:]
-    return jnp.concatenate(
-        [
-            first_half * cosine - second_half * sine_table,
-            second_half * cosine + first_half * sine_table,
-        ],
-        axis=-1,
-    )
-
-
-def unrotate(gradient, cosine, sine_table):
-    half_dim = gradient.shape[-1] // 2
-    first_half = gradient[..., :half_dim]
-    second_half = gradient[..., half_dim:]
-    return jnp.concatenate(
-        [
-            first_half * cosine + second_half * sine_table,
-            second_half * cosine - first_half * sine_table,
-        ],
-        axis=-1,
-    )
 
 
 def rms_forward(tensor, gain_vector):
@@ -132,12 +107,12 @@
         pl.when(cond)(fn)
 
 
-def ag_kernel(nz, ux, uy, uc, x_ref, o_ref, ssem, rsem, lsem):
+def gather_job(axes, x_ref, o_ref, ssem, rsem, lsem):
+    nz, ux, uy, uc = axes
     pc = Place(nz, ux, uy, uc)
     z, x, y, c = pc.z, pc.x, pc.y, pc.c
     rows = x_ref.shape[0]
     half = rows // 2
-    pc.greet()
     to_x, to_y, to_c = pc.dev(z, 1 - x, y, c), pc.dev(z, x, 1 - y, c), pc.dev(z, x, y, 1 - c)
 
     def part(b, p):
@@ -159,7 +134,6 @@
         )
 
     own = pltpu.make_async_copy(x_ref, o_ref.at[pc.blk(z, x, y, c)], lsem)
-    own.start()
 
     def hops(d, side, s):
         out = []
@@ -265,7 +239,8 @@
         when(ok, fn)
 
     groups = [[st for st in steps if st[0] == d] for d in range(nz)]
-    for t in range(nz + 2):
+
+    def phase(t):
         if t < nz:
             for st in groups[t]:
                 do_line(st)
@@ -276,51 +251,93 @@
             for st in groups[t - 2]:
                 do_pass(st, across)
 
-    for st in steps:
-        d, side, s, ok = st
-
-        def fn():
-            for cp in partner(d, side, s):
-                cp.wait_recv()
-            for cond, cp in hops(d, side, s):
-                when(cond, cp.wait_send)
-            for cp in spread(d, side, s):
-                cp.wait_send()
-            for which in (passed, across):
-                for _, go in which(d, side, s):
-                    for cp in go:
-                        cp.wait_send()
-
-        when(ok, fn)
-    own.wait()
-
-
-def all_gather(shard, nz, ux, uy, uc, collective_id, name):
-    group = (nz * 2 if ux else 1) * (4 if uc else 1)
-    nsem = nz * 20
+    def last():
+        for st in steps:
+            d, side, s, ok = st
+
+            def fn():
+                for cp in partner(d, side, s):
+                    cp.wait_recv()
+                for cond, cp in hops(d, side, s):
+                    when(cond, cp.wait_send)
+                for cp in spread(d, side, s):
+                    cp.wait_send()
+                for which in (passed, across):
+                    for _, go in which(d, side, s):
+                        for cp in go:
+                            cp.wait_send()
+
+            when(ok, fn)
+        own.wait()
+
+    return own.start, [functools.partial(phase, t) for t in range(nz + 2)], last
+
+
+WSH_AXES = (1, False, True, True)
+CTX_AXES = (4, True, False, False)
+ALL_AXES = (4, True, True, True)
+
+
+def run_jobs(axes_list, jobs):
+    Place(
+        max(a[0] for a in axes_list),
+        any(a[1] for a in axes_list),
+        any(a[2] for a in axes_list),
+        any(a[3] for a in axes_list),
+    ).greet()
+    for begin, _, _ in jobs:
+        begin()
+    for t in range(max(len(phases) for _, phases, _ in jobs)):
+        for _, phases, _ in jobs:
+            if t < len(phases):
+                phases[t]()
+    for _, _, last in jobs:
+        last()
+
+
+def group_of(axes):
+    return (axes[0] * 2 if axes[1] else 1) * (4 if axes[3] else 1)
+
+
+def gather_kernel(axes_list, *refs):
+    n = len(axes_list)
+    jobs = [
+        gather_job(axes_list[i], refs[i], refs[n + i], *refs[2 * n + 3 * i : 2 * n + 3 * i + 3])
+        for i in range(n)
+    ]
+    run_jobs(axes_list, jobs)
+
+
+def gather_sems(axes):
+    return [
+        pltpu.SemaphoreType.DMA((axes[0] * 20,)),
+        pltpu.SemaphoreType.DMA((axes[0] * 20,)),
+        pltpu.SemaphoreType.DMA,
+    ]
+
+
+def all_gather(shards, axes_list, collective_id):
     return pl.pallas_call(
-        functools.partial(ag_kernel, nz, ux, uy, uc),
-        out_shape=jax.ShapeDtypeStruct((group,) + shard.shape, shard.dtype),
-        in_specs=[pl.BlockSpec(memory_space=pl.ANY)],
-        out_specs=pl.BlockSpec(memory_space=pl.ANY),
-        scratch_shapes=[
-            pltpu.SemaphoreType.DMA((nsem,)),
-            pltpu.SemaphoreType.DMA((nsem,)),
-            pltpu.SemaphoreType.DMA,
+        functools.partial(gather_kernel, axes_list),
+        out_shape=[
+            jax.ShapeDtypeStruct((group_of(axes),) + shard.shape, shard.dtype)
+            for shard, axes in zip(shards, axes_list)
         ],
+        in_specs=[pl.BlockSpec(memory_space=pl.ANY)] * len(shards),
+        out_specs=[pl.BlockSpec(memory_space=pl.ANY)] * len(shards),
+        scratch_shapes=[x for axes in axes_list for x in gather_sems(axes)],
         compiler_params=pltpu.CompilerParams(collective_id=collective_id, has_side_effects=True),
-        name=name,
-    )(shard)
-
-
-def rs_kernel(nz, ux, uy, uc, p_ref, o_ref, acc, rc, rx, ry, ra, rb, rz, ssem, rsem, lsem):
+    )(*shards)
+
+
+def scatter_job(axes, p_ref, o_ref, acc, rc, rx, ry, ra, rb, rz, ssem, rsem, lsem):
+    nz, ux, uy, uc = axes
     pc = Place(nz, ux, uy, uc)
     z, x, y, c = pc.z, pc.x, pc.y, pc.c
-    rows, cols = o_ref.shape
+    rows, _ = o_ref.shape
     half = rows // 2
     chunk = math.gcd(half, 32)
     f32 = jnp.float32
-    pc.greet()
     to_x, to_y, to_c = pc.dev(z, 1 - x, y, c), pc.dev(z, x, 1 - y, c), pc.dev(z, x, y, 1 - c)
     rels = [(0, x, y)]
     if ux:
@@ -386,7 +403,7 @@
     def z_send(s, up):
         return rcopy(
             acc.at[slot(s) * 4],
-            rz.at[slot(s)] if up is None else rz.at[slot(s)],
+            rz.at[slot(s)],
             s,
             10,
             pc.dev(z + (1 if up else -1), x, y, c),
@@ -404,18 +421,19 @@
 
     steps = list(reversed(pc.line_steps()))
 
-    for d, side, s, ok in steps:
-
-        def fn():
-            for rel, px, py in reversed(rels):
-                load(s, rel, px, py).start()
-                if uc:
-                    give(s, rel, px, py).start()
-
-        when(ok, fn)
+    def begin():
+        for d, side, s, ok in steps:
+
+            def fn():
+                for rel, px, py in reversed(rels):
+                    load(s, rel, px, py).start()
+                    if uc:
+                        give(s, rel, px, py).start()
+
+            when(ok, fn)
 
     def first(step):
-        d, side, s, ok = step
+        _, _, s, ok = step
 
         def fn():
             for rel, px, py in reversed(rels):
@@ -438,7 +456,7 @@
         when(ok, fn)
 
     def second(step):
-        d, side, s, ok = step
+        _, _, s, ok = step
 
         def fn():
             if ux and uy:
@@ -514,7 +532,8 @@
         when(ok, fn)
 
     groups = [[st for st in steps if st[0] == d] for d in reversed(range(nz))]
-    for t in range(nz + 2):
+
+    def phase(t):
         if t < nz:
             for st in groups[t]:
                 first(st)
@@ -525,186 +544,505 @@
             for st in groups[t - 2]:
                 third(st)
 
-    for d, side, s, ok in steps:
-
-        def fn():
-            for rel, px, py in rels:
-                if uc:
-                    give(s, rel, px, py).wait_send()
-            if ux and uy:
-                over_a(s).wait_send()
-                over_b(s).wait_send()
-            if ux:
-                x_half(s, 0).wait_send()
-                x_half(s, 1).wait_send()
-            if uy:
-                y_half(s, 0).wait_send()
-                y_half(s, 1).wait_send()
-            if d > 0:
-                z_send(s, side == 1).wait_send()
-
-        when(ok, fn)
-
-
-def reduce_scatter(parts, nz, ux, uy, uc, out_dtype, collective_id, name):
-    group, rows, cols = parts.shape
-    dt = parts.dtype
-    lines = nz
-    buf = lambda n, r: pltpu.VMEM((n, r, cols), dt)
+    def last():
+        for d, side, s, ok in steps:
+
+            def fn():
+                for rel, px, py in rels:
+                    if uc:
+                        give(s, rel, px, py).wait_send()
+                if ux and uy:
+                    over_a(s).wait_send()
+                    over_b(s).wait_send()
+                if ux:
+                    x_half(s, 0).wait_send()
+                    x_half(s, 1).wait_send()
+                if uy:
+                    y_half(s, 0).wait_send()
+                    y_half(s, 1).wait_send()
+                if d > 0:
+                    z_send(s, side == 1).wait_send()
+
+            when(ok, fn)
+
+    return begin, [functools.partial(phase, t) for t in range(nz + 2)], last
+
+
+def scatter_kernel(axes_list, *refs):
+    n = len(axes_list)
+    jobs = [
+        scatter_job(axes_list[i], refs[i], refs[n + i], *refs[2 * n + 10 * i : 2 * n + 10 * i + 10])
+        for i in range(n)
+    ]
+    run_jobs(axes_list, jobs)
+
+
+def scatter_scratch(axes, rows, cols, dt):
+    nz, ux, uy, uc = axes
+    few = lambda use, n, r: pltpu.VMEM((n, r, cols) if use else (1, 16, cols), dt)
+    return [
+        few(True, nz * 4, rows),
+        few(uc, nz * 4, rows),
+        few(ux, nz, rows),
+        few(uy, nz, rows),
+        few(ux and uy, nz, rows // 2),
+        few(ux and uy, nz, rows // 2),
+        few(nz > 1, nz + 1, rows),
+        pltpu.SemaphoreType.DMA((nz * 12,)),
+        pltpu.SemaphoreType.DMA((nz * 12,)),
+        pltpu.SemaphoreType.DMA((nz * 4,)),
+    ]
+
+
+def reduce_scatter(parts, axes_list, collective_id):
     return pl.pallas_call(
-        functools.partial(rs_kernel, nz, ux, uy, uc),
-        out_shape=jax.ShapeDtypeStruct((rows, cols), out_dtype),
-        in_specs=[pl.BlockSpec(memory_space=pl.ANY)],
-        out_specs=pl.BlockSpec(memory_space=pltpu.VMEM),
+        functools.partial(scatter_kernel, axes_list),
+        out_shape=[jax.ShapeDtypeStruct(p.shape[1:], jnp.float32) for p in parts],
+        in_specs=[pl.BlockSpec(memory_space=pl.ANY)] * len(parts),
+        out_specs=[pl.BlockSpec(memory_space=pltpu.VMEM)] * len(parts),
         scratch_shapes=[
-            buf(lines * 4, rows),
-            buf(lines * 4 if uc else 1, rows if uc else 16),
-            buf(lines if ux else 1, rows if ux else 16),
-            buf(lines if uy else 1, rows if uy else 16),
-            buf(lines if ux and uy else 1, rows // 2 if ux and uy else 16),
-            buf(lines if ux and uy else 1, rows // 2 if ux and uy else 16),
-            buf(lines + 1 if nz > 1 else 1, rows if nz > 1 else 16),
-            pltpu.SemaphoreType.DMA((lines * 12,)),
-            pltpu.SemaphoreType.DMA((lines * 12,)),
-            pltpu.SemaphoreType.DMA((lines * 4,)),
+            x
+            for axes, p in zip(axes_list, parts)
+            for x in scatter_scratch(axes, p.shape[1], p.shape[2], p.dtype)
         ],
         compiler_params=pltpu.CompilerParams(
             collective_id=collective_id, has_side_effects=True, vmem_limit_bytes=60 * 1024 * 1024
         ),
-        name=name,
-    )(parts)
-
-
-def score_block(query_rot, key_piece, scaling):
+    )(*parts)
+
+
+LOG2E = 1.4426950408889634
+
+
+def lane_swap(tensor):
+    return pltpu.roll(tensor, tensor.shape[-1] // 2, tensor.ndim - 1)
+
+
+def head_norm(tensor, gain, cos2, sin2):
+    inverse = lax.rsqrt(jnp.mean(tensor * tensor, axis=-1, keepdims=True) + EPSILON)
+    scaled = tensor * inverse * gain
+    return scaled * cos2 + lane_swap(scaled) * sin2
+
+
+def head_norm_back(tensor, gain, cos2, sin2, gradient):
+    inverse = lax.rsqrt(jnp.mean(tensor * tensor, axis=-1, keepdims=True) + EPSILON)
+    turned = gradient * cos2 - lane_swap(gradient) * sin2
+    weighted = turned * gain
+    inner = jnp.mean(weighted * tensor, axis=-1, keepdims=True)
     return (
-        jnp.einsum("qsagd,ksad->sagqk", query_rot, key_piece, preferred_element_type=jnp.float32)
-        * scaling
+        inverse * weighted - tensor * (inverse * inverse * inverse) * inner,
+        turned * tensor * inverse,
     )
 
 
-def attend_keys(query_rot, query_pos, key_all, value_all, key_pos, scaling):
-    length = key_all.shape[0]
-    key_block = math.gcd(length, 512)
-    block_count = length // key_block
-    query_rows, seq_count, kv_count, group, head_dim = query_rot.shape
-    start_carry = (
-        jnp.full((seq_count, kv_count, group, query_rows), MASKED, jnp.float32),
-        jnp.zeros((seq_count, kv_count, group, query_rows), jnp.float32),
-        jnp.zeros((seq_count, kv_count, group, query_rows, head_dim), jnp.float32),
+def token_rows(piece, seq, seq_count, rows_dev):
+    return (piece * seq_count + seq) * rows_dev
+
+
+def kv_prep_kernel(pieces, seqs, proj_ref, gain_ref, cos_ref, sin_ref, o_ref):
+    hd = gain_ref.shape[-1]
+    rows = proj_ref.shape[0] // (pieces * seqs)
+    for piece in range(pieces):
+        cos2 = cos_ref[piece * rows : (piece + 1) * rows, :]
+        sin2 = sin_ref[piece * rows : (piece + 1) * rows, :]
+        for seq in range(seqs):
+            at = token_rows(piece, seq, seqs, rows)
+            raw = proj_ref[at : at + rows, :hd]
+            o_ref[at : at + rows, :hd] = head_norm(raw, gain_ref[...], cos2, sin2).astype(
+                o_ref.dtype
+            )
+            o_ref[at : at + rows, hd:] = proj_ref[at : at + rows, hd:].astype(o_ref.dtype)
+
+
+def kv_prep(projected, key_gain, cos2, sin2, heads, pieces, seqs):
+    rows, _ = projected.shape
+    hd = key_gain.shape[0]
+    whole = lambda *shape: pl.BlockSpec(shape, lambda i: (0,) * len(shape))
+    return pl.pallas_call(
+        functools.partial(kv_prep_kernel, pieces, seqs),
+        grid=(1,),
+        out_shape=jax.ShapeDtypeStruct((rows, 2 * hd), jnp.bfloat16),
+        in_specs=[
+            pl.BlockSpec((rows, 2 * hd), lambda i: (0, heads // 2)),
+            whole(1, hd),
+            whole(*cos2.shape),
+            whole(*sin2.shape),
+        ],
+        out_specs=whole(rows, 2 * hd),
+        name="kv_prep",
+    )(projected, key_gain.reshape(1, hd), cos2, sin2)
+
+
+def kv_back_kernel(pieces, seqs, proj_ref, cot_ref, gain_ref, cos_ref, sin_ref, _, low_ref, gg_ref):
+    hd = gain_ref.shape[-1]
+    rows = proj_ref.shape[0] // (pieces * seqs)
+    total = jnp.zeros((1, hd), jnp.float32)
+    for piece in range(pieces):
+        cos2 = cos_ref[piece * rows : (piece + 1) * rows, :]
+        sin2 = sin_ref[piece * rows : (piece + 1) * rows, :]
+        for seq in range(seqs):
+            at = token_rows(piece, seq, seqs, rows)
+            grad, terms = head_norm_back(
+                proj_ref[at : at + rows, :hd],
+                gain_ref[...],
+                cos2,
+                sin2,
+                cot_ref[at : at + rows, :hd],
+            )
+            low_ref[at : at + rows, :hd] = grad.astype(low_ref.dtype)
+            low_ref[at : at + rows, hd:] = cot_ref[at : at + rows, hd:].astype(low_ref.dtype)
+            total = total + jnp.sum(terms, axis=0, keepdims=True)
+    gg_ref[...] = total
+
+
+def kv_back(projected, kv_cot, key_gain, cos2, sin2, low, heads, pieces, seqs):
+    rows, _ = projected.shape
+    hd = key_gain.shape[0]
+    whole = lambda *shape: pl.BlockSpec(shape, lambda i: (0,) * len(shape))
+    return pl.pallas_call(
+        functools.partial(kv_back_kernel, pieces, seqs),
+        grid=(1,),
+        out_shape=(
+            jax.ShapeDtypeStruct(low.shape, low.dtype),
+            jax.ShapeDtypeStruct((1, hd), jnp.float32),
+        ),
+        in_specs=[
+            pl.BlockSpec((rows, 2 * hd), lambda i: (0, heads // 2)),
+            whole(rows, 2 * hd),
+            whole(1, hd),
+            whole(*cos2.shape),
+            whole(*sin2.shape),
+            pl.BlockSpec(memory_space=pl.ANY),
+        ],
+        out_specs=(pl.BlockSpec((rows, 2 * hd), lambda i: (0, heads // 2)), whole(1, hd)),
+        input_output_aliases={5: 0},
+        name="kv_back",
+    )(projected, kv_cot, key_gain.reshape(1, hd), cos2, sin2, low)
+
+
+def sort_blocks(loc_ref, kv_ref, dst, seqs, rows, pieces, hd, lo, blocks):
+    per_half = pieces // 2
+
+    def body(b, _):
+        loc = loc_ref[b]
+        chunk, half = loc // 2, loc % 2
+        for seq in range(seqs):
+            for i in range(per_half):
+                at = ((half * per_half + i) * seqs + seq) * rows
+                dst[seq, pl.ds(b * (per_half * rows) + i * rows, rows), :] = kv_ref[
+                    chunk, pl.ds(at, rows), lo : lo + hd
+                ]
+        return 0
+
+    lax.fori_loop(0, blocks, body, 0)
+
+
+def attend_kernel(
+    heads, pieces, seqs, scale, loc_ref, own_ref, proj_ref, kv_ref, gain_ref, cos_ref, sin_ref,
+    attn_ref, lse_ref, qs_ref, ks, vs, acc, tot,
+):
+    f32, bf16 = jnp.float32, jnp.bfloat16
+    hd = gain_ref.shape[-1]
+    rows = proj_ref.shape[0] // (pieces * seqs)
+    per_half = pieces // 2
+    block = per_half * rows
+    blocks = 2 * kv_ref.shape[0]
+    pair = 2 * block
+    tile = 2 * block
+    sort_blocks(loc_ref, kv_ref, ks, seqs, rows, pieces, hd, 0, blocks)
+    sort_blocks(loc_ref, kv_ref, vs, seqs, rows, pieces, hd, hd, blocks)
+    for seq in range(seqs):
+        for half in range(2):
+            unit = seq * 2 + half
+            for h in range(heads):
+                for i in range(per_half):
+                    piece = half * per_half + i
+                    at = token_rows(piece, seq, seqs, rows)
+                    turned = head_norm(
+                        proj_ref[at : at + rows, h * hd : (h + 1) * hd],
+                        gain_ref[...],
+                        cos_ref[piece * rows : (piece + 1) * rows, :],
+                        sin_ref[piece * rows : (piece + 1) * rows, :],
+                    )
+                    qs_ref[unit, h * block + i * rows : h * block + (i + 1) * rows, :] = (
+                        turned.astype(bf16)
+                    )
+            acc[...] = jnp.zeros_like(acc)
+            tot[...] = jnp.zeros_like(tot)
+            mine = own_ref[half]
+
+            def step(j, masked):
+                keys = ks[seq, pl.ds(j * pair, pair), :]
+                values = vs[seq, pl.ds(j * pair, pair), :]
+                for t in range(heads * block // tile):
+                    cols = slice(t * tile, (t + 1) * tile)
+                    scores = lax.dot_general(
+                        keys,
+                        qs_ref[unit, cols, :],
+                        (((1,), (1,)), ((), ())),
+                        preferred_element_type=f32,
+                    )
+                    expo = jnp.exp2(scores * (scale * LOG2E))
+                    if masked:
+                        key_pos = j * pair + lax.broadcasted_iota(jnp.int32, expo.shape, 0)
+                        query_pos = mine * block + (
+                            lax.broadcasted_iota(jnp.int32, expo.shape, 1) % block
+                        )
+                        expo = jnp.where(key_pos <= query_pos, expo, 0.0)
+                    tot[:, cols] += jnp.sum(expo.reshape(pair // 8, 8, tile), axis=0)
+                    acc[:, cols] += lax.dot_general(
+                        values,
+                        expo.astype(bf16),
+                        (((0,), (0,)), ((), ())),
+                        preferred_element_type=f32,
+                    )
+
+            def body(j, _):
+                step(j, False)
+                return 0
+
+            lax.fori_loop(0, mine // 2, body, 0)
+            step(mine // 2, True)
+            total = jnp.sum(tot[...], axis=0, keepdims=True)
+            lse_ref[unit, :, :] = jnp.log(total)
+            share = 1.0 / total
+            for h in range(heads):
+                cols = slice(h * block, (h + 1) * block)
+                out = jnp.transpose(acc[:, cols] * share[:, cols]).astype(bf16)
+                for i in range(per_half):
+                    at = token_rows(half * per_half + i, seq, seqs, rows)
+                    attn_ref[at : at + rows, h * hd : (h + 1) * hd] = out[
+                        i * rows : (i + 1) * rows, :
+                    ]
+
+
+def attend(projected, kv_all, query_gain, cos2, sin2, loc, own, heads, pieces, seqs):
+    rows = projected.shape[0]
+    hd = query_gain.shape[0]
+    units = 2 * seqs
+    block = rows // units
+    keys = kv_all.shape[0] * kv_all.shape[1] // seqs
+    whole = lambda *shape: pl.BlockSpec(shape, lambda i, *_: (0,) * len(shape))
+    f32, bf16 = jnp.float32, jnp.bfloat16
+    return pl.pallas_call(
+        functools.partial(attend_kernel, heads, pieces, seqs, hd**-0.5),
+        grid_spec=pltpu.PrefetchScalarGridSpec(
+            num_scalar_prefetch=2,
+            grid=(1,),
+            in_specs=[
+                pl.BlockSpec((rows, heads * hd), lambda i, *_: (0, 0)),
+                whole(*kv_all.shape),
+                whole(1, hd),
+                whole(*cos2.shape),
+                whole(*sin2.shape),
+            ],
+            out_specs=[
+                whole(rows, heads * hd),
+                whole(units, 1, heads * block),
+                whole(units, heads * block, hd),
+            ],
+            scratch_shapes=[
+                pltpu.VMEM((seqs, keys, hd), bf16),
+                pltpu.VMEM((seqs, keys, hd), bf16),
+                pltpu.VMEM((hd, heads * block), f32),
+                pltpu.VMEM((8, heads * block), f32),
+            ],
+        ),
+        out_shape=(
+            jax.ShapeDtypeStruct((rows, heads * hd), bf16),
+            jax.ShapeDtypeStruct((units, 1, heads * block), f32),
+            jax.ShapeDtypeStruct((units, heads * block, hd), bf16),
+        ),
+        compiler_params=pltpu.CompilerParams(vmem_limit_bytes=56 * 1024 * 1024),
+        name="attend",
+    )(loc, own, projected, kv_all, query_gain.reshape(1, hd), cos2, sin2)
+
+
+def attend_back_kernel(
+    heads, pieces, seqs, scale, loc_ref, own_ref, proj_ref, kv_ref, qs_ref, attn_ref, cot_ref,
+    lse_ref, gain_ref, cos_ref, sin_ref, low_ref, dkv_ref, gg_ref, ks, vs, dk, dv, dq, cs, dl,
+):
+    f32, bf16 = jnp.float32, jnp.bfloat16
+    hd = gain_ref.shape[-1]
+    rows = proj_ref.shape[0] // (pieces * seqs)
+    per_half = pieces // 2
+    block = per_half * rows
+    blocks = 2 * kv_ref.shape[0]
+    pair = 2 * block
+    tile = 2 * block
+    sort_blocks(loc_ref, kv_ref, ks, seqs, rows, pieces, hd, 0, blocks)
+    sort_blocks(loc_ref, kv_ref, vs, seqs, rows, pieces, hd, hd, blocks)
+    dk[...] = jnp.zeros_like(dk)
+    dv[...] = jnp.zeros_like(dv)
+    gain_total = jnp.zeros((1, hd), f32)
+    ones = jnp.ones((8, hd), bf16)
+    nt = (((1,), (1,)), ((), ()))
+    for seq in range(seqs):
+        for half in range(2):
+            unit = seq * 2 + half
+            for h in range(heads):
+                for i in range(per_half):
+                    at = token_rows(half * per_half + i, seq, seqs, rows)
+                    to = slice(h * block + i * rows, h * block + (i + 1) * rows)
+                    part = cot_ref[at : at + rows, h * hd : (h + 1) * hd]
+                    cs[to, :] = part
+                    prod = part.astype(f32) * attn_ref[
+                        at : at + rows, h * hd : (h + 1) * hd
+                    ].astype(f32)
+                    dq[to, :] = prod
+            for t in range(heads * block // tile):
+                cols = slice(t * tile, (t + 1) * tile)
+                prod = dq[cols, :]
+                high = prod.astype(bf16)
+                rest = (prod - high.astype(f32)).astype(bf16)
+                dl[:, cols] = lax.dot_general(
+                    ones, high, nt, preferred_element_type=f32
+                ) + lax.dot_general(ones, rest, nt, preferred_element_type=f32)
+            dq[...] = jnp.zeros_like(dq)
+            mine = own_ref[half]
+
+            def step(j, masked):
+                at = pl.ds(j * pair, pair)
+                keys = ks[seq, at, :]
+                values = vs[seq, at, :]
+                key_sum = jnp.zeros((pair, hd), f32)
+                value_sum = jnp.zeros((pair, hd), f32)
+                for t in range(heads * block // tile):
+                    cols = slice(t * tile, (t + 1) * tile)
+                    query = qs_ref[unit, cols, :]
+                    cot = cs[cols, :]
+                    scores = lax.dot_general(keys, query, nt, preferred_element_type=f32)
+                    weights = jnp.exp2(
+                        scores * (scale * LOG2E) - lse_ref[unit, :, cols] * LOG2E
+                    )
+                    if masked:
+                        key_pos = j * pair + lax.broadcasted_iota(jnp.int32, weights.shape, 0)
+                        query_pos = mine * block + (
+                            lax.broadcasted_iota(jnp.int32, weights.shape, 1) % block
+                        )
+                        weights = jnp.where(key_pos <= query_pos, weights, 0.0)
+                    prob_cot = lax.dot_general(values, cot, nt, preferred_element_type=f32)
+                    low = (weights * (prob_cot - dl[0:1, cols])).astype(bf16)
+                    value_sum = value_sum + jnp.dot(
+                        weights.astype(bf16), cot, preferred_element_type=f32
+                    )
+                    key_sum = key_sum + jnp.dot(low, query, preferred_element_type=f32)
+                    dq[cols, :] += lax.dot_general(
+                        low, keys, (((0,), (0,)), ((), ())), preferred_element_type=f32
+                    )
+                dk[seq, at, :] += key_sum
+                dv[seq, at, :] += value_sum
+
+            def body(j, _):
+                step(j, False)
+                return 0
+
+            lax.fori_loop(0, mine // 2, body, 0)
+            step(mine // 2, True)
+            for h in range(heads):
+                for i in range(per_half):
+                    piece = half * per_half + i
+                    at = token_rows(piece, seq, seqs, rows)
+                    grad, terms = head_norm_back(
+                        proj_ref[at : at + rows, h * hd : (h + 1) * hd],
+                        gain_ref[...],
+                        cos_ref[piece * rows : (piece + 1) * rows, :],
+                        sin_ref[piece * rows : (piece + 1) * rows, :],
+                        dq[h * block + i * rows : h * block + (i + 1) * rows, :] * scale,
+                    )
+                    low_ref[at : at + rows, h * hd : (h + 1) * hd] = grad.astype(bf16)
+                    gain_total = gain_total + jnp.sum(terms, axis=0, keepdims=True)
+    gg_ref[...] = gain_total
+
+    def unsort(b, _):
+        loc = loc_ref[b]
+        chunk, half = loc // 2, loc % 2
+        for seq in range(seqs):
+            for i in range(per_half):
+                at = pl.ds(((half * per_half + i) * seqs + seq) * rows, rows)
+                here = pl.ds(b * block + i * rows, rows)
+                dkv_ref[chunk, at, 0:hd] = (dk[seq, here, :] * scale).astype(bf16)
+                dkv_ref[chunk, at, hd : 2 * hd] = dv[seq, here, :].astype(bf16)
+        return 0
+
+    lax.fori_loop(0, blocks, unsort, 0)
+
+
+def attend_back(
+    projected, kv_all, rotated, attention, attention_cot, log_total, query_gain, cos2, sin2, loc,
+    own, heads, pieces, seqs,
+):
+    rows, all_cols = projected.shape
+    hd = query_gain.shape[0]
+    units = 2 * seqs
+    block = rows // units
+    keys = kv_all.shape[0] * kv_all.shape[1] // seqs
+    whole = lambda *shape: pl.BlockSpec(shape, lambda i, *_: (0,) * len(shape))
+    f32, bf16 = jnp.float32, jnp.bfloat16
+    return pl.pallas_call(
+        functools.partial(attend_back_kernel, heads, pieces, seqs, hd**-0.5),
+        grid_spec=pltpu.PrefetchScalarGridSpec(
+            num_scalar_prefetch=2,
+            grid=(1,),
+            in_specs=[
+                pl.BlockSpec((rows, heads * hd), lambda i, *_: (0, 0)),
+                whole(*kv_all.shape),
+                whole(*rotated.shape),
+                whole(rows, heads * hd),
+                whole(rows, heads * hd),
+                whole(*log_total.shape),
+                whole(1, hd),
+                whole(*cos2.shape),
+                whole(*sin2.shape),
+            ],
+            out_specs=[
+                pl.BlockSpec((rows, heads * hd), lambda i, *_: (0, 0)),
+                whole(*kv_all.shape),
+                whole(1, hd),
+            ],
+            scratch_shapes=[
+                pltpu.VMEM((seqs, keys, hd), bf16),
+                pltpu.VMEM((seqs, keys, hd), bf16),
+                pltpu.VMEM((seqs, keys, hd), f32),
+                pltpu.VMEM((seqs, keys, hd), f32),
+                pltpu.VMEM((heads * block, hd), f32),
+                pltpu.VMEM((heads * block, hd), bf16),
+                pltpu.VMEM((8, heads * block), f32),
+            ],
+        ),
+        out_shape=(
+            jax.ShapeDtypeStruct((rows, all_cols), bf16),
+            jax.ShapeDtypeStruct(kv_all.shape, bf16),
+            jax.ShapeDtypeStruct((1, hd), f32),
+        ),
+        compiler_params=pltpu.CompilerParams(vmem_limit_bytes=60 * 1024 * 1024),
+        name="attend_back",
+    )(
+        loc, own, projected, kv_all, rotated, attention, attention_cot, log_total,
+        query_gain.reshape(1, hd), cos2, sin2,
     )
 
-    def step(block_id, carry):
-        row_top, row_total, accum = carry
-        start = block_id * key_block
-        key_piece = lax.dynamic_slice_in_dim(key_all, start, key_block, 0)
-        value_piece = lax.dynamic_slice_in_dim(value_all, start, key_block, 0)
-        piece_pos = lax.dynamic_slice_in_dim(key_pos, start, key_block, 0)
-        scores = score_block(query_rot, key_piece, scaling)
-        allowed = piece_pos[None, :] <= query_pos[:, None]
-        new_top = jnp.maximum(row_top, jnp.max(jnp.where(allowed, scores, MASKED), axis=-1))
-        expo = jnp.where(allowed, jnp.exp(scores - new_top[..., None]), 0.0)
-        decay = jnp.exp(row_top - new_top)
-        row_total = row_total * decay + jnp.sum(expo, axis=-1)
-        accum = accum * decay[..., None] + jnp.einsum(
-            "sagqk,ksad->sagqd",
-            expo.astype(jnp.bfloat16),
-            value_piece,
-            preferred_element_type=jnp.float32,
-        )
-        return (new_top, row_total, accum)
-
-    return lax.fori_loop(0, block_count, step, start_carry)
-
-
-def attend_grads(
-    query_rot, query_pos, key_all, value_all, key_pos, attn_cot, delta, log_total, scaling
-):
-    length = key_all.shape[0]
-    key_block = math.gcd(length, 512)
-    block_count = length // key_block
-    query_rows, seq_count, kv_count, group, head_dim = query_rot.shape
-
-    def step(query_cot, block_id):
-        start = block_id * key_block
-        key_piece = lax.dynamic_slice_in_dim(key_all, start, key_block, 0)
-        value_piece = lax.dynamic_slice_in_dim(value_all, start, key_block, 0)
-        piece_pos = lax.dynamic_slice_in_dim(key_pos, start, key_block, 0)
-        scores = score_block(query_rot, key_piece, scaling)
-        allowed = piece_pos[None, :] <= query_pos[:, None]
-        weights_back = jnp.where(allowed, jnp.exp(scores - log_total[..., None]), 0.0)
-        prob_cot = jnp.einsum(
-            "qsagd,ksad->sagqk", attn_cot, value_piece, preferred_element_type=jnp.float32
-        )
-        score_cot = weights_back * (prob_cot - delta[..., None])
-        value_cot = jnp.einsum(
-            "sagqk,qsagd->ksad",
-            weights_back.astype(jnp.bfloat16),
-            attn_cot,
-            preferred_element_type=jnp.float32,
-        )
-        score_low = score_cot.astype(jnp.bfloat16)
-        query_cot = (
-            query_cot
-            + jnp.einsum(
-                "sagqk,ksad->qsagd", score_low, key_piece, preferred_element_type=jnp.float32
-            )
-            * scaling
-        )
-        key_cot = (
-            jnp.einsum(
-                "sagqk,qsagd->ksad", score_low, query_rot, preferred_element_type=jnp.float32
-            )
-            * scaling
-        )
-        return (query_cot, (key_cot, value_cot))
-
-    start_carry = jnp.zeros((query_rows, seq_count, kv_count, group, head_dim), jnp.float32)
-    query_cot, (key_cot, value_cot) = lax.scan(
-        step, start_carry, jnp.arange(block_count, dtype=jnp.int32)
-    )
-    return (
-        query_cot,
-        key_cot.reshape(length, seq_count, kv_count * head_dim),
-        value_cot.reshape(length, seq_count, kv_count * head_dim),
-    )
-
-
-def gather_ctx(shard, name, ident):
-    if lax.axis_size("ctx") == 8 and lax.axis_size("wsh") == 4:
-        return all_gather(shard, 4, True, False, False, ident, name)
-    return lax.all_gather(shard, "ctx", axis=0)
-
-
-def gather_wsh(shard, name, ident):
-    if lax.axis_size("ctx") == 8 and lax.axis_size("wsh") == 4:
-        return all_gather(shard, 1, False, True, True, ident, name)
-    return lax.all_gather(shard, "wsh", axis=0)
-
-
-def gather_all(shard, name, ident):
-    if lax.axis_size("ctx") == 8 and lax.axis_size("wsh") == 4:
-        return all_gather(shard, 4, True, True, True, ident, name)
-    return lax.all_gather(shard, ("ctx", "wsh"), axis=0)
-
-
-def scatter_ctx(parts, name, ident):
-    if lax.axis_size("ctx") == 8 and lax.axis_size("wsh") == 4:
-        return reduce_scatter(parts, 4, True, False, False, jnp.float32, ident, name)
-    return lax.psum_scatter(parts, "ctx", scatter_dimension=0, tiled=False).astype(jnp.float32)
-
-
-def scatter_wsh(parts, name, ident):
-    if lax.axis_size("ctx") == 8 and lax.axis_size("wsh") == 4:
-        return reduce_scatter(parts, 1, False, True, True, jnp.float32, ident, name)
-    return lax.psum_scatter(parts, "wsh", scatter_dimension=0, tiled=False).astype(jnp.float32)
-
-
-def scatter_all(parts, name, ident):
-    if lax.axis_size("ctx") == 8 and lax.axis_size("wsh") == 4:
-        return reduce_scatter(parts, 4, True, True, True, jnp.float32, ident, name)
-    return lax.psum_scatter(
-        parts, ("ctx", "wsh"), scatter_dimension=0, tiled=False
-    ).astype(jnp.float32)
+
+def own_kernels():
+    return lax.axis_size("ctx") == 8 and lax.axis_size("wsh") == 4
+
+
+AXIS_NAMES = {WSH_AXES: "wsh", CTX_AXES: "ctx", ALL_AXES: ("ctx", "wsh")}
+
+
+def gather(shards, axes_list, ident):
+    if own_kernels():
+        return all_gather(shards, axes_list, ident)
+    return [lax.all_gather(x, AXIS_NAMES[axes], axis=0) for x, axes in zip(shards, axes_list)]
+
+
+def scatter(parts, axes_list, ident):
+    if own_kernels():
+        return reduce_scatter(parts, axes_list, ident)
+    return [
+        lax.psum_scatter(x, AXIS_NAMES[axes], scatter_dimension=0, tiled=False).astype(jnp.float32)
+        for x, axes in zip(parts, axes_list)
+    ]
 
 
 def exchange(pieces):
@@ -748,72 +1086,52 @@
     top_count = expert_ids.shape[-1]
     expert_count = router.shape[1]
     capacity = max(2, 3 * top_count * block_len // (2 * device_count))
-    scaling = head_dim ** (-0.5)
     positions = positions_of(pair_map, seq_len, block_len, pair_map.shape[0])
-    query_pos = lax.dynamic_slice_in_dim(
-        positions, lax.axis_index("ctx") * group_rows, group_rows, 0
+    me_ctx = lax.axis_index("ctx")
+    query_pos = lax.dynamic_slice_in_dim(positions, me_ctx * group_rows, group_rows, 0)
+    cosine, sine_table = rope_tables(query_pos, head_dim)
+    cos2 = jnp.concatenate([cosine, cosine], axis=1)
+    sin2 = jnp.concatenate([-sine_table, sine_table], axis=1)
+    block_ids = jnp.arange(2 * ctx_count, dtype=jnp.int32)
+    blocks_by_loc = jnp.stack([pair_map, 2 * ctx_count - 1 - pair_map], axis=1).reshape(-1)
+    loc = jnp.sum(
+        jnp.where(blocks_by_loc[None, :] == block_ids[:, None], block_ids[None, :], 0), axis=1
+    ).astype(jnp.int32)
+    own_blocks = lax.dynamic_slice_in_dim(blocks_by_loc, 2 * me_ctx, 2, 0)
+
+    inputs_f = inputs.transpose(1, 0, 2).reshape(tokens, width).astype(f32)
+    cot_flat = cotangent.transpose(1, 0, 2).reshape(tokens, width)
+    normed_f, inverse_one = rms_forward(inputs_f, norm_gain)
+    q_cols, kv_cols = query_weight.shape[1], key_weight.shape[1]
+    heads_loc = q_cols // head_dim
+    qkv_shard = jnp.concatenate([query_weight, key_weight, value_weight], axis=1)
+    normed_flat, qkv_full = gather([normed_f.astype(bf16), qkv_shard], [WSH_AXES, CTX_AXES], 1)
+    normed_flat = normed_flat.reshape(group_tokens, width)
+    qkv_full = qkv_full.reshape(width, q_cols + 2 * kv_cols)
+    out_shard, qkv_full = lax.optimization_barrier((out_weight.T, qkv_full))
+    out_full = lax.all_gather(out_shard, "ctx", axis=0, tiled=True)
+    projected = jnp.dot(normed_flat, qkv_full, preferred_element_type=f32)
+    kv_own = kv_prep(projected, key_gain, cos2, sin2, heads_loc, wsh_count, seq_count)
+    (kv_all,) = gather([kv_own], [CTX_AXES], 3)
+    cot_low, kv_all = lax.optimization_barrier((cot_flat.astype(bf16), kv_all))
+    cot_all = lax.all_gather(cot_low, ("ctx", "wsh"), axis=0)
+
+    attention, log_total, rotated = attend(
+        projected, kv_all, query_gain, cos2, sin2, loc, own_blocks, heads_loc, wsh_count, seq_count
     )
-    cosine, sine_table = rope_tables(query_pos, head_dim)
-    cosine = cosine[:, None, None, :]
-    sine_table = sine_table[:, None, None, :]
-
-    inputs_f = inputs.astype(f32)
-    normed_f, inverse_one = rms_forward(inputs_f, norm_gain)
-    normed = normed_f.astype(bf16)
-    normed_flat = gather_wsh(normed.reshape(tokens, width), "ag_normed", 1).reshape(
-        group_tokens, width
-    )
-    q_cols, kv_cols = query_weight.shape[1], key_weight.shape[1]
-    qkv_shard = jnp.concatenate([query_weight, key_weight, value_weight], axis=1)
-    qkv_full = gather_ctx(qkv_shard, "ag_qkv", 2).reshape(width, q_cols + 2 * kv_cols)
-    out_shard = out_weight.T
-    out_full = lax.all_gather(out_shard, "ctx", axis=0, tiled=True)
-    cot_flat = cotangent.reshape(tokens, width)
-    cot_all = lax.all_gather(cot_flat.astype(bf16), ("ctx", "wsh"), axis=0)
-    heads_loc = q_cols // head_dim
-    kv_loc = kv_cols // head_dim
-    group = heads_loc // kv_loc
-    projected = jnp.dot(normed_flat, qkv_full, preferred_element_type=f32)
-    queries = projected[:, :q_cols].reshape(group_rows, seq_count, heads_loc, head_dim)
-    keys_raw = projected[:, q_cols : q_cols + kv_cols].reshape(
-        group_rows, seq_count, kv_loc, head_dim
-    )
-    value_rows = projected[:, q_cols + kv_cols :].astype(bf16)
-    query_normed, query_inverse = rms_forward(queries, query_gain)
-    key_normed, key_inverse = rms_forward(keys_raw, key_gain)
-    query_rot = (
-        rotate(query_normed, cosine, sine_table)
-        .astype(bf16)
-        .reshape(group_rows, seq_count, kv_loc, group, head_dim)
-    )
-    key_rot = rotate(key_normed, cosine, sine_table).astype(bf16)
-    kv_width = seq_count * kv_cols
-    kv_own = jnp.concatenate(
-        [key_rot.reshape(group_rows, kv_width), value_rows.reshape(group_rows, kv_width)], axis=1
-    )
-    kv_all = gather_ctx(kv_own, "ag_kv", 3).reshape(seq_len, 2 * kv_width)
-    key_all = kv_all[:, :kv_width].reshape(seq_len, seq_count, kv_loc, head_dim)
-    value_all = kv_all[:, kv_width:].reshape(seq_len, seq_count, kv_loc, head_dim)
-
-    row_top, row_total, accum = attend_keys(
-        query_rot, query_pos, key_all, value_all, positions, scaling
-    )
-    log_total = row_top + jnp.log(row_total)
-    attention = (accum / row_total[..., None]).astype(bf16)
-    attention_flat = attention.transpose(3, 0, 1, 2, 4).reshape(
-        group_tokens, heads_loc * head_dim
-    )
-    mixed = jnp.einsum("tc,dc->td", attention_flat, out_full, preferred_element_type=f32)
-    residual = inputs_f.reshape(tokens, width) + scatter_wsh(
-        mixed.astype(bf16).reshape(wsh_count, tokens, width), "rs_mixed", 4
-    )
+    mixed = jnp.einsum("tc,dc->td", attention, out_full, preferred_element_type=f32)
+    (mixed,) = scatter([mixed.astype(bf16).reshape(wsh_count, tokens, width)], [WSH_AXES], 4)
+    residual = inputs_f + mixed
+
+    def rows_first(value):
+        return value.reshape(seq_count, rows_dev, width).transpose(1, 0, 2)
 
     moe_normed_f, inverse_two = rms_forward(residual, moe_gain)
     moe_flat = moe_normed_f.astype(bf16)
-    moe_all = gather_all(moe_flat, "ag_moe", 5)
+    (moe_all,) = gather([moe_flat], [ALL_AXES], 5)
     logits = jnp.dot(moe_flat, router, preferred_element_type=f32)
-    route_ids = expert_ids.reshape(tokens, top_count)
-    slots = dispatch_slot.reshape(tokens, top_count)
+    route_ids = expert_ids.transpose(1, 0, 2).reshape(tokens, top_count)
+    slots = dispatch_slot.transpose(1, 0, 2).reshape(tokens, top_count)
     expert_onehot = (
         route_ids[:, :, None] == jnp.arange(expert_count, dtype=jnp.int32)[None, None, :]
     )
@@ -867,9 +1185,11 @@
     up_grad = jnp.einsum("rd,rf->df", rows_in, up_cot, preferred_element_type=f32)
     row_cot = jnp.einsum("rf,df->rd", gate_cot, gate_w, preferred_element_type=f32)
     row_cot = row_cot + jnp.einsum("rf,df->rd", up_cot, up_w, preferred_element_type=f32)
-    row_sum = scatter_all(put(row_cot.astype(bf16)), "rs_rows", 6)
-    moe_sum = scatter_all(out_parts, "rs_outputs", 7)
-    outputs = (residual + moe_sum).reshape(rows_dev, seq_count, width).astype(bf16)
+    (row_sum,) = scatter([put(row_cot.astype(bf16))], [ALL_AXES], 6)
+    out_parts, row_sum = lax.optimization_barrier((out_parts, row_sum))
+    moe_sum = lax.psum_scatter(
+        out_parts, ("ctx", "wsh"), scatter_dimension=0, tiled=False
+    ).astype(f32)
 
     chosen_cot = weight_dense * (
         weight_cot - jnp.sum(weight_dense * weight_cot, axis=-1, keepdims=True)
@@ -895,70 +1215,55 @@
     )
     residual_cot = cot_flat + residual_norm_cot
     residual_low = residual_cot.astype(bf16)
-    residual_flat = gather_wsh(residual_low, "ag_residual", 8).reshape(group_tokens, width)
-
-    out_grad = jnp.einsum(
-        "td,tc->dc", residual_flat, attention_flat, preferred_element_type=f32
-    ).astype(bf16)
-    out_weight_grad = (
-        lax.psum_scatter(out_grad, "ctx", scatter_dimension=0, tiled=True).astype(f32).T
-    )
+    (residual_flat,) = gather([residual_low], [WSH_AXES], 8)
+    residual_flat = residual_flat.reshape(group_tokens, width)
+
     attention_cot = jnp.einsum(
         "td,dc->tc", residual_flat, out_full, preferred_element_type=f32
     ).astype(bf16)
-    attention_cot = attention_cot.reshape(group_rows, seq_count, kv_loc, group, head_dim)
-    attention_q = attention_flat.reshape(group_rows, seq_count, kv_loc, group, head_dim)
-    delta = jnp.sum(attention_cot.astype(f32) * attention_q.astype(f32), axis=-1).transpose(
-        1, 2, 3, 0
+    low, kv_sums, query_gain_grad = attend_back(
+        projected,
+        kv_all,
+        rotated,
+        attention,
+        attention_cot,
+        log_total,
+        query_gain,
+        cos2,
+        sin2,
+        loc,
+        own_blocks,
+        heads_loc,
+        wsh_count,
+        seq_count,
     )
-    query_rot_cot, key_cot_all, value_cot_all = attend_grads(
-        query_rot,
-        query_pos,
-        key_all,
-        value_all,
-        positions,
-        attention_cot,
-        delta,
-        log_total,
-        scaling,
+    out_grad = jnp.einsum("td,tc->dc", residual_flat, attention, preferred_element_type=f32).astype(
+        bf16
     )
-    kv_cot_all = jnp.concatenate(
-        [key_cot_all.reshape(seq_len, kv_width), value_cot_all.reshape(seq_len, kv_width)], axis=1
-    ).astype(bf16)
-    kv_cot = scatter_ctx(kv_cot_all.reshape(ctx_count, group_rows, 2 * kv_width), "rs_kv", 9)
-    key_cot_own = kv_cot[:, :kv_width]
-    value_cot_own = kv_cot[:, kv_width:]
-    query_cot, query_gain_grad = rms_backward(
-        queries,
-        query_inverse,
-        query_gain,
-        unrotate(
-            query_rot_cot.reshape(group_rows, seq_count, heads_loc, head_dim), cosine, sine_table
-        ),
+    out_grad, kv_sums = lax.optimization_barrier((out_grad, kv_sums))
+    out_weight_grad = lax.psum_scatter(out_grad, "ctx", scatter_dimension=0, tiled=True)
+    out_weight_grad = out_weight_grad.astype(f32).T
+    (kv_cot,) = scatter([kv_sums], [CTX_AXES], 9)
+    low, key_gain_grad = kv_back(
+        projected, kv_cot, key_gain, cos2, sin2, low, heads_loc, wsh_count, seq_count
     )
-    key_cot, key_gain_grad = rms_backward(
-        keys_raw,
-        key_inverse,
-        key_gain,
-        unrotate(key_cot_own.reshape(group_rows, seq_count, kv_loc, head_dim), cosine, sine_table),
+    summed = jnp.einsum("tq,cq->tc", low, qkv_full, preferred_element_type=f32)
+    qkv_grad = jnp.einsum("tc,tq->cq", normed_flat, low, preferred_element_type=f32).astype(bf16)
+    normed_cot, qkv_grad = scatter(
+        [
+            summed.astype(bf16).reshape(wsh_count, tokens, width),
+            qkv_grad.reshape(ctx_count, width // ctx_count, q_cols + 2 * kv_cols),
+        ],
+        [WSH_AXES, CTX_AXES],
+        10,
     )
-    query_low = query_cot.astype(bf16).reshape(group_tokens, q_cols)
-    key_low = key_cot.astype(bf16).reshape(group_tokens, kv_cols)
-    value_low = value_cot_own.astype(bf16).reshape(group_tokens, kv_cols)
-    low = jnp.concatenate([query_low, key_low, value_low], axis=1)
-    summed = jnp.einsum("tq,cq->tc", low, qkv_full, preferred_element_type=f32)
-    normed_cot = scatter_wsh(
-        summed.astype(bf16).reshape(wsh_count, tokens, width), "rs_normed", 10
-    )
-    qkv_grad = jnp.einsum("tc,tq->cq", normed_flat, low, preferred_element_type=f32).astype(bf16)
-    qkv_grad = scatter_ctx(
-        qkv_grad.reshape(ctx_count, width // ctx_count, q_cols + 2 * kv_cols), "rs_qkv", 11
-    )
-    inputs_flat = inputs_f.reshape(tokens, width)
-    input_norm_cot, norm_gain_grad = rms_backward(
-        inputs_flat, inverse_one.reshape(tokens, 1), norm_gain, normed_cot
-    )
-    input_grad = (residual_cot + input_norm_cot).reshape(rows_dev, seq_count, width)
+    value_weight_grad = qkv_grad[:, q_cols + kv_cols :]
+    moe_sum, value_weight_grad = lax.optimization_barrier((moe_sum, value_weight_grad))
+    outputs = rows_first((residual + moe_sum).astype(bf16))
+    input_norm_cot, norm_gain_grad = rms_backward(inputs_f, inverse_one, norm_gain, normed_cot)
+    input_grad = rows_first(residual_cot + input_norm_cot)
+    query_gain_grad = query_gain_grad.reshape(head_dim)
+    key_gain_grad = key_gain_grad.reshape(head_dim)
     gains = jnp.concatenate([norm_gain_grad, moe_gain_grad, query_gain_grad, key_gain_grad])
     gains = jnp.sum(to_everyone(gains, device_count), axis=0)
     return (
@@ -967,7 +1272,7 @@
         gains[:width],
         qkv_grad[:, :q_cols],
         qkv_grad[:, q_cols : q_cols + kv_cols],
-        qkv_grad[:, q_cols + kv_cols :],
+        value_weight_grad,
         gains[2 * width : 2 * width + head_dim],
         gains[2 * width + head_dim :],
         out_weight_grad,

time: 1040 us -> 935 us (0.90)
  waiting for transfers between devices: 5.55 us -> 98.5 us
  local copies, waits for them, and re-layouts: 103 us -> 22.1 us
  matrix products: 229 us -> 164 us
  Pallas kernels: 581 us -> 549 us
  other arithmetic: 76 us -> 44 us
  starting transfers between devices: 16.6 us -> 31.7 us
    reduce_scatter x0 -> x1, waiting for transfers between devices: none -> 87.4 us  [local(): lax.psum_scatter(out_parts, ('ctx', 'wsh'), scatter_dimension=0, tiled=Fa...]
    dot_general x30 -> x2, matrix products: 85 us -> 12.7 us  [the longest x1 6.34 us: local(): jnp.einsum('td,tc->dc', residual_flat, attention, preferred_element_type=...]
    pallas_call x11 -> x12, Pallas kernels: 581 us -> 549 us  [the longest x4 251 us: all_gather(): pl.pallas_call(functools.partial(gather_kernel, axes_list), out_shape=[ja...]
    unnamed x203 -> x74, local copies, waits for them, and re-layouts: 30.6 us -> 6.82 us
    all_to_all x4, starting transfers between devices: 16.4 us -> 31.3 us  [exchange(): lax.all_to_all(pieces, ('ctx', 'wsh'), split_axis=0, concat_axis=0, tiled...]
    reshape x9 -> x2, local copies, waits for them, and re-layouts: 16.2 us -> 3.11 us  [rows_first(): return value.reshape(seq_count, rows_dev, width).transpose(1, 0, 2)]
  transfers between devices with their start and end apart: 7 -> 8, of which waited for: 1 -> 2; matrix products, arithmetic and copies ran while one was open for 32% -> 19% of each run, Pallas kernels for 55% -> 46%
where the time goes in v2:
time: 935 us; the launch traced here: 924 us
  Pallas kernels  549 us (59%)
  matrix products  164 us (18%)
  waiting for transfers between devices  98.5 us (11%)
  other arithmetic  44 us (5%)
  starting transfers between devices  31.7 us (3%)
  local copies, waits for them, and re-layouts  22.1 us (2%)
  between operations  14.8 us (2%)
    pallas_call x4, Pallas kernels, all_gather(): pl.pallas_call(functools.partial(gather_kernel, axes_list), out_shape=[ja...  251 us
    pallas_call x4, Pallas kernels, reduce_scatter(): pl.pallas_call(functools.partial(scatter_kernel, axes_list), out_shape=[j...  230 us
    reduce_scatter x1, waiting for transfers between devices, local(): lax.psum_scatter(out_parts, ('ctx', 'wsh'), scatter_dimension=0, tiled=Fa...  87.4 us
    pallas_call x1, Pallas kernels, attend_back(): pl.pallas_call(functools.partial(attend_back_kernel, heads, pieces, seqs,...  35.4 us
    all_to_all x4, starting transfers between devices, exchange(): lax.all_to_all(pieces, ('ctx', 'wsh'), split_axis=0, concat_axis=0, tiled...  31.3 us
    pallas_call x1, Pallas kernels, attend(): pl.pallas_call(functools.partial(attend_kernel, heads, pieces, seqs, hd *...  27.6 us
    dot_general x2, matrix products, put(): jnp.einsum('dct,dcw->dtw', picks_low, rows.reshape(device_count, capacity...  26.1 us
  transfers between devices with their start and end apart: 8, of which 2 were waited for; matrix products, arithmetic and copies ran while one was open for 19% of the time, Pallas kernels for 46%

profile of v2, /device:TPU:0, one launch (start us, length us, event | category | flops | bytes accessed | tf_op | source)
XLA Modules:
  0.0 923.9 jit_solution(16828162965618661717)
XLA Ops:
  9.1 2.6 convert_bitcast_fusion
  11.9 1.8 copy.81
  13.7 2.4 pad_maximum_fusion.refs_1_
  17.0 66.6 %shard_map.272 = (bf16[4,128,2048]{2,1,0:T(8,128)(2,1)}, bf16[8,256,1280]{2,1,0:T(8,128)(2,1)}) custom-call(bf16[128,2048]{1,0:T(8,128)(2,1)} %fusion.17.refs_0_, bf16[256,1280]{1,0:T(8,128)(2,1)} %pad_maximum_fusion.refs_1_), custom_call_target="tpu_custom_call" | custom-call | tf_op jit(solution)/shard_map/pallas_call | solution.py:320
  83.8 2.8 copy.84
  88.9 7.8 fusion.50.proj_ref
  96.7 2.4 kv_prep.1.refs_0_
  99.1 51.0 %shard_map.273.kv_ref = bf16[8,512,256]{2,1,0:T(8,128)(2,1)} custom-call(bf16[512,256]{1,0:T(8,128)(2,1)} %kv_prep.1.refs_0_), custom_call_target="tpu_custom_call" | custom-call | tf_op jit(solution)/shard_map/pallas_call | solution.py:320
  150.1 2.1 bitcast_convert_fusion
  153.8 27.6 %attend.1 = (bf16[512,1024]{1,0:T(8,128)(2,1)}, f32[4,1,1024]{2,1,0:T(1,128)}, bf16[4,1024,128]{2,1,0:T(8,128)(2,1)}) custom-call(s32[16]{0:T(128)} %select_reduce_fusion.5.loc_ref, s32[2]{0:T(128)} %dynamic_slice.6.own_ref, f32[512,1280]{1,0:T(8,128)} %fusion.50.proj_ref, bf16[8,512,256]{2,1,0:T(8,128)(2,1)} %shard_map.273.kv_ref, f32[1,128]{1,0:T(1,128)} %bitcast.192, ...), custom_call_target="tpu_custom_call" | custom-call | tf_op jit(solution)/shard_map/attend/pallas_call | solution.py:827
  181.5 6.3 convolution_convert_fusion.7
  187.8 16.9 %shard_map.274 = f32[128,2048]{1,0:T(8,128)} custom-call(bf16[4,128,2048]{2,1,0:T(8,128)(2,1)} %bitcast.178), custom_call_target="tpu_custom_call" | custom-call | tf_op jit(solution)/shard_map/pallas_call | solution.py:598
  209.5 11.3 %all-to-all-start = ((f32[32,2,128]{2,1,0:T(2,128)}), f32[32,2,128]{2,1,0:T(2,128)S(1)}, u32[]{:S(2)}, u32[]{:S(2)}) async-start(f32[32,2,128]{2,1,0:T(2,128)} %copy.87), calls=%async_computation | async-start | bytes 65536 | tf_op jit(solution)/shard_map/all_to_all | solution.py:1049
  220.8 114.8 %shard_map.275 = bf16[32,128,2048]{2,1,0:T(8,128)(2,1)} custom-call(bf16[128,2048]{1,0:T(8,128)(2,1)} %copy-done.9), custom_call_target="tpu_custom_call" | custom-call | tf_op jit(solution)/shard_map/pallas_call | solution.py:320
  335.7 8.2 convolution_convert_fusion.5
  343.9 5.2 fusion.13
  349.2 2.2 copy-done.32
  351.4 7.7 multiply_convert_fusion.2
  359.2 8.2 convolution_convert_fusion.4
  367.4 7.1 fusion.1
  375.6 6.6 fusion.2
  382.2 3.1 all-to-all-start.1
  385.4 11.1 %multiply_convert_fusion = (bf16[1536,768]{1,0:T(8,128)(2,1)S(1)}, bf16[1536,768]{1,0:T(8,128)(2,1)S(1)}) fusion(f32[1536,768]{1,0:T(8,128)} %copy-done.32, f32[1536,768]{1,0:T(8,128)} %get-tuple-element.172, bf16[1536,2048]{1,0:T(8,128)(2,1)} %bitcast.168, bf16[1,768,2048]{2,1,0:T(8,128)(2,1)S(1)} %copy-done), kind=kOutput, calls=%fused_computation.13 | convolution fusion | flops 4847173632 | bytes 23592960 | tf_op jit(solution)/shard_map/rd,fd->rf/dot_general | solution.py:1181
  396.6 5.1 fusion.11
  401.7 7.5 add_convert_fusion
  409.2 13.1 %convolution_convert_fusion.refs_0_ = bf16[32,128,2048]{2,1,0:T(8,128)(2,1)} fusion(bf16[32,48,2048]{2,1,0:T(8,128)(2,1)} %bitcast.171, s32[32,128]{1,0:T(8,128)S(1)} %bitcast.182), kind=kOutput, calls=%fused_computation.2 | convolution fusion | flops 813891584 | bytes 23085056 | tf_op jit(solution)/shard_map/dct,dcw->dtw/dot_general | solution.py:1158
  422.3 10.9 %fusion.3 = (bf16[1536,2048]{1,0:T(8,128)(2,1)}, bf16[1536,2048]{1,0:T(8,128)(2,1)}) fusion(bf16[32,48,2048]{2,1,0:T(8,128)(2,1)} %copy-done.2, f32[1536]{0:T(1024)S(1)} %mul.217, bf16[1536,2048]{1,0:T(8,128)(2,1)} %get-tuple-element.174), kind=kLoop, calls=%fused_computation.9 | loop fusion | flops 18874368 | bytes 25171968 | tf_op jit(solution)/shard_map/convert_element_type | solution.py:1169
  433.2 13.1 %convolution_convert_fusion.1 = bf16[32,128,2048]{2,1,0:T(8,128)(2,1)} fusion(bf16[32,48,2048]{2,1,0:T(8,128)(2,1)} %bitcast.163, s32[32,128]{1,0:T(8,128)S(1)} %bitcast.183), kind=kOutput, calls=%fused_computation.3 | convolution fusion | flops 813891584 | bytes 23085056 | tf_op jit(solution)/shard_map/dct,dcw->dtw/dot_general | solution.py:1158
  446.3 84.4 %shard_map.276 = f32[128,2048]{1,0:T(8,128)} custom-call(bf16[32,128,2048]{2,1,0:T(8,128)(2,1)} %convolution_convert_fusion.refs_0_), custom_call_target="tpu_custom_call" | custom-call | tf_op jit(solution)/shard_map/pallas_call | solution.py:598
  533.7 18.8 %shard_map.277 = bf16[4,128,2048]{2,1,0:T(8,128)(2,1)} custom-call(bf16[128,2048]{1,0:T(8,128)(2,1)} %get-tuple-element.148.refs_0_), custom_call_target="tpu_custom_call" | custom-call | tf_op jit(solution)/shard_map/pallas_call | solution.py:320
  552.5 6.3 convolution_convert_fusion.6
  558.9 5.5 convolution_convert_fusion.9.cot_ref
  564.4 35.4 %attend_back.1 = (bf16[512,1280]{1,0:T(8,128)(2,1)}, bf16[8,512,256]{2,1,0:T(8,128)(2,1)}, f32[1,128]{1,0:T(1,128)}) custom-call(s32[16]{0:T(128)} %select_reduce_fusion.5.loc_ref, s32[2]{0:T(128)} %dynamic_slice.6.own_ref, f32[512,1280]{1,0:T(8,128)} %fusion.50.proj_ref, bf16[8,512,256]{2,1,0:T(8,128)(2,1)} %shard_map.273.kv_ref, ...), custom_call_target="tpu_custom_call" | custom-call | tf_op jit(solution)/shard_map/attend_back/pallas_call | solution.py:982
  600.5 9.8 %convolution_bitcast_fusion.1 = f32[1,2048,768]{2,1,0:T(8,128)} fusion(bf16[1536,2048]{1,0:T(8,128)(2,1)} %bitcast.166, bf16[1536,768]{1,0:T(8,128)(2,1)} %copy-done.33), kind=kOutput, calls=%fused_computation.21 | convolution fusion | flops 4831838208 | bytes 14942208 | tf_op jit(solution)/shard_map/rd,rf->df/dot_general | solution.py:1185
  610.3 10.0 %convolution_bitcast_fusion.2 = f32[1,2048,768]{2,1,0:T(8,128)} fusion(bf16[1536,2048]{1,0:T(8,128)(2,1)} %bitcast.167, bf16[1536,768]{1,0:T(8,128)(2,1)S(1)} %copy-done.31), kind=kOutput, calls=%fused_computation.22 | convolution fusion | flops 4831838208 | bytes 14942208 | tf_op jit(solution)/shard_map/rd,rf->df/dot_general | solution.py:1184
  620.4 7.0 convolution_bitcast_fusion
  628.1 2.9 all-to-all-start.3
  631.0 43.0 %shard_map.278.cot_ref = f32[512,256]{1,0:T(8,128)} custom-call(bf16[8,512,256]{2,1,0:T(8,128)(2,1)} %get-tuple-element.48.refs_0_), custom_call_target="tpu_custom_call" | custom-call | tf_op jit(solution)/shard_map/pallas_call | solution.py:598
  674.0 2.7 kv_back.1
  676.7 7.3 convolution_convert_fusion.2
  684.1 6.6 convolution_convert_fusion.8
  690.6 85.6 %shard_map.279 = (f32[128,2048]{1,0:T(8,128)}, f32[256,1280]{1,0:T(8,128)}) custom-call(bf16[4,128,2048]{2,1,0:T(8,128)(2,1)} %bitcast.174, bf16[8,256,1280]{2,1,0:T(8,128)(2,1)} %bitcast.172), custom_call_target="tpu_custom_call" | custom-call | tf_op jit(solution)/shard_map/pallas_call | solution.py:598
  783.7 14.1 %all-to-all-start.2 = ((f32[32,1,4352]{2,1,0:T(1,128)}), f32[32,1,4352]{2,1,0:T(1,128)}, u32[]{:S(2)}, u32[]{:S(2)}) async-start(f32[32,1,4352]{2,1,0:T(1,128)} %broadcast_in_dim.128), calls=%async_computation.3 | async-start | bytes 1114112 | tf_op jit(solution)/shard_map/all_to_all | solution.py:1049
  799.5 8.4 convolution_bitcast_fusion.3
  807.8 10.7 %all-to-all-done.2 = f32[32,1,4352]{2,1,0:T(1,128)} async-done(((f32[32,1,4352]{2,1,0:T(1,128)}), f32[32,1,4352]{2,1,0:T(1,128)}, u32[]{:S(2)}, u32[]{:S(2)}) %all-to-all-start.2) | async-done | bytes 557088 | tf_op jit(solution)/shard_map/all_to_all | solution.py:1049
  821.1 2.2 convert_bitcast_fusion.1
  823.3 2.5 copy.91
  825.8 87.4 %reduce-scatter.3.cloned.1.call-done = bf16[1,128,2048]{2,1,0:T(8,128)(2,1)} async-done(((bf16[32,128,2048]{2,1,0:T(8,128)(2,1)}), bf16[1,128,2048]{2,1,0:T(8,128)(2,1)}) %reduce-scatter.3.cloned.1.call-update) | async-done | bytes 524304 | tf_op jit(solution)/shard_map/reduce_scatter | solution.py:1190
  (147 shorter events, 32.7 us)
Async XLA Ops:
  7.2 360.2 %copy-start = (bf16[1,768,2048]{2,1,0:T(8,128)(2,1)S(1)}, bf16[1,768,2048]{2,1,0:T(8,128)(2,1)}, u32[]{:S(2)}) copy-start(bf16[1,768,2048]{2,1,0:T(8,128)(2,1)} %param.30) | copy-start | bytes 9437188
  7.2 8.9 copy-start.15
  7.2 174.2 %all-gather.4.cloned.1.call-start = ((), (), s32[]{:S(2)}) async-start(), calls=%async_computation.6 | async-start | bytes 4718592 | tf_op jit(solution)/shard_map/all_gather | solution.py:1112
  11.7 74.9 %copy-start.21 = (s32[8]{0:T(128)S(1)}, s32[8]{0:T(128)}, u32[]{:S(2)}) copy-start(s32[8]{0:T(128)} %param.18) | copy-start | bytes 100
  11.9 76.3 %copy-start.19 = (f32[128]{0:T(128)}, f32[128]{0:T(128)S(1)}, u32[]{:S(2)}) copy-start(f32[128]{0:T(128)S(1)} %rsqrt.26) | copy-start | bytes 1540
  13.7 2.4 copy-start.3
  83.7 275.5 %all-gather.6.cloned.1.call-start = ((), (), s32[]{:S(2)}) async-start(), calls=%async_computation.9 | async-start | bytes 17301504 | tf_op jit(solution)/shard_map/all_gather | solution.py:1117
  96.7 55.7 %copy-start.17 = (s32[64,2,8]{0,2,1:T(8,128)S(1)}, s32[64,2,8]{0,2,1:T(8,128)}, u32[]{:S(2)}) copy-start(s32[64,2,8]{0,2,1:T(8,128)} %param.31) | copy-start | bytes 12292
  96.7 55.8 %copy-start.18 = (s32[64,2,8]{0,2,1:T(8,128)S(1)}, s32[64,2,8]{0,2,1:T(8,128)}, u32[]{:S(2)}) copy-start(s32[64,2,8]{0,2,1:T(8,128)} %param.32) | copy-start | bytes 12292
  187.8 19.7 %copy-start.14 = (f32[2048]{0:T(1024)S(1)}, f32[2048]{0:T(1024)}, u32[]{:S(2)}) copy-start(f32[2048]{0:T(1024)} %param.26) | copy-start | bytes 24580
  187.8 20.7 %copy-start.13 = (bf16[2048,32]{0,1:T(8,128)(2,1)S(1)}, bf16[2048,32]{0,1:T(8,128)(2,1)}, u32[]{:S(2)}) copy-start(bf16[2048,32]{0,1:T(8,128)(2,1)} %param.27) | copy-start | bytes 393220
  206.6 1.0 copy-start.5
  207.7 0.8 copy-start.9
  209.5 126.1 %all-to-all-start = ((f32[32,2,128]{2,1,0:T(2,128)}), f32[32,2,128]{2,1,0:T(2,128)S(1)}, u32[]{:S(2)}, u32[]{:S(2)}) async-start(f32[32,2,128]{2,1,0:T(2,128)} %copy.87), calls=%async_computation | async-start | bytes 65536 | tf_op jit(solution)/shard_map/all_to_all | solution.py:1049
  335.6 8.3 copy-start.24
  343.9 5.3 copy-start.7
  343.9 7.5 copy-start.26
  349.2 2.3 copy-start.32
  359.2 8.3 copy-start.28
  367.4 7.1 copy-start.2
  382.2 148.5 %all-to-all-start.1 = ((f32[32,1,128]{2,1,0:T(1,128)}), f32[32,1,128]{2,1,0:T(1,128)S(1)}, u32[]{:S(2)}, u32[]{:S(2)}) async-start(f32[32,1,128]{2,1,0:T(1,128)} %bitcast.32), calls=%async_computation.2 | async-start | bytes 32768 | tf_op jit(solution)/shard_map/all_to_all | solution.py:1049
  385.3 435.8 %reduce-scatter.5.cloned.1.call-start = ((), (), s32[]{:S(2)}) async-start(), calls=%async_computation.8 | async-start | bytes 4718592 | tf_op jit(solution)/shard_map/reduce_scatter | solution.py:1244
  385.4 11.2 %copy-start.25 = (bf16[1,2048,768]{2,1,0:T(8,128)(2,1)S(1)}, bf16[1,2048,768]{2,1,0:T(8,128)(2,1)}, u32[]{:S(2)}) copy-start(bf16[1,2048,768]{2,1,0:T(8,128)(2,1)} %param.28) | copy-start | bytes 9437188
  396.5 5.2 copy-start.30
  396.5 5.2 copy-start.33
  396.5 5.1 copy-start.27
  446.3 84.5 %copy-start.6 = (f32[128,2048]{1,0:T(8,128)S(1)}, f32[128,2048]{1,0:T(8,128)}, u32[]{:S(2)}) copy-start(f32[128,2048]{1,0:T(8,128)} %copy-done.5) | copy-start | bytes 3145732
  446.3 86.2 %copy-start.8 = (f32[2,64,2048]{2,1,0:T(8,128)S(1)}, f32[2,64,2048]{2,1,0:T(8,128)}, u32[]{:S(2)}) copy-start(f32[2,64,2048]{2,1,0:T(8,128)} %copy.84) | copy-start | bytes 3145732
  552.5 6.4 copy-start.10
  599.9 0.7 copy-start.20
  599.9 313.3 %reduce-scatter.3.cloned.1.call-start = ((), (), s32[]{:S(2)}) async-start(), calls=%async_computation.7 | async-start | bytes 17301504 | tf_op jit(solution)/shard_map/reduce_scatter | solution.py:1190
  600.5 9.8 %copy-start.31 = (bf16[1536,768]{1,0:T(8,128)(2,1)S(1)}, bf16[1536,768]{1,0:T(8,128)(2,1)}, u32[]{:S(2)}) copy-start(bf16[1536,768]{1,0:T(8,128)(2,1)} %copy-done.30) | copy-start | bytes 7077892
  600.5 19.9 %slice-start = ((s8[6291456]{0:T(1024)(128)(4,1)}), s8[4194304]{0:T(1024)(128)(4,1)S(1)}, s32[]{:S(2)}) async-start(s8[6291456]{0:T(1024)(128)(4,1)} %bitcast.169), calls=%async_computation.10 | async-start | bytes 8388608
  610.3 10.1 %slice-start.1 = ((s8[6291456]{0:T(1024)(128)(4,1)}), s8[2097152]{0:T(1024)(128)(4,1)S(1)}, s32[]{:S(2)}) async-start(s8[6291456]{0:T(1024)(128)(4,1)} %bitcast.169), calls=%async_computation.11 | async-start | bytes 4194304
  610.3 10.1 %copy-start.29 = (bf16[1536,768]{1,0:T(8,128)(2,1)S(1)}, bf16[1536,768]{1,0:T(8,128)(2,1)}, u32[]{:S(2)}) copy-start(bf16[1536,768]{1,0:T(8,128)(2,1)} %get-tuple-element.171) | copy-start | bytes 7077892
  628.1 154.4 %all-to-all-start.3 = ((bf16[32,128,32]{1,2,0:T(8,128)(2,1)}), bf16[32,128,32]{1,2,0:T(8,128)(2,1)S(1)}, u32[]{:S(2)}, u32[]{:S(2)}) async-start(bf16[32,128,32]{1,2,0:T(8,128)(2,1)} %broadcast_in_dim.129), calls=%async_computation.5 | async-start | bytes 524288 | tf_op jit(solution)/shard_map/all_to_all | solution.py:1049
  676.7 7.3 copy-start.11
  690.6 85.6 %copy-start.4 = (f32[2,64,2048]{2,1,0:T(8,128)S(1)}, f32[2,64,2048]{2,1,0:T(8,128)}, u32[]{:S(2)}) copy-start(f32[2,64,2048]{2,1,0:T(8,128)} %copy-done.3) | copy-start | bytes 3145732
  690.6 85.6 %copy-start.16 = (f32[2048]{0:T(1024)S(1)}, f32[2048]{0:T(1024)}, u32[]{:S(2)}) copy-start(f32[2048]{0:T(1024)} %param.19) | copy-start | bytes 24580
  776.2 5.3 copy-start.12
  777.8 4.7 copy-start.22
  777.8 4.7 copy-start.23
  783.7 34.9 %all-to-all-start.2 = ((f32[32,1,4352]{2,1,0:T(1,128)}), f32[32,1,4352]{2,1,0:T(1,128)}, u32[]{:S(2)}, u32[]{:S(2)}) async-start(f32[32,1,4352]{2,1,0:T(1,128)} %broadcast_in_dim.128), calls=%async_computation.3 | async-start | bytes 1114112 | tf_op jit(solution)/shard_map/all_to_all | solution.py:1049
  799.5 117.5 %copy-start.1 = (bf16[1,768,2048]{2,1,0:T(8,128)(2,1)S(1)}, bf16[1,768,2048]{2,1,0:T(8,128)(2,1)}, u32[]{:S(2)}) copy-start(bf16[1,768,2048]{2,1,0:T(8,128)(2,1)} %param.30) | copy-start | bytes 9437188
Sparse Core Ops, SparseCore 0:
  83.8 86.5 all-gather.3
  173.9 154.1 all-gather.5
  600.0 101.9 reduce-scatter.4
  704.1 209.0 reduce-scatter.2

commit v3 on v2

--- a/solution.py
+++ b/solution.py
@@ -100,6 +100,12 @@
         return steps
 
 
+def both(a, b):
+    if a is None or b is None:
+        return a if b is None else b
+    return a.astype(jnp.int32) * b.astype(jnp.int32) > 0
+
+
 def when(cond, fn):
     if cond is None:
         fn()
@@ -107,18 +113,18 @@
         pl.when(cond)(fn)
 
 
-def gather_job(axes, x_ref, o_ref, ssem, rsem, lsem):
+def gather_line_first(axes, lo, rows, x_ref, o_ref, ssem, rsem):
     nz, ux, uy, uc = axes
     pc = Place(nz, ux, uy, uc)
     z, x, y, c = pc.z, pc.x, pc.y, pc.c
-    rows = x_ref.shape[0]
     half = rows // 2
+    x_ref = x_ref.at[pl.ds(lo, rows)]
     to_x, to_y, to_c = pc.dev(z, 1 - x, y, c), pc.dev(z, x, 1 - y, c), pc.dev(z, x, y, 1 - c)
 
     def part(b, p):
         if p == 0:
-            return o_ref.at[b]
-        return o_ref.at[b, pl.ds((p - 1) * half, half)]
+            return o_ref.at[b, pl.ds(lo, rows)]
+        return o_ref.at[b, pl.ds(lo + (p - 1) * half, half)]
 
     def sid(d, side, kind):
         return (d * 2 + side) * 10 + kind
@@ -132,8 +138,6 @@
             device_id=device,
             device_id_type=MESH_ID,
         )
-
-    own = pltpu.make_async_copy(x_ref, o_ref.at[pc.blk(z, x, y, c)], lsem)
 
     def hops(d, side, s):
         out = []
@@ -268,14 +272,120 @@
                             cp.wait_send()
 
             when(ok, fn)
-        own.wait()
-
-    return own.start, [functools.partial(phase, t) for t in range(nz + 2)], last
+
+    return lambda: None, [functools.partial(phase, t) for t in range(nz + 2)], last
+
+
+def gather_plane_first(axes, lo, rows, x_ref, o_ref, ssem, rsem):
+    nz, ux, uy, uc = axes
+    pc = Place(nz, ux, uy, uc)
+    z, x, y, c = pc.z, pc.x, pc.y, pc.c
+    half = rows // 2
+    own = x_ref.at[pl.ds(lo, rows)]
+    to_x, to_y, to_c = pc.dev(z, 1 - x, y, c), pc.dev(z, x, 1 - y, c), pc.dev(z, x, y, 1 - c)
+    items = [(0, 0, x, y, (lo, rows))]
+    if ux:
+        items.append((1, 1, 1 - x, y, (lo, rows)))
+    if uy:
+        items.append((2, 1, x, 1 - y, (lo, rows)))
+    if ux and uy:
+        items.append((3, 2, 1 - x, 1 - y, (lo, half)))
+        items.append((4, 2, 1 - x, 1 - y, (lo + half, half)))
+    per = 5
+    base = nz * 2 * per
+
+    def iid(d, side, item):
+        return (d * 2 + side) * per + item
+
+    def copy(s, px, py, core, span, sidx, ridx, device, src=None):
+        ref = o_ref.at[pc.blk(s, px, py, core), pl.ds(span[0], span[1])]
+        return pltpu.make_async_remote_copy(
+            src_ref=ref if src is None else src,
+            dst_ref=ref,
+            send_sem=ssem.at[sidx],
+            recv_sem=rsem.at[ridx],
+            device_id=device,
+            device_id_type=MESH_ID,
+        )
+
+    def arrival(d, side, s, it):
+        item, _, px, py, span = it
+        return copy(s, px, py, c, span, 0, iid(d, side, item), to_x)
+
+    def outgoing(d, side, s, it):
+        item, _, px, py, span = it
+        src = own if d == 0 and item == 0 else None
+        out = []
+        if d + 1 < nz:
+            if d == 0 or side == 0:
+                out.append(
+                    (
+                        z + 1 < nz,
+                        copy(s, px, py, c, span, iid(d, 0, item), iid(d + 1, 0, item), pc.dev(z + 1, x, y, c), src),
+                    )
+                )
+            if d == 0 or side == 1:
+                out.append(
+                    (
+                        z >= 1,
+                        copy(s, px, py, c, span, iid(d, 1, item), iid(d + 1, 1, item), pc.dev(z - 1, x, y, c), src),
+                    )
+                )
+        if uc:
+            at = base + iid(d, side, item)
+            out.append((None, copy(s, px, py, c, span, at, at, to_c, src)))
+        if d == 0:
+            if item == 0 and ux:
+                out.append((None, copy(s, px, py, c, span, 2 * base, iid(0, 0, 1), to_x, src)))
+            if item == 0 and uy:
+                out.append((None, copy(s, px, py, c, span, 2 * base + 1, iid(0, 0, 2), to_y, src)))
+            if item == 1 and uy:
+                out.append(
+                    (None, copy(s, px, py, c, (lo, half), 2 * base + 2, iid(0, 0, 3), to_y))
+                )
+            if item == 2 and ux:
+                out.append(
+                    (None, copy(s, px, py, c, (lo + half, half), 2 * base + 3, iid(0, 0, 4), to_x))
+                )
+        return out
+
+    steps = pc.line_steps()
+
+    def phase(t):
+        for d, side, s, ok in steps:
+            for it in items:
+                if d + it[1] != t:
+                    continue
+
+                if d > 0 or it[0] > 0:
+                    when(ok, arrival(d, side, s, it).wait_recv)
+                for cond, cp in outgoing(d, side, s, it):
+                    when(both(ok, cond), cp.start)
+
+    def last():
+        for d, side, s, ok in steps:
+
+            for it in items:
+                if uc:
+                    item, _, px, py, span = it
+                    there = copy(s, px, py, 1 - c, span, 0, base + iid(d, side, item), to_c)
+                    when(ok, there.wait_recv)
+                for cond, cp in outgoing(d, side, s, it):
+                    when(both(ok, cond), cp.wait_send)
+
+    return lambda: None, [functools.partial(phase, t) for t in range(nz + 2)], last
 
 
 WSH_AXES = (1, False, True, True)
 CTX_AXES = (4, True, False, False)
 ALL_AXES = (4, True, True, True)
+
+
+def spans_of(axes, rows):
+    if axes[0] == 1 or rows % 128:
+        return rows, 0
+    second = rows // 4 if axes[3] else rows // 8
+    return rows - second, second
 
 
 def run_jobs(axes_list, jobs):
@@ -299,42 +409,103 @@
     return (axes[0] * 2 if axes[1] else 1) * (4 if axes[3] else 1)
 
 
-def gather_kernel(axes_list, *refs):
-    n = len(axes_list)
-    jobs = [
-        gather_job(axes_list[i], refs[i], refs[n + i], *refs[2 * n + 3 * i : 2 * n + 3 * i + 3])
-        for i in range(n)
-    ]
+GATHER_REFS, SCATTER_REFS = 5, 20
+
+
+def gather_scratch(axes):
+    dma = pltpu.SemaphoreType.DMA
+    nz = axes[0]
+    return [dma((nz * 20,)), dma((nz * 20,)), dma((nz * 20 + 4,)), dma((nz * 20,)), dma]
+
+
+def gather_jobs(axes, x_ref, o_ref, s1, r1, s2, r2, lsem):
+    pc = Place(*axes)
+    rows = x_ref.shape[0]
+    main, rest = spans_of(axes, rows)
+    own = pltpu.make_async_copy(x_ref, o_ref.at[pc.blk(pc.z, pc.x, pc.y, pc.c)], lsem)
+    _, phases, last = gather_line_first(axes, 0, main, x_ref, o_ref, s1, r1)
+
+    def end():
+        last()
+        own.wait()
+
+    jobs = [(own.start, phases, end)]
+    if rest:
+        jobs.append(gather_plane_first(axes, main, rest, x_ref, o_ref, s2, r2))
+    return jobs
+
+
+def scatter_scratch(axes, shape, dt):
+    rows, cols = shape
+    nz, ux, uy, uc = axes
+    dma = pltpu.SemaphoreType.DMA
+    out = []
+    for second, n in enumerate(spans_of(axes, rows)):
+        few = lambda use, k, r: pltpu.VMEM((k, r, cols) if use and n else (1, 16, cols), dt)
+        lines = 1 if second else nz
+        out += [
+            few(True, nz * 4, n),
+            few(uc, nz * 4, n),
+            few(ux, lines, n),
+            few(uy, lines, n),
+            few(ux and uy, lines, n // 2),
+            few(ux and uy, lines, n // 2),
+            few(nz > 1, (nz + 1) * (4 if second else 1), n),
+            dma((nz * (14 if second else 12),)),
+            dma((nz * (18 if second else 12),)),
+            dma((nz * 4,)),
+        ]
+    return out
+
+
+def scatter_jobs(axes, p_ref, o_ref, *refs):
+    rows = o_ref.shape[0]
+    main, rest = spans_of(axes, rows)
+    jobs = [scatter_line_last(axes, 0, main, p_ref, o_ref, *refs[:10])]
+    if rest:
+        jobs.append(scatter_line_first(axes, main, rest, p_ref, o_ref, *refs[10:]))
+    return jobs
+
+
+def transfer_kernel(kinds, axes_list, *refs):
+    n = len(kinds)
+    at = 2 * n
+    jobs = []
+    for i, (kind, axes) in enumerate(zip(kinds, axes_list)):
+        many = GATHER_REFS if kind == "gather" else SCATTER_REFS
+        make = gather_jobs if kind == "gather" else scatter_jobs
+        jobs += make(axes, refs[i], refs[n + i], *refs[at : at + many])
+        at += many
     run_jobs(axes_list, jobs)
 
 
-def gather_sems(axes):
-    return [
-        pltpu.SemaphoreType.DMA((axes[0] * 20,)),
-        pltpu.SemaphoreType.DMA((axes[0] * 20,)),
-        pltpu.SemaphoreType.DMA,
-    ]
-
-
-def all_gather(shards, axes_list, collective_id):
+def transfer(kinds, values, axes_list, collective_id):
+    shapes, specs, scratch = [], [], []
+    for kind, value, axes in zip(kinds, values, axes_list):
+        if kind == "gather":
+            shapes.append(jax.ShapeDtypeStruct((group_of(axes),) + value.shape, value.dtype))
+            specs.append(pl.BlockSpec(memory_space=pl.ANY))
+            scratch += gather_scratch(axes)
+        else:
+            shapes.append(jax.ShapeDtypeStruct(value.shape[1:], jnp.float32))
+            specs.append(pl.BlockSpec(memory_space=pltpu.VMEM))
+            scratch += scatter_scratch(axes, value.shape[1:], value.dtype)
     return pl.pallas_call(
-        functools.partial(gather_kernel, axes_list),
-        out_shape=[
-            jax.ShapeDtypeStruct((group_of(axes),) + shard.shape, shard.dtype)
-            for shard, axes in zip(shards, axes_list)
-        ],
-        in_specs=[pl.BlockSpec(memory_space=pl.ANY)] * len(shards),
-        out_specs=[pl.BlockSpec(memory_space=pl.ANY)] * len(shards),
-        scratch_shapes=[x for axes in axes_list for x in gather_sems(axes)],
-        compiler_params=pltpu.CompilerParams(collective_id=collective_id, has_side_effects=True),
-    )(*shards)
-
-
-def scatter_job(axes, p_ref, o_ref, acc, rc, rx, ry, ra, rb, rz, ssem, rsem, lsem):
+        functools.partial(transfer_kernel, kinds, axes_list),
+        out_shape=shapes,
+        in_specs=[pl.BlockSpec(memory_space=pl.ANY)] * len(values),
+        out_specs=specs,
+        scratch_shapes=scratch,
+        compiler_params=pltpu.CompilerParams(
+            collective_id=collective_id, has_side_effects=True, vmem_limit_bytes=61 * 1024 * 1024
+        ),
+    )(*values)
+
+
+def scatter_line_last(axes, lo, rows, p_ref, o_ref, acc, rc, rx, ry, ra, rb, rz, ssem, rsem, lsem):
     nz, ux, uy, uc = axes
     pc = Place(nz, ux, uy, uc)
     z, x, y, c = pc.z, pc.x, pc.y, pc.c
-    rows, _ = o_ref.shape
     half = rows // 2
     chunk = math.gcd(half, 32)
     f32 = jnp.float32
@@ -369,12 +540,12 @@
 
     def load(s, rel, px, py):
         return pltpu.make_async_copy(
-            p_ref.at[pc.blk(s, px, py, c)], acc.at[slot(s) * 4 + rel], lsem.at[slot(s) * 4 + rel]
+            p_ref.at[pc.blk(s, px, py, c), pl.ds(lo, rows)], acc.at[slot(s) * 4 + rel], lsem.at[slot(s) * 4 + rel]
         )
 
     def give(s, rel, px, py):
         return rcopy(
-            p_ref.at[pc.blk(s, px, py, 1 - c)], rc.at[slot(s) * 4 + rel], s, rel, to_c
+            p_ref.at[pc.blk(s, px, py, 1 - c), pl.ds(lo, rows)], rc.at[slot(s) * 4 + rel], s, rel, to_c
         )
 
     def fold(dst, lo, n, srcs):
@@ -516,7 +687,9 @@
                         total = acc[slot(s) * 4, pl.ds(r, chunk), :].astype(f32)
                         for ref, at in terms:
                             total = total + ref[pl.ds(at + r, chunk), :].astype(f32)
-                        o_ref[pl.ds(r, chunk), :] = total.astype(o_ref.dtype)
+                        o_ref[pl.ds(pl.multiple_of(lo + i * chunk, chunk), chunk), :] = total.astype(
+                            o_ref.dtype
+                        )
                         return 0
 
                     lax.fori_loop(0, rows // chunk, step_, 0)
@@ -524,10 +697,9 @@
                 if nz == 1:
                     body(False, False)
                 else:
-                    lo, hi = z >= 1, z + 1 < nz
-                    pl.when(jnp.logical_and(lo, hi))(lambda: body(True, True))
-                    pl.when(jnp.logical_and(lo, jnp.logical_not(hi)))(lambda: body(True, False))
-                    pl.when(jnp.logical_and(jnp.logical_not(lo), hi))(lambda: body(False, True))
+                    pl.when(jnp.logical_and(z >= 1, z + 1 < nz))(lambda: body(True, True))
+                    pl.when(z == nz - 1)(lambda: body(True, False))
+                    pl.when(z == 0)(lambda: body(False, True))
 
         when(ok, fn)
 
@@ -568,47 +740,212 @@
     return begin, [functools.partial(phase, t) for t in range(nz + 2)], last
 
 
-def scatter_kernel(axes_list, *refs):
-    n = len(axes_list)
-    jobs = [
-        scatter_job(axes_list[i], refs[i], refs[n + i], *refs[2 * n + 10 * i : 2 * n + 10 * i + 10])
-        for i in range(n)
-    ]
-    run_jobs(axes_list, jobs)
-
-
-def scatter_scratch(axes, rows, cols, dt):
+def scatter_line_first(axes, lo, rows, p_ref, o_ref, acc, rc, rx, ry, ra, rb, rz, ssem, rsem, lsem):
     nz, ux, uy, uc = axes
-    few = lambda use, n, r: pltpu.VMEM((n, r, cols) if use else (1, 16, cols), dt)
-    return [
-        few(True, nz * 4, rows),
-        few(uc, nz * 4, rows),
-        few(ux, nz, rows),
-        few(uy, nz, rows),
-        few(ux and uy, nz, rows // 2),
-        few(ux and uy, nz, rows // 2),
-        few(nz > 1, nz + 1, rows),
-        pltpu.SemaphoreType.DMA((nz * 12,)),
-        pltpu.SemaphoreType.DMA((nz * 12,)),
-        pltpu.SemaphoreType.DMA((nz * 4,)),
-    ]
-
-
-def reduce_scatter(parts, axes_list, collective_id):
-    return pl.pallas_call(
-        functools.partial(scatter_kernel, axes_list),
-        out_shape=[jax.ShapeDtypeStruct(p.shape[1:], jnp.float32) for p in parts],
-        in_specs=[pl.BlockSpec(memory_space=pl.ANY)] * len(parts),
-        out_specs=[pl.BlockSpec(memory_space=pltpu.VMEM)] * len(parts),
-        scratch_shapes=[
-            x
-            for axes, p in zip(axes_list, parts)
-            for x in scatter_scratch(axes, p.shape[1], p.shape[2], p.dtype)
-        ],
-        compiler_params=pltpu.CompilerParams(
-            collective_id=collective_id, has_side_effects=True, vmem_limit_bytes=60 * 1024 * 1024
-        ),
-    )(*parts)
+    pc = Place(nz, ux, uy, uc)
+    z, x, y, c = pc.z, pc.x, pc.y, pc.c
+    half = rows // 2
+    chunk = math.gcd(half, 32)
+    f32 = jnp.float32
+    to_x, to_y, to_c = pc.dev(z, 1 - x, y, c), pc.dev(z, x, 1 - y, c), pc.dev(z, x, y, 1 - c)
+    rels = [(0, x, y)]
+    if ux:
+        rels.append((1, 1 - x, y))
+    if uy:
+        rels.append((2, x, 1 - y))
+    if ux and uy:
+        rels.append((3, 1 - x, 1 - y))
+    plane = nz * 4 * 3
+
+    def hf(ref, h):
+        return ref.at[pl.ds(h * half, half)]
+
+    def rcopy(src, dst, sidx, ridx, device):
+        return pltpu.make_async_remote_copy(
+            src_ref=src,
+            dst_ref=dst,
+            send_sem=ssem.at[sidx],
+            recv_sem=rsem.at[ridx],
+            device_id=device,
+            device_id_type=MESH_ID,
+        )
+
+    def load(s, rel, px, py):
+        return pltpu.make_async_copy(
+            p_ref.at[pc.blk(s, px, py, c), pl.ds(lo, rows)], acc.at[s * 4 + rel], lsem.at[s * 4 + rel]
+        )
+
+    def give(s, rel, px, py):
+        at = s * 4 + rel
+        return rcopy(p_ref.at[pc.blk(s, px, py, 1 - c), pl.ds(lo, rows)], rc.at[at], at, at, to_c)
+
+    def hop(s, rel, up, final):
+        extra = final and not up
+        return rcopy(
+            acc.at[s * 4 + rel],
+            rz.at[nz * 4 + rel] if extra else rz.at[s * 4 + rel],
+            nz * 4 + s * 4 + rel,
+            (nz * 8 + s * 4 + rel) if extra else (nz * 4 + s * 4 + rel),
+            pc.dev(z + (1 if up else -1), x, y, c),
+        )
+
+    def fold(dst, at, n, srcs):
+        def body(i, _):
+            r = pl.multiple_of(i * chunk, chunk)
+            total = dst[pl.ds(pl.multiple_of(at + r, chunk), chunk), :].astype(f32)
+            for ref, first in srcs:
+                total = total + ref[pl.ds(pl.multiple_of(first + r, chunk), chunk), :].astype(f32)
+            dst[pl.ds(pl.multiple_of(at + r, chunk), chunk), :] = total.astype(dst.dtype)
+            return 0
+
+        lax.fori_loop(0, n // chunk, body, 0)
+
+    def mine(rel):
+        return acc.at[z * 4 + rel]
+
+    def over_a():
+        return rcopy(hf(mine(3), 0), ra.at[0], nz * 8, plane, to_y)
+
+    def over_b():
+        return rcopy(hf(mine(3), 1), rb.at[0], nz * 8 + 1, plane + 1, to_x)
+
+    def x_half(h):
+        return rcopy(hf(mine(1), h), hf(rx.at[0], h), nz * 8 + 2 + h, plane + 2 + h, to_x)
+
+    def y_half(h):
+        return rcopy(hf(mine(2), h), hf(ry.at[0], h), nz * 8 + 4 + h, plane + 4 + h, to_y)
+
+    steps = list(reversed(pc.line_steps()))
+
+    def begin():
+        for d, side, s, ok in steps:
+
+            def fn():
+                for rel, px, py in reversed(rels):
+                    load(s, rel, px, py).start()
+                    if uc:
+                        give(s, rel, px, py).start()
+
+            when(ok, fn)
+
+    def line(step):
+        d, side, s, ok = step
+
+        def fn():
+            more = (z + 1 < nz) if side == 0 else (z >= 1)
+            for rel, px, py in reversed(rels):
+                load(s, rel, px, py).wait()
+                srcs = []
+                if uc:
+                    give(s, rel, px, py).wait_recv()
+                    srcs = [(rc.at[s * 4 + rel], 0)]
+                target = acc.at[s * 4 + rel]
+                if d > 0:
+
+                    @pl.when(more)
+                    def _():
+                        hop(s, rel, side == 1, False).wait_recv()
+                        fold(target, 0, rows, srcs + [(rz.at[s * 4 + rel], 0)])
+
+                    if srcs:
+
+                        @pl.when(jnp.logical_not(more))
+                        def _():
+                            fold(target, 0, rows, srcs)
+
+                    hop(s, rel, side == 1, d == 1).start()
+                else:
+                    lower, upper = (rz.at[s * 4 + rel], 0), (rz.at[nz * 4 + rel], 0)
+
+                    @pl.when(z >= 1)
+                    def _():
+                        hop(s, rel, True, True).wait_recv()
+
+                    @pl.when(z + 1 < nz)
+                    def _():
+                        hop(s, rel, False, True).wait_recv()
+
+                    both = jnp.logical_and(z >= 1, z + 1 < nz)
+                    pl.when(both)(lambda: fold(target, 0, rows, srcs + [lower, upper]))
+                    pl.when(z == 0)(lambda: fold(target, 0, rows, srcs + [upper]))
+                    pl.when(z == nz - 1)(lambda: fold(target, 0, rows, srcs + [lower]))
+                    if rel == 3:
+                        over_a().start()
+                        over_b().start()
+                    if rel == 2:
+                        y_half(0).start()
+                        if not ux:
+                            y_half(1).start()
+                    if rel == 1:
+                        x_half(1).start()
+                        if not uy:
+                            x_half(0).start()
+
+        when(ok, fn)
+
+    def cross():
+        if ux and uy:
+            over_a().wait_recv()
+            fold(mine(1), 0, half, [(ra.at[0], 0)])
+            x_half(0).start()
+            over_b().wait_recv()
+            fold(mine(2), half, half, [(rb.at[0], 0)])
+            y_half(1).start()
+
+    def total():
+        srcs = []
+        if ux:
+            x_half(0).wait_recv()
+            x_half(1).wait_recv()
+            srcs.append(rx)
+        if uy:
+            y_half(0).wait_recv()
+            y_half(1).wait_recv()
+            srcs.append(ry)
+
+        def body(i, _):
+            r = pl.multiple_of(i * chunk, chunk)
+            value = acc[z * 4, pl.ds(r, chunk), :].astype(f32)
+            for ref in srcs:
+                value = value + ref[0, pl.ds(r, chunk), :].astype(f32)
+            o_ref[pl.ds(pl.multiple_of(lo + i * chunk, chunk), chunk), :] = value.astype(o_ref.dtype)
+            return 0
+
+        lax.fori_loop(0, rows // chunk, body, 0)
+
+    groups = [[st for st in steps if st[0] == d] for d in reversed(range(nz))]
+
+    def phase(t):
+        if t < nz:
+            for st in groups[t]:
+                line(st)
+        elif t == nz:
+            cross()
+        else:
+            total()
+
+    def last():
+        for d, side, s, ok in steps:
+
+            def fn():
+                for rel, px, py in rels:
+                    if uc:
+                        give(s, rel, px, py).wait_send()
+                    if d > 0:
+                        hop(s, rel, side == 1, d == 1).wait_send()
+
+            when(ok, fn)
+        if ux and uy:
+            over_a().wait_send()
+            over_b().wait_send()
+        if ux:
+            x_half(0).wait_send()
+            x_half(1).wait_send()
+        if uy:
+            y_half(0).wait_send()
+            y_half(1).wait_send()
+
+    return begin, [functools.partial(phase, t) for t in range(nz + 2)], last
 
 
 LOG2E = 1.4426950408889634
@@ -1023,6 +1360,180 @@
     )
 
 
+def picks_of(slots, capacity):
+    return lax.broadcasted_iota(jnp.int32, (capacity, slots.shape[1]), 0) == slots
+
+
+def expert_forward_kernel(
+    capacity, slot_ref, weight_ref, x_ref, c_ref, gate_ref, up_ref, down_ref,
+    rows_ref, cot_ref, gate_out, up_out, parts_ref, wc_ref, w_sc, cot_sc,
+):
+    f32, bf16 = jnp.float32, jnp.bfloat16
+    devices = x_ref.shape[0]
+    for d in range(devices):
+        pick = picks_of(slot_ref[d : d + 1, :], capacity)
+        low = pick.astype(bf16)
+        at = slice(d * capacity, (d + 1) * capacity)
+        rows_ref[at, :] = jnp.dot(low, x_ref[d], preferred_element_type=f32).astype(bf16)
+        cot_sc[at, :] = jnp.dot(low, c_ref[d], preferred_element_type=f32).astype(bf16)
+        w_sc[at, :] = jnp.sum(
+            jnp.where(pick, weight_ref[d : d + 1, :], 0.0), axis=1, keepdims=True
+        )
+    rows = rows_ref[...]
+    gate = jnp.dot(rows, gate_ref[...], preferred_element_type=f32)
+    gate_out[...] = gate
+    up = jnp.dot(rows, up_ref[...], preferred_element_type=f32)
+    up_out[...] = up
+    activation = (gate * jax.nn.sigmoid(gate) * up).astype(bf16)
+    produced = jnp.dot(activation, down_ref[...], preferred_element_type=f32).astype(bf16)
+    for d in range(devices):
+        pick = picks_of(slot_ref[d : d + 1, :], capacity)
+        at = slice(d * capacity, (d + 1) * capacity)
+        cot = cot_sc[at, :].astype(f32)
+        made = produced[at, :].astype(f32)
+        weight = w_sc[at, :]
+        share = jnp.sum(cot * made, axis=1, keepdims=True)
+        wc_ref[d : d + 1, :] = jnp.sum(jnp.where(pick, share, 0.0), axis=0, keepdims=True)
+        cot_ref[at, :] = (weight * cot).astype(bf16)
+        parts_ref[d] = lax.dot_general(
+            pick.astype(bf16),
+            (weight * made).astype(bf16),
+            (((0,), (0,)), ((), ())),
+            preferred_element_type=f32,
+        ).astype(bf16)
+
+
+def expert_forward(slots, weights, tokens_all, cot_all, gate_w, up_w, down_w, capacity, per_step):
+    f32, bf16 = jnp.float32, jnp.bfloat16
+    devices, tokens, width = tokens_all.shape
+    hidden = gate_w.shape[1]
+    rows = per_step * capacity
+    lead = lambda *shape: pl.BlockSpec(shape, lambda i: (i,) + (0,) * (len(shape) - 1))
+    fixed = lambda a: pl.BlockSpec(a.shape, lambda i: (0, 0), pipeline_mode=pl.Buffered(1))
+    total = devices * capacity
+    return pl.pallas_call(
+        functools.partial(expert_forward_kernel, capacity),
+        grid=(devices // per_step,),
+        in_specs=[
+            lead(per_step, tokens),
+            lead(per_step, tokens),
+            lead(per_step, tokens, width),
+            lead(per_step, tokens, width),
+            fixed(gate_w),
+            fixed(up_w),
+            fixed(down_w),
+        ],
+        out_specs=[
+            lead(rows, width),
+            lead(rows, width),
+            lead(rows, hidden),
+            lead(rows, hidden),
+            lead(per_step, tokens, width),
+            lead(per_step, tokens),
+        ],
+        out_shape=[
+            jax.ShapeDtypeStruct((total, width), bf16),
+            jax.ShapeDtypeStruct((total, width), bf16),
+            jax.ShapeDtypeStruct((total, hidden), f32),
+            jax.ShapeDtypeStruct((total, hidden), f32),
+            jax.ShapeDtypeStruct((devices, tokens, width), bf16),
+            jax.ShapeDtypeStruct((devices, tokens), f32),
+        ],
+        scratch_shapes=[pltpu.VMEM((rows, 1), f32), pltpu.VMEM((rows, width), bf16)],
+        compiler_params=pltpu.CompilerParams(vmem_limit_bytes=62 * 1024 * 1024),
+        name="expert_forward",
+    )(slots, weights, tokens_all, cot_all, gate_w, up_w, down_w)
+
+
+def expert_back_kernel(
+    capacity, slot_ref, cot_ref, gate_pre, up_pre, gate_ref, up_ref, down_ref,
+    act_ref, gate_cot, up_cot, parts_ref,
+):
+    f32, bf16 = jnp.float32, jnp.bfloat16
+    devices = parts_ref.shape[0]
+    nt = (((1,), (1,)), ((), ()))
+    act_cot = lax.dot_general(cot_ref[...], down_ref[...], nt, preferred_element_type=f32)
+    gate, up = gate_pre[...], up_pre[...]
+    sigmoid = jax.nn.sigmoid(gate)
+    swish = gate * sigmoid
+    act_ref[...] = (swish * up).astype(bf16)
+    low_gate = (act_cot * up * sigmoid * (1.0 + gate * (1.0 - sigmoid))).astype(bf16)
+    low_up = (act_cot * swish).astype(bf16)
+    gate_cot[...] = low_gate
+    up_cot[...] = low_up
+    row_cot = lax.dot_general(low_gate, gate_ref[...], nt, preferred_element_type=f32)
+    row_cot = row_cot + lax.dot_general(low_up, up_ref[...], nt, preferred_element_type=f32)
+    row_cot = row_cot.astype(bf16)
+    for d in range(devices):
+        pick = picks_of(slot_ref[d : d + 1, :], capacity)
+        parts_ref[d] = lax.dot_general(
+            pick.astype(bf16),
+            row_cot[d * capacity : (d + 1) * capacity, :],
+            (((0,), (0,)), ((), ())),
+            preferred_element_type=f32,
+        ).astype(bf16)
+
+
+def expert_back(slots, route_cot, gate_pre, up_pre, gate_w, up_w, down_w, capacity, per_step):
+    bf16 = jnp.bfloat16
+    devices, tokens = slots.shape
+    width, hidden = gate_w.shape
+    rows = per_step * capacity
+    lead = lambda *shape: pl.BlockSpec(shape, lambda i: (i,) + (0,) * (len(shape) - 1))
+    fixed = lambda a: pl.BlockSpec(a.shape, lambda i: (0, 0), pipeline_mode=pl.Buffered(1))
+    total = devices * capacity
+    return pl.pallas_call(
+        functools.partial(expert_back_kernel, capacity),
+        grid=(devices // per_step,),
+        in_specs=[
+            lead(per_step, tokens),
+            lead(rows, width),
+            lead(rows, hidden),
+            lead(rows, hidden),
+            fixed(gate_w),
+            fixed(up_w),
+            fixed(down_w),
+        ],
+        out_specs=[
+            lead(rows, hidden),
+            lead(rows, hidden),
+            lead(rows, hidden),
+            lead(per_step, tokens, width),
+        ],
+        out_shape=[
+            jax.ShapeDtypeStruct((total, hidden), bf16),
+            jax.ShapeDtypeStruct((total, hidden), bf16),
+            jax.ShapeDtypeStruct((total, hidden), bf16),
+            jax.ShapeDtypeStruct((devices, tokens, width), bf16),
+        ],
+        compiler_params=pltpu.CompilerParams(vmem_limit_bytes=60 * 1024 * 1024),
+        name="expert_back",
+    )(slots, route_cot, gate_pre, up_pre, gate_w, up_w, down_w)
+
+
+def product_kernel(a_ref, *refs):
+    n = len(refs) // 2
+    for b_ref, o_ref in zip(refs[:n], refs[n:]):
+        o_ref[0] = lax.dot_general(
+            a_ref[...], b_ref[...], (((0,), (0,)), ((), ())), preferred_element_type=jnp.float32
+        )
+
+
+def column_products(a, others, block):
+    rows, k = a.shape
+    return pl.pallas_call(
+        product_kernel,
+        grid=(k // block,),
+        in_specs=[pl.BlockSpec((rows, block), lambda i: (0, i))]
+        + [
+            pl.BlockSpec(b.shape, lambda i: (0, 0), pipeline_mode=pl.Buffered(1)) for b in others
+        ],
+        out_specs=[pl.BlockSpec((1, block, b.shape[1]), lambda i: (0, i, 0)) for b in others],
+        out_shape=[jax.ShapeDtypeStruct((1, k, b.shape[1]), jnp.float32) for b in others],
+        compiler_params=pltpu.CompilerParams(vmem_limit_bytes=60 * 1024 * 1024),
+    )(a, *others)
+
+
 def own_kernels():
     return lax.axis_size("ctx") == 8 and lax.axis_size("wsh") == 4
 
@@ -1032,13 +1543,13 @@
 
 def gather(shards, axes_list, ident):
     if own_kernels():
-        return all_gather(shards, axes_list, ident)
+        return transfer(["gather"] * len(shards), shards, axes_list, ident)
     return [lax.all_gather(x, AXIS_NAMES[axes], axis=0) for x, axes in zip(shards, axes_list)]
 
 
 def scatter(parts, axes_list, ident):
     if own_kernels():
-        return reduce_scatter(parts, axes_list, ident)
+        return transfer(["scatter"] * len(parts), parts, axes_list, ident)
     return [
         lax.psum_scatter(x, AXIS_NAMES[axes], scatter_dimension=0, tiled=False).astype(jnp.float32)
         for x, axes in zip(parts, axes_list)
@@ -1051,6 +1562,61 @@
 
 def to_everyone(value, device_count):
     return exchange(jnp.broadcast_to(value[None], (device_count,) + value.shape))
+
+
+def experts_plain(
+    slot_mine, weight_mine, moe_all, cot_all, gate_w, up_w, down_w, capacity
+):
+    f32, bf16 = jnp.float32, jnp.bfloat16
+    device_count, _, width = moe_all.shape
+    picks = slot_mine[:, None, :] == jnp.arange(capacity, dtype=jnp.int32)[None, :, None]
+    picks_low = picks.astype(bf16)
+    slot_weight = jnp.sum(jnp.where(picks, weight_mine[:, None, :], 0.0), axis=-1)
+
+    def take(everyone):
+        return (
+            jnp.einsum("dct,dtw->dcw", picks_low, everyone, preferred_element_type=f32)
+            .astype(bf16)
+            .reshape(device_count * capacity, width)
+        )
+
+    def put(rows):
+        return jnp.einsum(
+            "dct,dcw->dtw",
+            picks_low,
+            rows.reshape(device_count, capacity, width),
+            preferred_element_type=f32,
+        ).astype(bf16)
+
+    rows_in = take(moe_all)
+    cot_rows = take(cot_all).astype(f32)
+    weight_rows = slot_weight.reshape(device_count * capacity, 1)
+    route_cot = (weight_rows * cot_rows).astype(bf16)
+    gate_pre = jnp.dot(rows_in, gate_w, preferred_element_type=f32)
+    up_pre = jnp.dot(rows_in, up_w, preferred_element_type=f32)
+    sigmoid = jax.nn.sigmoid(gate_pre)
+    swish = gate_pre * sigmoid
+    activation = (swish * up_pre).astype(bf16)
+    produced = jnp.dot(activation, down_w, preferred_element_type=f32).astype(bf16).astype(f32)
+    out_parts = put((weight_rows * produced).astype(bf16))
+    slot_cot = jnp.sum(cot_rows * produced, axis=-1).reshape(device_count, capacity)
+    cot_mine = jnp.sum(jnp.where(picks, slot_cot[:, :, None], 0.0), axis=1)
+    down_grad = jnp.einsum("rf,rd->fd", activation, route_cot, preferred_element_type=f32)
+    act_cot = jnp.einsum("rd,fd->rf", route_cot, down_w, preferred_element_type=f32)
+    gate_cot = (act_cot * up_pre * sigmoid * (1.0 + gate_pre * (1.0 - sigmoid))).astype(bf16)
+    up_cot = (act_cot * swish).astype(bf16)
+    gate_grad = jnp.einsum("rd,rf->df", rows_in, gate_cot, preferred_element_type=f32)
+    up_grad = jnp.einsum("rd,rf->df", rows_in, up_cot, preferred_element_type=f32)
+    row_cot = jnp.einsum("rf,df->rd", gate_cot, gate_w, preferred_element_type=f32)
+    row_cot = row_cot + jnp.einsum("rf,df->rd", up_cot, up_w, preferred_element_type=f32)
+    return (
+        out_parts,
+        cot_mine,
+        put(row_cot.astype(bf16)),
+        gate_grad[None],
+        up_grad[None],
+        down_grad[None],
+    )
 
 
 def local(
@@ -1143,70 +1709,38 @@
     routing = exchange(jnp.stack([slot_dense.astype(f32).T, weight_dense.T], axis=1))
     slot_mine = routing[:, 0, :].astype(jnp.int32)
     weight_mine = routing[:, 1, :]
-    picks = slot_mine[:, None, :] == jnp.arange(capacity, dtype=jnp.int32)[None, :, None]
-    picks_low = picks.astype(bf16)
-    slot_weight = jnp.sum(jnp.where(picks, weight_mine[:, None, :], 0.0), axis=-1)
-
-    def take(everyone):
-        return (
-            jnp.einsum("dct,dtw->dcw", picks_low, everyone, preferred_element_type=f32)
-            .astype(bf16)
-            .reshape(device_count * capacity, width)
+    gate_w, up_w, down_w = (expert_gate[0], expert_up[0], expert_down[0])
+    if capacity % 16 == 0:
+        per_step = 8
+        rows_in, route_cot, gate_pre, up_pre, out_parts, cot_mine = expert_forward(
+            slot_mine, weight_mine, moe_all, cot_all, gate_w, up_w, down_w, capacity, per_step
         )
-
-    def put(rows):
-        return jnp.einsum(
-            "dct,dcw->dtw",
-            picks_low,
-            rows.reshape(device_count, capacity, width),
-            preferred_element_type=f32,
-        ).astype(bf16)
-
-    gate_w, up_w, down_w = (expert_gate[0], expert_up[0], expert_down[0])
-    rows_in = take(moe_all)
-    cot_rows = take(cot_all).astype(f32)
-    weight_rows = slot_weight.reshape(device_count * capacity, 1)
-    route_cot = (weight_rows * cot_rows).astype(bf16)
-    gate_pre = jnp.dot(rows_in, gate_w, preferred_element_type=f32)
-    up_pre = jnp.dot(rows_in, up_w, preferred_element_type=f32)
-    sigmoid = jax.nn.sigmoid(gate_pre)
-    swish = gate_pre * sigmoid
-    activation = (swish * up_pre).astype(bf16)
-    produced = jnp.dot(activation, down_w, preferred_element_type=f32).astype(bf16).astype(f32)
-    out_parts = put((weight_rows * produced).astype(bf16))
-    slot_cot = jnp.sum(cot_rows * produced, axis=-1).reshape(device_count, capacity)
-    cot_mine = jnp.sum(jnp.where(picks, slot_cot[:, :, None], 0.0), axis=1)
+        activation, gate_cot, up_cot, row_parts = expert_back(
+            slot_mine, route_cot, gate_pre, up_pre, gate_w, up_w, down_w, capacity, per_step
+        )
+        gate_grad, up_grad = column_products(rows_in, [gate_cot, up_cot], 256)
+        (down_grad,) = column_products(activation, [route_cot], 256)
+    else:
+        out_parts, cot_mine, row_parts, gate_grad, up_grad, down_grad = experts_plain(
+            slot_mine, weight_mine, moe_all, cot_all, gate_w, up_w, down_w, capacity
+        )
     weight_cot = exchange(cot_mine).T
-    down_grad = jnp.einsum("rf,rd->fd", activation, route_cot, preferred_element_type=f32)
-    act_cot = jnp.einsum("rd,fd->rf", route_cot, down_w, preferred_element_type=f32)
-    gate_cot = (act_cot * up_pre * sigmoid * (1.0 + gate_pre * (1.0 - sigmoid))).astype(bf16)
-    up_cot = (act_cot * swish).astype(bf16)
-    gate_grad = jnp.einsum("rd,rf->df", rows_in, gate_cot, preferred_element_type=f32)
-    up_grad = jnp.einsum("rd,rf->df", rows_in, up_cot, preferred_element_type=f32)
-    row_cot = jnp.einsum("rf,df->rd", gate_cot, gate_w, preferred_element_type=f32)
-    row_cot = row_cot + jnp.einsum("rf,df->rd", up_cot, up_w, preferred_element_type=f32)
-    (row_sum,) = scatter([put(row_cot.astype(bf16))], [ALL_AXES], 6)
-    out_parts, row_sum = lax.optimization_barrier((out_parts, row_sum))
-    moe_sum = lax.psum_scatter(
-        out_parts, ("ctx", "wsh"), scatter_dimension=0, tiled=False
-    ).astype(f32)
 
     chosen_cot = weight_dense * (
         weight_cot - jnp.sum(weight_dense * weight_cot, axis=-1, keepdims=True)
     )
     logit_cot = chosen_cot.astype(bf16)
-    if device_count > 32:
-        router_grad = lax.psum(
-            jnp.einsum("td,te->de", moe_flat, logit_cot, preferred_element_type=f32),
-            ("ctx", "wsh"),
+    router_part = jnp.einsum("te,td->ed", logit_cot, moe_flat, preferred_element_type=f32)
+    if own_kernels():
+        row_sum, moe_sum, router_sum = scatter(
+            [row_parts, out_parts, router_part.reshape(device_count, -1, 128)],
+            [ALL_AXES, ALL_AXES, ALL_AXES],
+            6,
         )
     else:
-        router_grad = jnp.einsum(
-            "td,te->de",
-            moe_all.reshape(device_count * tokens, width),
-            to_everyone(logit_cot, device_count).reshape(device_count * tokens, expert_count),
-            preferred_element_type=f32,
-        )
+        row_sum, moe_sum = scatter([row_parts, out_parts], [ALL_AXES, ALL_AXES], 6)
+        router_grad = lax.psum(router_part, ("ctx", "wsh")).T
+    outputs = rows_first((residual + moe_sum).astype(bf16))
     normed_two_cot = (
         jnp.einsum("te,de->td", logit_cot, router, preferred_element_type=f32) + row_sum
     )
@@ -1218,6 +1752,12 @@
     (residual_flat,) = gather([residual_low], [WSH_AXES], 8)
     residual_flat = residual_flat.reshape(group_tokens, width)
 
+    out_grad = jnp.einsum("td,tc->dc", residual_flat, attention, preferred_element_type=f32).astype(
+        bf16
+    )
+    out_weight_grad = lax.psum_scatter(out_grad, "ctx", scatter_dimension=0, tiled=True)
+    out_weight_grad = out_weight_grad.astype(f32).T
+    residual_flat, _ = lax.optimization_barrier((residual_flat, out_grad))
     attention_cot = jnp.einsum(
         "td,dc->tc", residual_flat, out_full, preferred_element_type=f32
     ).astype(bf16)
@@ -1237,29 +1777,29 @@
         wsh_count,
         seq_count,
     )
-    out_grad = jnp.einsum("td,tc->dc", residual_flat, attention, preferred_element_type=f32).astype(
-        bf16
+    kv_sums, gate_grad, up_grad, down_grad = lax.optimization_barrier(
+        (kv_sums, gate_grad, up_grad, down_grad)
     )
-    out_grad, kv_sums = lax.optimization_barrier((out_grad, kv_sums))
-    out_weight_grad = lax.psum_scatter(out_grad, "ctx", scatter_dimension=0, tiled=True)
-    out_weight_grad = out_weight_grad.astype(f32).T
     (kv_cot,) = scatter([kv_sums], [CTX_AXES], 9)
     low, key_gain_grad = kv_back(
         projected, kv_cot, key_gain, cos2, sin2, low, heads_loc, wsh_count, seq_count
     )
     summed = jnp.einsum("tq,cq->tc", low, qkv_full, preferred_element_type=f32)
     qkv_grad = jnp.einsum("tc,tq->cq", normed_flat, low, preferred_element_type=f32).astype(bf16)
-    normed_cot, qkv_grad = scatter(
-        [
-            summed.astype(bf16).reshape(wsh_count, tokens, width),
-            qkv_grad.reshape(ctx_count, width // ctx_count, q_cols + 2 * kv_cols),
-        ],
-        [WSH_AXES, CTX_AXES],
-        10,
-    )
-    value_weight_grad = qkv_grad[:, q_cols + kv_cols :]
-    moe_sum, value_weight_grad = lax.optimization_barrier((moe_sum, value_weight_grad))
-    outputs = rows_first((residual + moe_sum).astype(bf16))
+    last_parts = [
+        summed.astype(bf16).reshape(wsh_count, tokens, width),
+        qkv_grad.reshape(ctx_count, width // ctx_count, q_cols + 2 * kv_cols),
+    ]
+    if own_kernels():
+        normed_cot, qkv_grad, router_all = transfer(
+            ["scatter", "scatter", "gather"],
+            last_parts + [router_sum],
+            [WSH_AXES, CTX_AXES, ALL_AXES],
+            10,
+        )
+        router_grad = router_all.reshape(expert_count, width).T
+    else:
+        normed_cot, qkv_grad = scatter(last_parts, [WSH_AXES, CTX_AXES], 10)
     input_norm_cot, norm_gain_grad = rms_backward(inputs_f, inverse_one, norm_gain, normed_cot)
     input_grad = rows_first(residual_cot + input_norm_cot)
     query_gain_grad = query_gain_grad.reshape(head_dim)
@@ -1272,15 +1812,15 @@
         gains[:width],
         qkv_grad[:, :q_cols],
         qkv_grad[:, q_cols : q_cols + kv_cols],
-        value_weight_grad,
+        qkv_grad[:, q_cols + kv_cols :],
         gains[2 * width : 2 * width + head_dim],
         gains[2 * width + head_dim :],
         out_weight_grad,
         gains[width : 2 * width],
         router_grad,
-        gate_grad[None],
-        up_grad[None],
-        down_grad[None],
+        gate_grad,
+        up_grad,
+        down_grad,
     )
 
 

time: 935 us -> 816 us (0.87)
  Pallas kernels: 549 us -> 697 us
  matrix products: 164 us -> 39.3 us
  waiting for transfers between devices: 98.5 us -> 10.2 us
  other arithmetic: 44 us -> 17.6 us
  starting transfers between devices: 31.7 us -> 12.7 us
    pallas_call x8 -> x12, Pallas kernels: 481 us -> 629 us  [the longest x8 538 us: transfer(): pl.pallas_call(functools.partial(transfer_kernel, kinds, axes_list), out_...]
    dot_general x14 -> x1, matrix products: 122 us -> 0.2 us  [local(): jnp.einsum('te,td->ed', logit_cot, moe_flat, preferred_element_type=f32)]
    reduce_scatter x1 -> x0, waiting for transfers between devices: 87.4 us -> none  [local(): lax.psum_scatter(out_parts, ('ctx', 'wsh'), scatter_dimension=0, tiled=Fa...]
    convert_element_type x4 -> x1, other arithmetic: 20 us -> 0.6 us  [local(): slot_mine = routing[:, 0, :].astype(jnp.int32)]
    all_to_all x4 -> x3, starting transfers between devices: 31.3 us -> 12.2 us  [exchange(): lax.all_to_all(pieces, ('ctx', 'wsh'), split_axis=0, concat_axis=0, tiled...]
  transfers between devices with their start and end apart: 8 -> 6, of which waited for: 2 -> 1; matrix products, arithmetic and copies ran while one was open for 19% -> 6% of each run, Pallas kernels for 46% -> 54%
where the time goes in v3:
time: 816 us; the launch traced here: 807 us
  Pallas kernels  697 us (85%)
  matrix products  39.3 us (5%)
  other arithmetic  17.6 us (2%)
  local copies, waits for them, and re-layouts  15.6 us (2%)
  between operations  14.9 us (2%)
  starting transfers between devices  12.7 us (2%)
  waiting for transfers between devices  10.2 us (1%)
    pallas_call x8, Pallas kernels, transfer(): pl.pallas_call(functools.partial(transfer_kernel, kinds, axes_list), out_...  538 us
    pallas_call x1, Pallas kernels, attend_back(): pl.pallas_call(functools.partial(attend_back_kernel, heads, pieces, seqs,...  35.5 us
    pallas_call x1, Pallas kernels, expert_forward(): pl.pallas_call(functools.partial(expert_forward_kernel, capacity), grid=(...  33.8 us
    pallas_call x1, Pallas kernels, expert_back(): pl.pallas_call(functools.partial(expert_back_kernel, capacity), grid=(dev...  31.7 us
    pallas_call x1, Pallas kernels, attend(): pl.pallas_call(functools.partial(attend_kernel, heads, pieces, seqs, hd *...  27.6 us
    pallas_call x2, Pallas kernels, column_products(): pl.pallas_call(product_kernel, grid=(k // block,), in_specs=[pl.BlockSpec...  25 us
  transfers between devices with their start and end apart: 6, of which 1 were waited for; matrix products, arithmetic and copies ran while one was open for 6% of the time, Pallas kernels for 54%

profile of v3, /device:TPU:0, one launch (start us, length us, event | category | flops | bytes accessed | tf_op | source)
XLA Modules:
  0.0 807.1 jit_solution(9931352714418028750)
XLA Ops:
  7.3 1.6 convert_bitcast_fusion
  8.9 1.7 fusion
  11.5 1.0 fusion.2.refs_0_
  12.4 0.9 pad_maximum_fusion.refs_1_
  13.3 64.3 %shard_map.272 = (bf16[4,128,2048]{2,1,0:T(8,128)(2,1)}, bf16[8,256,1280]{2,1,0:T(8,128)(2,1)}) custom-call(bf16[128,2048]{1,0:T(8,128)(2,1)} %fusion.2.refs_0_, bf16[256,1280]{1,0:T(8,128)(2,1)} %pad_maximum_fusion.refs_1_), custom_call_target="tpu_custom_call" | custom-call | tf_op jit(solution)/shard_map/pallas_call | solution.py:493
  78.4 0.8 pad_maximum_fusion.1.cos_ref
  79.2 0.8 pad_maximum_fusion.2.sin_ref
  80.0 7.5 fusion.31.proj_ref
  87.5 2.5 kv_prep.1.refs_0_
  89.9 49.3 %shard_map.273.kv_ref = bf16[8,512,256]{2,1,0:T(8,128)(2,1)} custom-call(bf16[512,256]{1,0:T(8,128)(2,1)} %kv_prep.1.refs_0_), custom_call_target="tpu_custom_call" | custom-call | tf_op jit(solution)/shard_map/pallas_call | solution.py:493
  139.9 1.0 copy-done.4
  140.9 0.8 bitcast_convert_fusion
  143.3 27.6 %attend.1 = (bf16[512,1024]{1,0:T(8,128)(2,1)}, f32[4,1,1024]{2,1,0:T(1,128)}, bf16[4,1024,128]{2,1,0:T(8,128)(2,1)}) custom-call(s32[16]{0:T(128)} %select_reduce_fusion.3.loc_ref, s32[2]{0:T(128)} %dynamic_slice.6.own_ref, f32[512,1280]{1,0:T(8,128)} %fusion.31.proj_ref, bf16[8,512,256]{2,1,0:T(8,128)(2,1)} %shard_map.273.kv_ref, f32[1,128]{1,0:T(1,128)} %bitcast.151, ...), custom_call_target="tpu_custom_call" | custom-call | tf_op jit(solution)/shard_map/attend/pallas_call | solution.py:1164
  171.0 6.2 convolution_convert_fusion.2
  177.2 18.0 %shard_map.274 = f32[128,2048]{1,0:T(8,128)} custom-call(bf16[4,128,2048]{2,1,0:T(8,128)(2,1)} %bitcast.135), custom_call_target="tpu_custom_call" | custom-call | tf_op jit(solution)/shard_map/pallas_call | solution.py:493
  195.2 1.4 multiply_reduce_fusion.2
  196.7 1.0 copy-done.2
  198.8 4.0 all-to-all-start
  202.8 129.0 %shard_map.275.x_ref = bf16[32,128,2048]{2,1,0:T(8,128)(2,1)} custom-call(bf16[128,2048]{1,0:T(8,128)(2,1)} %copy-done.6), custom_call_target="tpu_custom_call" | custom-call | tf_op jit(solution)/shard_map/pallas_call | solution.py:493
  333.1 33.8 %expert_forward.1 = (bf16[1536,2048]{1,0:T(8,128)(2,1)}, bf16[1536,2048]{1,0:T(8,128)(2,1)}, f32[1536,768]{1,0:T(8,128)}, f32[1536,768]{1,0:T(8,128)}, bf16[32,1...) custom-call(s32[32,128]{1,0:T(8,128)} %convert_bitcast_fusion.2.slot_ref, f32[32,128]{1,0:T(8,128)} %bitcast.147, ...), custom_call_target="tpu_custom_call" | custom-call | tf_op jit(solution)/shard_map/expert_forward/pallas_call | solution.py:1414
  366.8 4.6 all-to-all-start.1
  371.9 31.7 %expert_back.1 = (bf16[1536,768]{1,0:T(8,128)(2,1)}, bf16[1536,768]{1,0:T(8,128)(2,1)}, bf16[1536,768]{1,0:T(8,128)(2,1)}, bf16[32,128,2048]{2,1,0:T(8,128)(2,1)}) custom-call(s32[32,128]{1,0:T(8,128)} %convert_bitcast_fusion.2.slot_ref, bf16[1536,2048]{1,0:T(8,128)(2,1)} %get-tuple-element.58.cot_ref.refs_0_, f32[1536,768]{1,0:T(8,128)} %get-tuple-element.59.gate_pre, ...), custom_call_target="tpu_custom_call" | custom-call | tf_op jit(solution)/shard_map/expert_back/pallas_call | solution.py:1485
  403.8 0.8 copy.111
  404.6 140.3 %shard_map.276 = (f32[128,2048]{1,0:T(8,128)}, f32[128,2048]{1,0:T(8,128)}, f32[16,128]{1,0:T(8,128)}) custom-call(bf16[32,128,2048]{2,1,0:T(8,128)(2,1)} %get-tuple-element.61.refs_0_, bf16[32,128,2048]{2,1,0:T(8,128)(2,1)} %get-tuple-element.62.refs_1_, f32[32,16,128]{2,1,0:T(8,128)} %bitcast.138), custom_call_target="tpu_custom_call" | custom-call | tf_op jit(solution)/shard_map/pallas_call | solution.py:493
  544.9 1.9 multiply_reduce_fusion
  546.8 1.8 fusion.26
  548.6 19.2 %shard_map.277 = bf16[4,128,2048]{2,1,0:T(8,128)(2,1)} custom-call(bf16[128,2048]{1,0:T(8,128)(2,1)} %get-tuple-element.176.refs_0_), custom_call_target="tpu_custom_call" | custom-call | tf_op jit(solution)/shard_map/pallas_call | solution.py:493
  567.8 6.0 convolution_convert_fusion.1
  573.8 9.9 %shard_map.279 = f32[1,768,2048]{2,1,0:T(8,128)} custom-call(bf16[1536,768]{1,0:T(8,128)(2,1)} %get-tuple-element.75.a_ref, bf16[1536,2048]{1,0:T(8,128)(2,1)} %get-tuple-element.58.cot_ref.refs_0_), custom_call_target="tpu_custom_call" | custom-call | tf_op jit(solution)/shard_map/pallas_call | solution.py:1524
  583.7 15.1 %shard_map.278 = (f32[1,2048,768]{2,1,0:T(8,128)}, f32[1,2048,768]{2,1,0:T(8,128)}) custom-call(bf16[1536,2048]{1,0:T(8,128)(2,1)} %get-tuple-element.70.a_ref, bf16[1536,768]{1,0:T(8,128)(2,1)} %get-tuple-element.71.refs_0_, bf16[1536,768]{1,0:T(8,128)(2,1)} %get-tuple-element.72.refs_1_), custom_call_target="tpu_custom_call" | custom-call | tf_op jit(solution)/shard_map/pallas_call | solution.py:1524
  598.9 5.7 convolution_convert_fusion.4.cot_ref
  604.5 35.5 %attend_back.1 = (bf16[512,1280]{1,0:T(8,128)(2,1)}, bf16[8,512,256]{2,1,0:T(8,128)(2,1)}, f32[1,128]{1,0:T(1,128)}) custom-call(s32[16]{0:T(128)} %select_reduce_fusion.3.loc_ref, s32[2]{0:T(128)} %dynamic_slice.6.own_ref, f32[512,1280]{1,0:T(8,128)} %fusion.31.proj_ref, bf16[8,512,256]{2,1,0:T(8,128)(2,1)} %shard_map.273.kv_ref, ...), custom_call_target="tpu_custom_call" | custom-call | tf_op jit(solution)/shard_map/attend_back/pallas_call | solution.py:1319
  640.0 46.2 %shard_map.280.cot_ref = f32[512,256]{1,0:T(8,128)} custom-call(bf16[8,512,256]{2,1,0:T(8,128)(2,1)} %get-tuple-element.76.refs_0_), custom_call_target="tpu_custom_call" | custom-call | tf_op jit(solution)/shard_map/pallas_call | solution.py:493
  686.2 2.8 kv_back.1
  689.0 7.4 convolution_convert_fusion
  696.4 4.2 convolution_convert_fusion.3
  700.6 71.9 %shard_map.281 = (f32[128,2048]{1,0:T(8,128)}, f32[256,1280]{1,0:T(8,128)}, f32[32,16,128]{2,1,0:T(8,128)}) custom-call(bf16[4,128,2048]{2,1,0:T(8,128)(2,1)} %bitcast.136, bf16[8,256,1280]{2,1,0:T(8,128)(2,1)} %bitcast.131, f32[16,128]{1,0:T(8,128)} %get-tuple-element.79.refs_2_), custom_call_target="tpu_custom_call" | custom-call | tf_op jit(solution)/shard_map/pallas_call | solution.py:493
  772.5 1.7 fusion.8
  774.2 1.1 broadcast_in_dim.80
  775.3 3.6 all-to-all-start.2
  779.3 1.8 copy.117
  781.1 1.1 slice.30
  782.2 0.8 copy.119
  783.0 1.3 copy.118
  785.0 10.1 %all-to-all-done.2 = f32[32,1,4352]{2,1,0:T(1,128)} async-done(((f32[32,1,4352]{2,1,0:T(1,128)}), f32[32,1,4352]{2,1,0:T(1,128)}, u32[]{:S(2)}, u32[]{:S(2)}) %all-to-all-start.2) | async-done | bytes 557088 | tf_op jit(solution)/shard_map/all_to_all | solution.py:1560
  795.1 1.4 reduce_sum.119
  797.6 1.1 convert_bitcast_fusion.1
  798.8 1.3 copy.103
  (116 shorter events, 9.3 us)
Async XLA Ops:
  7.2 190.6 %copy-start = (bf16[2048,32]{0,1:T(8,128)(2,1)S(1)}, bf16[2048,32]{0,1:T(8,128)(2,1)}, u32[]{:S(2)}) copy-start(bf16[2048,32]{0,1:T(8,128)(2,1)} %param.27) | copy-start | bytes 393220
  7.2 4.3 copy-start.20
  7.2 163.8 %all-gather.4.cloned.1.call-start = ((), (), s32[]{:S(2)}) async-start(), calls=%async_computation.4 | async-start | bytes 4718592 | tf_op jit(solution)/shard_map/all_gather | solution.py:1678
  8.9 3.5 copy-start.17
  8.9 3.5 copy-start.21
  8.9 3.5 copy-start.22
  11.3 66.4 %copy-start.25 = (s32[8]{0:T(128)S(1)}, s32[8]{0:T(128)}, u32[]{:S(2)}) copy-start(s32[8]{0:T(128)} %param.18) | copy-start | bytes 100
  77.6 255.5 %all-gather.6.cloned.1.call-start = ((), (), s32[]{:S(2)}) async-start(), calls=%async_computation.6 | async-start | bytes 17301504 | tf_op jit(solution)/shard_map/all_gather | solution.py:1683
  87.5 51.8 %copy-start.15 = (f32[64,2,2048]{2,1,0:T(2,128)S(1)}, f32[64,2,2048]{2,1,0:T(2,128)}, u32[]{:S(2)}) copy-start(f32[64,2,2048]{2,1,0:T(2,128)} %param.33) | copy-start | bytes 3145732
  139.2 2.7 copy-start.23
  139.3 2.8 copy-start.24
  139.9 1.0 copy-start.4
  195.2 2.4 copy-start.19
  196.7 1.0 copy-start.2
  197.8 5.0 copy-start.6
  198.8 133.0 %all-to-all-start = ((f32[32,2,128]{2,1,0:T(2,128)}), f32[32,2,128]{2,1,0:T(2,128)S(1)}, u32[]{:S(2)}, u32[]{:S(2)}) async-start(f32[32,2,128]{2,1,0:T(2,128)} %copy.96), calls=%async_computation | async-start | bytes 65536 | tf_op jit(solution)/shard_map/all_to_all | solution.py:1560
  366.8 36.7 %all-to-all-start.1 = ((f32[32,1,128]{2,1,0:T(1,128)}), f32[32,1,128]{2,1,0:T(1,128)S(1)}, u32[]{:S(2)}, u32[]{:S(2)}) async-start(f32[32,1,128]{2,1,0:T(1,128)} %bitcast.149), calls=%async_computation.1 | async-start | bytes 32768 | tf_op jit(solution)/shard_map/all_to_all | solution.py:1560
  371.4 426.2 %reduce-scatter.2.cloned.1.call-start = ((), (), s32[]{:S(2)}) async-start(), calls=%async_computation.5 | async-start | bytes 4718592 | tf_op jit(solution)/shard_map/reduce_scatter | solution.py:1758
  371.8 31.7 %copy-start.7 = (bf16[128,2048]{1,0:T(8,128)(2,1)S(1)}, bf16[128,2048]{1,0:T(8,128)(2,1)}, u32[]{:S(2)}) copy-start(bf16[128,2048]{1,0:T(8,128)(2,1)} %copy-done.6) | copy-start | bytes 1572868
  404.6 140.3 %copy-start.3 = (f32[128,2048]{1,0:T(8,128)S(1)}, f32[128,2048]{1,0:T(8,128)}, u32[]{:S(2)}) copy-start(f32[128,2048]{1,0:T(8,128)} %copy-done.2) | copy-start | bytes 3145732
  544.8 1.9 copy-start.5
  544.9 1.9 copy-start.16
  548.6 19.2 %copy-start.14 = (bf16[512,1024]{1,0:T(8,128)(2,1)S(1)}, bf16[512,1024]{1,0:T(8,128)(2,1)}, u32[]{:S(2)}) copy-start(bf16[512,1024]{1,0:T(8,128)(2,1)} %get-tuple-element.55.attn_ref) | copy-start | bytes 3145732
  583.7 15.1 %copy-start.10 = (bf16[4,128,2048]{2,1,0:T(8,128)(2,1)S(1)}, bf16[4,128,2048]{2,1,0:T(8,128)(2,1)}, u32[]{:S(2)}) copy-start(bf16[4,128,2048]{2,1,0:T(8,128)(2,1)} %shard_map.277) | copy-start | bytes 6291460
  686.2 10.2 %slice-start = ((s8[5242880]{0:T(1024)(128)(4,1)}), s8[1048576]{0:T(1024)(128)(4,1)S(1)}, s32[]{:S(2)}) async-start(s8[5242880]{0:T(1024)(128)(4,1)} %bitcast.160), calls=%async_computation.7 | async-start | bytes 2097152
  689.0 7.4 copy-start.12
  689.0 7.4 slice-start.1
  700.6 73.6 %copy-start.26 = (f32[1,128]{1,0:T(1,128)S(1)}, f32[1,128]{1,0:T(1,128)}, u32[]{:S(2)}) copy-start(f32[1,128]{1,0:T(1,128)} %get-tuple-element.81) | copy-start | bytes 1540
  700.6 73.6 %copy-start.27 = (f32[1,128]{1,0:T(1,128)S(1)}, f32[1,128]{1,0:T(1,128)}, u32[]{:S(2)}) copy-start(f32[1,128]{1,0:T(1,128)} %get-tuple-element.82) | copy-start | bytes 1540
  772.5 6.5 copy-start.8
  772.5 6.5 copy-start.9
  775.3 19.8 %all-to-all-start.2 = ((f32[32,1,4352]{2,1,0:T(1,128)}), f32[32,1,4352]{2,1,0:T(1,128)}, u32[]{:S(2)}, u32[]{:S(2)}) async-start(f32[32,1,4352]{2,1,0:T(1,128)} %broadcast_in_dim.80), calls=%async_computation.2 | async-start | bytes 1114112 | tf_op jit(solution)/shard_map/all_to_all | solution.py:1560
  779.0 2.1 copy-start.13
  779.3 2.9 copy-start.18
  779.3 3.7 copy-start.11
  783.0 17.1 %copy-start.1 = (bf16[2048,32]{0,1:T(8,128)(2,1)S(1)}, bf16[2048,32]{0,1:T(8,128)(2,1)}, u32[]{:S(2)}) copy-start(bf16[2048,32]{0,1:T(8,128)(2,1)} %param.27) | copy-start | bytes 393220
Sparse Core Ops, SparseCore 0:
  77.7 88.1 all-gather.3
  169.3 159.6 all-gather.5
  574.0 98.9 reduce-scatter.1

commit v4 on v3

--- a/solution.py
+++ b/solution.py
@@ -1085,7 +1085,7 @@
     block = per_half * rows
     blocks = 2 * kv_ref.shape[0]
     pair = 2 * block
-    tile = 2 * block
+    tile = heads * block
     sort_blocks(loc_ref, kv_ref, ks, seqs, rows, pieces, hd, 0, blocks)
     sort_blocks(loc_ref, kv_ref, vs, seqs, rows, pieces, hd, hd, blocks)
     for seq in range(seqs):
@@ -1206,7 +1206,7 @@
     block = per_half * rows
     blocks = 2 * kv_ref.shape[0]
     pair = 2 * block
-    tile = 2 * block
+    tile = heads * block
     sort_blocks(loc_ref, kv_ref, ks, seqs, rows, pieces, hd, 0, blocks)
     sort_blocks(loc_ref, kv_ref, vs, seqs, rows, pieces, hd, hd, blocks)
     dk[...] = jnp.zeros_like(dk)
@@ -1364,59 +1364,70 @@
     return lax.broadcasted_iota(jnp.int32, (capacity, slots.shape[1]), 0) == slots
 
 
-def expert_forward_kernel(
+def expert_kernel(
     capacity, slot_ref, weight_ref, x_ref, c_ref, gate_ref, up_ref, down_ref,
-    rows_ref, cot_ref, gate_out, up_out, parts_ref, wc_ref, w_sc, cot_sc,
+    rows_ref, cot_ref, act_ref, gate_cot, up_cot, out_parts, row_parts, wc_ref, w_sc, cot_sc,
 ):
     f32, bf16 = jnp.float32, jnp.bfloat16
+    nt = (((1,), (1,)), ((), ()))
+    tn = (((0,), (0,)), ((), ()))
     devices = x_ref.shape[0]
+    picks = [picks_of(slot_ref[d], capacity) for d in range(devices)]
+    spans = [slice(d * capacity, (d + 1) * capacity) for d in range(devices)]
     for d in range(devices):
-        pick = picks_of(slot_ref[d : d + 1, :], capacity)
-        low = pick.astype(bf16)
-        at = slice(d * capacity, (d + 1) * capacity)
-        rows_ref[at, :] = jnp.dot(low, x_ref[d], preferred_element_type=f32).astype(bf16)
-        cot_sc[at, :] = jnp.dot(low, c_ref[d], preferred_element_type=f32).astype(bf16)
-        w_sc[at, :] = jnp.sum(
-            jnp.where(pick, weight_ref[d : d + 1, :], 0.0), axis=1, keepdims=True
+        low = picks[d].astype(bf16)
+        rows_ref[spans[d], :] = jnp.dot(low, x_ref[d], preferred_element_type=f32).astype(bf16)
+        cot_sc[spans[d], :] = jnp.dot(low, c_ref[d], preferred_element_type=f32).astype(bf16)
+        w_sc[spans[d], :] = jnp.sum(
+            jnp.where(picks[d], weight_ref[d], 0.0), axis=1, keepdims=True
         )
     rows = rows_ref[...]
     gate = jnp.dot(rows, gate_ref[...], preferred_element_type=f32)
-    gate_out[...] = gate
     up = jnp.dot(rows, up_ref[...], preferred_element_type=f32)
-    up_out[...] = up
-    activation = (gate * jax.nn.sigmoid(gate) * up).astype(bf16)
+    sigmoid = jax.nn.sigmoid(gate)
+    swish = gate * sigmoid
+    activation = (swish * up).astype(bf16)
+    act_ref[...] = activation
+    cot_ref[...] = (w_sc[...] * cot_sc[...].astype(f32)).astype(bf16)
+    act_cot = lax.dot_general(cot_ref[...], down_ref[...], nt, preferred_element_type=f32)
+    low_gate = (act_cot * up * sigmoid * (1.0 + gate * (1.0 - sigmoid))).astype(bf16)
+    low_up = (act_cot * swish).astype(bf16)
+    gate_cot[...] = low_gate
+    up_cot[...] = low_up
     produced = jnp.dot(activation, down_ref[...], preferred_element_type=f32).astype(bf16)
     for d in range(devices):
-        pick = picks_of(slot_ref[d : d + 1, :], capacity)
-        at = slice(d * capacity, (d + 1) * capacity)
-        cot = cot_sc[at, :].astype(f32)
-        made = produced[at, :].astype(f32)
-        weight = w_sc[at, :]
-        share = jnp.sum(cot * made, axis=1, keepdims=True)
-        wc_ref[d : d + 1, :] = jnp.sum(jnp.where(pick, share, 0.0), axis=0, keepdims=True)
-        cot_ref[at, :] = (weight * cot).astype(bf16)
-        parts_ref[d] = lax.dot_general(
-            pick.astype(bf16),
-            (weight * made).astype(bf16),
-            (((0,), (0,)), ((), ())),
+        made = produced[spans[d], :].astype(f32)
+        share = jnp.sum(cot_sc[spans[d], :].astype(f32) * made, axis=1, keepdims=True)
+        wc_ref[d] = jnp.sum(jnp.where(picks[d], share, 0.0), axis=0, keepdims=True)
+        out_parts[d] = lax.dot_general(
+            picks[d].astype(bf16),
+            (w_sc[spans[d], :] * made).astype(bf16),
+            tn,
             preferred_element_type=f32,
         ).astype(bf16)
-
-
-def expert_forward(slots, weights, tokens_all, cot_all, gate_w, up_w, down_w, capacity, per_step):
+    row_cot = lax.dot_general(low_gate, gate_ref[...], nt, preferred_element_type=f32)
+    row_cot = row_cot + lax.dot_general(low_up, up_ref[...], nt, preferred_element_type=f32)
+    row_cot = row_cot.astype(bf16)
+    for d in range(devices):
+        row_parts[d] = lax.dot_general(
+            picks[d].astype(bf16), row_cot[spans[d], :], tn, preferred_element_type=f32
+        ).astype(bf16)
+
+
+def expert_pass(slots, weights, tokens_all, cot_all, gate_w, up_w, down_w, capacity, per_step):
     f32, bf16 = jnp.float32, jnp.bfloat16
     devices, tokens, width = tokens_all.shape
     hidden = gate_w.shape[1]
     rows = per_step * capacity
+    total = devices * capacity
     lead = lambda *shape: pl.BlockSpec(shape, lambda i: (i,) + (0,) * (len(shape) - 1))
     fixed = lambda a: pl.BlockSpec(a.shape, lambda i: (0, 0), pipeline_mode=pl.Buffered(1))
-    total = devices * capacity
     return pl.pallas_call(
-        functools.partial(expert_forward_kernel, capacity),
+        functools.partial(expert_kernel, capacity),
         grid=(devices // per_step,),
         in_specs=[
-            lead(per_step, tokens),
-            lead(per_step, tokens),
+            lead(per_step, 1, tokens),
+            lead(per_step, 1, tokens),
             lead(per_step, tokens, width),
             lead(per_step, tokens, width),
             fixed(gate_w),
@@ -1428,87 +1439,25 @@
             lead(rows, width),
             lead(rows, hidden),
             lead(rows, hidden),
+            lead(rows, hidden),
             lead(per_step, tokens, width),
-            lead(per_step, tokens),
+            lead(per_step, tokens, width),
+            lead(per_step, 1, tokens),
         ],
         out_shape=[
             jax.ShapeDtypeStruct((total, width), bf16),
             jax.ShapeDtypeStruct((total, width), bf16),
-            jax.ShapeDtypeStruct((total, hidden), f32),
-            jax.ShapeDtypeStruct((total, hidden), f32),
-            jax.ShapeDtypeStruct((devices, tokens, width), bf16),
-            jax.ShapeDtypeStruct((devices, tokens), f32),
-        ],
-        scratch_shapes=[pltpu.VMEM((rows, 1), f32), pltpu.VMEM((rows, width), bf16)],
-        compiler_params=pltpu.CompilerParams(vmem_limit_bytes=62 * 1024 * 1024),
-        name="expert_forward",
-    )(slots, weights, tokens_all, cot_all, gate_w, up_w, down_w)
-
-
-def expert_back_kernel(
-    capacity, slot_ref, cot_ref, gate_pre, up_pre, gate_ref, up_ref, down_ref,
-    act_ref, gate_cot, up_cot, parts_ref,
-):
-    f32, bf16 = jnp.float32, jnp.bfloat16
-    devices = parts_ref.shape[0]
-    nt = (((1,), (1,)), ((), ()))
-    act_cot = lax.dot_general(cot_ref[...], down_ref[...], nt, preferred_element_type=f32)
-    gate, up = gate_pre[...], up_pre[...]
-    sigmoid = jax.nn.sigmoid(gate)
-    swish = gate * sigmoid
-    act_ref[...] = (swish * up).astype(bf16)
-    low_gate = (act_cot * up * sigmoid * (1.0 + gate * (1.0 - sigmoid))).astype(bf16)
-    low_up = (act_cot * swish).astype(bf16)
-    gate_cot[...] = low_gate
-    up_cot[...] = low_up
-    row_cot = lax.dot_general(low_gate, gate_ref[...], nt, preferred_element_type=f32)
-    row_cot = row_cot + lax.dot_general(low_up, up_ref[...], nt, preferred_element_type=f32)
-    row_cot = row_cot.astype(bf16)
-    for d in range(devices):
-        pick = picks_of(slot_ref[d : d + 1, :], capacity)
-        parts_ref[d] = lax.dot_general(
-            pick.astype(bf16),
-            row_cot[d * capacity : (d + 1) * capacity, :],
-            (((0,), (0,)), ((), ())),
-            preferred_element_type=f32,
-        ).astype(bf16)
-
-
-def expert_back(slots, route_cot, gate_pre, up_pre, gate_w, up_w, down_w, capacity, per_step):
-    bf16 = jnp.bfloat16
-    devices, tokens = slots.shape
-    width, hidden = gate_w.shape
-    rows = per_step * capacity
-    lead = lambda *shape: pl.BlockSpec(shape, lambda i: (i,) + (0,) * (len(shape) - 1))
-    fixed = lambda a: pl.BlockSpec(a.shape, lambda i: (0, 0), pipeline_mode=pl.Buffered(1))
-    total = devices * capacity
-    return pl.pallas_call(
-        functools.partial(expert_back_kernel, capacity),
-        grid=(devices // per_step,),
-        in_specs=[
-            lead(per_step, tokens),
-            lead(rows, width),
-            lead(rows, hidden),
-            lead(rows, hidden),
-            fixed(gate_w),
-            fixed(up_w),
-            fixed(down_w),
-        ],
-        out_specs=[
-            lead(rows, hidden),
-            lead(rows, hidden),
-            lead(rows, hidden),
-            lead(per_step, tokens, width),
-        ],
-        out_shape=[
             jax.ShapeDtypeStruct((total, hidden), bf16),
             jax.ShapeDtypeStruct((total, hidden), bf16),
             jax.ShapeDtypeStruct((total, hidden), bf16),
             jax.ShapeDtypeStruct((devices, tokens, width), bf16),
+            jax.ShapeDtypeStruct((devices, tokens, width), bf16),
+            jax.ShapeDtypeStruct((devices, 1, tokens), f32),
         ],
-        compiler_params=pltpu.CompilerParams(vmem_limit_bytes=60 * 1024 * 1024),
-        name="expert_back",
-    )(slots, route_cot, gate_pre, up_pre, gate_w, up_w, down_w)
+        scratch_shapes=[pltpu.VMEM((rows, 1), f32), pltpu.VMEM((rows, width), bf16)],
+        compiler_params=pltpu.CompilerParams(vmem_limit_bytes=62 * 1024 * 1024),
+        name="expert_pass",
+    )(slots, weights, tokens_all, cot_all, gate_w, up_w, down_w)
 
 
 def product_kernel(a_ref, *refs):
@@ -1674,13 +1623,12 @@
     normed_flat, qkv_full = gather([normed_f.astype(bf16), qkv_shard], [WSH_AXES, CTX_AXES], 1)
     normed_flat = normed_flat.reshape(group_tokens, width)
     qkv_full = qkv_full.reshape(width, q_cols + 2 * kv_cols)
-    out_shard, qkv_full = lax.optimization_barrier((out_weight.T, qkv_full))
-    out_full = lax.all_gather(out_shard, "ctx", axis=0, tiled=True)
+    out_full = lax.all_gather(out_weight.T, "ctx", axis=0, tiled=True)
+    cot_low, qkv_full = lax.optimization_barrier((cot_flat.astype(bf16), qkv_full))
+    cot_all = lax.all_gather(cot_low, ("ctx", "wsh"), axis=0)
     projected = jnp.dot(normed_flat, qkv_full, preferred_element_type=f32)
     kv_own = kv_prep(projected, key_gain, cos2, sin2, heads_loc, wsh_count, seq_count)
     (kv_all,) = gather([kv_own], [CTX_AXES], 3)
-    cot_low, kv_all = lax.optimization_barrier((cot_flat.astype(bf16), kv_all))
-    cot_all = lax.all_gather(cot_low, ("ctx", "wsh"), axis=0)
 
     attention, log_total, rotated = attend(
         projected, kv_all, query_gain, cos2, sin2, loc, own_blocks, heads_loc, wsh_count, seq_count
@@ -1711,13 +1659,20 @@
     weight_mine = routing[:, 1, :]
     gate_w, up_w, down_w = (expert_gate[0], expert_up[0], expert_down[0])
     if capacity % 16 == 0:
-        per_step = 8
-        rows_in, route_cot, gate_pre, up_pre, out_parts, cot_mine = expert_forward(
-            slot_mine, weight_mine, moe_all, cot_all, gate_w, up_w, down_w, capacity, per_step
+        rows_in, route_cot, activation, gate_cot, up_cot, out_parts, row_parts, cot_mine = (
+            expert_pass(
+                slot_mine[:, None],
+                weight_mine[:, None],
+                moe_all,
+                cot_all,
+                gate_w,
+                up_w,
+                down_w,
+                capacity,
+                8,
+            )
         )
-        activation, gate_cot, up_cot, row_parts = expert_back(
-            slot_mine, route_cot, gate_pre, up_pre, gate_w, up_w, down_w, capacity, per_step
-        )
+        cot_mine = cot_mine[:, 0]
         gate_grad, up_grad = column_products(rows_in, [gate_cot, up_cot], 256)
         (down_grad,) = column_products(activation, [route_cot], 256)
     else:
@@ -1729,6 +1684,7 @@
     chosen_cot = weight_dense * (
         weight_cot - jnp.sum(weight_dense * weight_cot, axis=-1, keepdims=True)
     )
+    out_parts, gate_grad, up_grad = lax.optimization_barrier((out_parts, gate_grad, up_grad))
     logit_cot = chosen_cot.astype(bf16)
     router_part = jnp.einsum("te,td->ed", logit_cot, moe_flat, preferred_element_type=f32)
     if own_kernels():
@@ -1777,9 +1733,7 @@
         wsh_count,
         seq_count,
     )
-    kv_sums, gate_grad, up_grad, down_grad = lax.optimization_barrier(
-        (kv_sums, gate_grad, up_grad, down_grad)
-    )
+    kv_sums, down_grad = lax.optimization_barrier((kv_sums, down_grad))
     (kv_cot,) = scatter([kv_sums], [CTX_AXES], 9)
     low, key_gain_grad = kv_back(
         projected, kv_cot, key_gain, cos2, sin2, low, heads_loc, wsh_count, seq_count

time: 816 us -> 776 us (0.951)
  Pallas kernels: 697 us -> 660 us
    pallas_call x8, Pallas kernels: 538 us -> 517 us  [transfer(): pl.pallas_call(functools.partial(transfer_kernel, kinds, axes_list), out_...]
    pallas_call x2 -> x1, Pallas kernels: 65.4 us -> 53.3 us  [expert_pass(): pl.pallas_call(functools.partial(expert_kernel, capacity), grid=(devices...]
  transfers between devices with their start and end apart: 6 -> 6, of which waited for: 1 -> 1; matrix products, arithmetic and copies ran while one was open for 6% -> 7% of each run, Pallas kernels for 54% -> 58%
where the time goes in v4:
time: 776 us; the launch traced here: 767 us
  Pallas kernels  660 us (85%)
  matrix products  39.3 us (5%)
  other arithmetic  17.2 us (2%)
  between operations  14.9 us (2%)
  local copies, waits for them, and re-layouts  14.6 us (2%)
  waiting for transfers between devices  10.8 us (1%)
  starting transfers between devices  10.3 us (1%)
    pallas_call x8, Pallas kernels, transfer(): pl.pallas_call(functools.partial(transfer_kernel, kinds, axes_list), out_...  517 us
    pallas_call x1, Pallas kernels, expert_pass(): pl.pallas_call(functools.partial(expert_kernel, capacity), grid=(devices...  53.3 us
    pallas_call x1, Pallas kernels, attend(): pl.pallas_call(functools.partial(attend_kernel, heads, pieces, seqs, hd *...  32.1 us
    pallas_call x1, Pallas kernels, attend_back(): pl.pallas_call(functools.partial(attend_back_kernel, heads, pieces, seqs,...  28 us
    pallas_call x2, Pallas kernels, column_products(): pl.pallas_call(product_kernel, grid=(k // block,), in_specs=[pl.BlockSpec...  25.1 us
  transfers between devices with their start and end apart: 6, of which 1 were waited for; matrix products, arithmetic and copies ran while one was open for 7% of the time, Pallas kernels for 58%

profile of v4, /device:TPU:0, one launch (start us, length us, event | category | flops | bytes accessed | tf_op | source)
XLA Modules:
  0.0 767.5 jit_solution(13268915819354102526)
XLA Ops:
  7.3 0.7 all-gather.4.cloned.1.call-update
  8.0 1.6 convert_bitcast_fusion
  11.1 1.8 copy.83
  13.0 0.9 pad_maximum_fusion.refs_1_
  13.9 0.9 fusion.2.refs_0_
  14.9 107.0 %shard_map.272 = (bf16[4,128,2048]{2,1,0:T(8,128)(2,1)}, bf16[8,256,1280]{2,1,0:T(8,128)(2,1)}) custom-call(bf16[128,2048]{1,0:T(8,128)(2,1)} %fusion.2.refs_0_, bf16[256,1280]{1,0:T(8,128)(2,1)} %pad_maximum_fusion.refs_1_), custom_call_target="tpu_custom_call" | custom-call | tf_op jit(solution)/shard_map/pallas_call | solution.py:493
  121.9 0.8 bitcast_convert_fusion
  123.6 0.8 pad_maximum_fusion.1.cos_ref
  124.4 0.8 pad_maximum_fusion.2.sin_ref
  125.1 7.5 fusion.30.proj_ref
  132.7 2.4 kv_prep.1.refs_0_
  135.1 51.1 %shard_map.273.kv_ref = bf16[8,512,256]{2,1,0:T(8,128)(2,1)} custom-call(bf16[512,256]{1,0:T(8,128)(2,1)} %kv_prep.1.refs_0_), custom_call_target="tpu_custom_call" | custom-call | tf_op jit(solution)/shard_map/pallas_call | solution.py:493
  187.8 32.1 %attend.1 = (bf16[512,1024]{1,0:T(8,128)(2,1)}, f32[4,1,1024]{2,1,0:T(1,128)}, bf16[4,1024,128]{2,1,0:T(8,128)(2,1)}) custom-call(s32[16]{0:T(128)} %select_reduce_fusion.3.loc_ref, s32[2]{0:T(128)} %dynamic_slice.6.own_ref, f32[512,1280]{1,0:T(8,128)} %fusion.30.proj_ref, bf16[8,512,256]{2,1,0:T(8,128)(2,1)} %shard_map.273.kv_ref, f32[1,128]{1,0:T(1,128)} %bitcast.134, ...), custom_call_target="tpu_custom_call" | custom-call | tf_op jit(solution)/shard_map/attend/pallas_call | solution.py:1164
  220.0 6.3 convolution_convert_fusion.2
  226.3 18.1 %shard_map.274 = f32[128,2048]{1,0:T(8,128)} custom-call(bf16[4,128,2048]{2,1,0:T(8,128)(2,1)} %bitcast.119), custom_call_target="tpu_custom_call" | custom-call | tf_op jit(solution)/shard_map/pallas_call | solution.py:493
  244.3 1.4 multiply_reduce_fusion.2
  245.8 1.0 copy-done.2
  247.9 2.6 all-to-all-start
  250.6 72.6 %shard_map.275.x_ref = bf16[32,128,2048]{2,1,0:T(8,128)(2,1)} custom-call(bf16[128,2048]{1,0:T(8,128)(2,1)} %copy-done.6), custom_call_target="tpu_custom_call" | custom-call | tf_op jit(solution)/shard_map/pallas_call | solution.py:493
  323.8 53.3 %expert_pass.1 = (bf16[1536,2048]{1,0:T(8,128)(2,1)}, bf16[1536,2048]{1,0:T(8,128)(2,1)}, bf16[1536,768]{1,0:T(8,128)(2,1)}, bf16[1536,768]{1,0:T(8,128)(2,1)}, ...) custom-call(s32[32,1,128]{2,1,0:T(1,128)} %get-tuple-element.178.slo, ...), custom_call_target="tpu_custom_call" | custom-call | tf_op jit(solution)/shard_map/expert_pass/pallas_call | solution.py:1425
  377.1 3.9 all-to-all-start.1
  381.1 15.1 %shard_map.276 = (f32[1,2048,768]{2,1,0:T(8,128)}, f32[1,2048,768]{2,1,0:T(8,128)}) custom-call(bf16[1536,2048]{1,0:T(8,128)(2,1)} %get-tuple-element.55.a_ref, bf16[1536,768]{1,0:T(8,128)(2,1)} %get-tuple-element.56.refs_0_, bf16[1536,768]{1,0:T(8,128)(2,1)} %get-tuple-element.57.refs_1_), custom_call_target="tpu_custom_call" | custom-call | tf_op jit(solution)/shard_map/pallas_call | solution.py:1473
  396.4 0.8 copy.95
  397.2 140.3 %shard_map.277 = (f32[128,2048]{1,0:T(8,128)}, f32[128,2048]{1,0:T(8,128)}, f32[16,128]{1,0:T(8,128)}) custom-call(bf16[32,128,2048]{2,1,0:T(8,128)(2,1)} %get-tuple-element.53.refs_0_, bf16[32,128,2048]{2,1,0:T(8,128)(2,1)} %get-tuple-element.60.refs_1_, f32[32,16,128]{2,1,0:T(8,128)} %bitcast.122), custom_call_target="tpu_custom_call" | custom-call | tf_op jit(solution)/shard_map/pallas_call | solution.py:493
  537.5 1.9 multiply_reduce_fusion
  539.4 1.8 fusion.25
  541.2 19.2 %shard_map.278 = bf16[4,128,2048]{2,1,0:T(8,128)(2,1)} custom-call(bf16[128,2048]{1,0:T(8,128)(2,1)} %get-tuple-element.170.refs_0_), custom_call_target="tpu_custom_call" | custom-call | tf_op jit(solution)/shard_map/pallas_call | solution.py:493
  560.4 6.0 convolution_convert_fusion.1
  566.5 10.0 %shard_map.279 = f32[1,768,2048]{2,1,0:T(8,128)} custom-call(bf16[1536,768]{1,0:T(8,128)(2,1)} %get-tuple-element.68.a_ref, bf16[1536,2048]{1,0:T(8,128)(2,1)} %get-tuple-element.69.refs_0_), custom_call_target="tpu_custom_call" | custom-call | tf_op jit(solution)/shard_map/pallas_call | solution.py:1473
  576.5 5.6 convolution_convert_fusion.4.cot_ref
  582.0 28.0 %attend_back.1 = (bf16[512,1280]{1,0:T(8,128)(2,1)}, bf16[8,512,256]{2,1,0:T(8,128)(2,1)}, f32[1,128]{1,0:T(1,128)}) custom-call(s32[16]{0:T(128)} %select_reduce_fusion.3.loc_ref, s32[2]{0:T(128)} %dynamic_slice.6.own_ref, f32[512,1280]{1,0:T(8,128)} %fusion.30.proj_ref, bf16[8,512,256]{2,1,0:T(8,128)(2,1)} %shard_map.273.kv_ref, ...), custom_call_target="tpu_custom_call" | custom-call | tf_op jit(solution)/shard_map/attend_back/pallas_call | solution.py:1319
  610.0 37.1 %shard_map.280.cot_ref = f32[512,256]{1,0:T(8,128)} custom-call(bf16[8,512,256]{2,1,0:T(8,128)(2,1)} %get-tuple-element.70.refs_0_), custom_call_target="tpu_custom_call" | custom-call | tf_op jit(solution)/shard_map/pallas_call | solution.py:493
  647.1 2.8 kv_back.1
  650.0 7.4 convolution_convert_fusion
  657.4 4.2 convolution_convert_fusion.3
  661.5 71.3 %shard_map.281 = (f32[128,2048]{1,0:T(8,128)}, f32[256,1280]{1,0:T(8,128)}, f32[32,16,128]{2,1,0:T(8,128)}) custom-call(bf16[4,128,2048]{2,1,0:T(8,128)(2,1)} %bitcast.120, bf16[8,256,1280]{2,1,0:T(8,128)(2,1)} %bitcast.112, f32[16,128]{1,0:T(8,128)} %get-tuple-element.73.refs_2_), custom_call_target="tpu_custom_call" | custom-call | tf_op jit(solution)/shard_map/pallas_call | solution.py:493
  732.9 1.7 fusion.8
  734.5 1.1 broadcast_in_dim.81
  735.6 3.6 all-to-all-start.2
  739.7 1.8 copy.101
  741.4 1.1 slice.30
  742.5 0.8 copy.103
  743.3 1.3 copy.102
  744.7 0.7 fusion.26
  745.4 10.1 %all-to-all-done.2 = f32[32,1,4352]{2,1,0:T(1,128)} async-done(((f32[32,1,4352]{2,1,0:T(1,128)}), f32[32,1,4352]{2,1,0:T(1,128)}, u32[]{:S(2)}, u32[]{:S(2)}) %all-to-all-start.2) | async-done | bytes 557088 | tf_op jit(solution)/shard_map/all_to_all | solution.py:1509
  755.5 1.4 reduce_sum.119
  758.0 1.1 convert_bitcast_fusion.1
  759.1 1.3 copy.89
  (113 shorter events, 7.6 us)
Async XLA Ops:
  7.2 239.7 %copy-start = (bf16[2048,32]{0,1:T(8,128)(2,1)S(1)}, bf16[2048,32]{0,1:T(8,128)(2,1)}, u32[]{:S(2)}) copy-start(bf16[2048,32]{0,1:T(8,128)(2,1)} %param.27) | copy-start | bytes 393220
  7.2 3.1 copy-start.11
  7.2 212.8 %all-gather.4.cloned.1.call-start = ((), (), s32[]{:S(2)}) async-start(), calls=%async_computation.4 | async-start | bytes 4718592 | tf_op jit(solution)/shard_map/all_gather | solution.py:1626
  7.9 315.8 %all-gather.6.cloned.1.call-start = ((), (), s32[]{:S(2)}) async-start(), calls=%async_computation.6 | async-start | bytes 17301504 | tf_op jit(solution)/shard_map/all_gather | solution.py:1628
  9.6 3.3 copy-start.17
  9.6 3.3 copy-start.21
  9.6 3.3 copy-start.22
  10.3 3.6 copy-start.20
  13.0 109.8 %copy-start.4 = (f32[2,64,2048]{2,1,0:T(8,128)}, f32[2,64,2048]{2,1,0:T(8,128)S(1)}, u32[]{:S(2)}) copy-start(f32[2,64,2048]{2,1,0:T(8,128)S(1)} %copy.83) | copy-start | bytes 3145732
  13.9 108.9 %copy-start.25 = (s32[8]{0:T(128)S(1)}, s32[8]{0:T(128)}, u32[]{:S(2)}) copy-start(s32[8]{0:T(128)} %param.18) | copy-start | bytes 100
  132.7 53.8 %copy-start.23 = (s32[64,2,8]{0,2,1:T(8,128)S(1)}, s32[64,2,8]{0,2,1:T(8,128)}, u32[]{:S(2)}) copy-start(s32[64,2,8]{0,2,1:T(8,128)} %param.31) | copy-start | bytes 12292
  132.7 53.8 %copy-start.24 = (s32[64,2,8]{0,2,1:T(8,128)S(1)}, s32[64,2,8]{0,2,1:T(8,128)}, u32[]{:S(2)}) copy-start(s32[64,2,8]{0,2,1:T(8,128)} %param.32) | copy-start | bytes 12292
  244.3 2.4 copy-start.19
  245.8 1.0 copy-start.2
  246.9 3.6 copy-start.6
  247.9 75.2 %all-to-all-start = ((f32[32,2,128]{2,1,0:T(2,128)}), f32[32,2,128]{2,1,0:T(2,128)S(1)}, u32[]{:S(2)}, u32[]{:S(2)}) async-start(f32[32,2,128]{2,1,0:T(2,128)} %pad_maximum_fusion.3), calls=%async_computation | async-start | bytes 65536 | tf_op jit(solution)/shard_map/all_to_all | solution.py:1509
  377.1 19.0 %all-to-all-start.1 = ((f32[32,1,128]{2,1,0:T(1,128)}), f32[32,1,128]{2,1,0:T(1,128)S(1)}, u32[]{:S(2)}, u32[]{:S(2)}) async-start(f32[32,1,128]{2,1,0:T(1,128)} %get-tuple-element.61), calls=%async_computation.1 | async-start | bytes 32768 | tf_op jit(solution)/shard_map/all_to_all | solution.py:1509
  381.0 376.9 %reduce-scatter.2.cloned.1.call-start = ((), (), s32[]{:S(2)}) async-start(), calls=%async_computation.5 | async-start | bytes 4718592 | tf_op jit(solution)/shard_map/reduce_scatter | solution.py:1714
  381.1 15.1 %copy-start.7 = (bf16[128,2048]{1,0:T(8,128)(2,1)S(1)}, bf16[128,2048]{1,0:T(8,128)(2,1)}, u32[]{:S(2)}) copy-start(bf16[128,2048]{1,0:T(8,128)(2,1)} %copy-done.6) | copy-start | bytes 1572868
  397.2 140.3 %copy-start.3 = (f32[128,2048]{1,0:T(8,128)S(1)}, f32[128,2048]{1,0:T(8,128)}, u32[]{:S(2)}) copy-start(f32[128,2048]{1,0:T(8,128)} %copy-done.2) | copy-start | bytes 3145732
  537.5 1.9 copy-start.5
  537.5 1.9 copy-start.16
  541.2 19.2 %copy-start.15 = (bf16[512,1024]{1,0:T(8,128)(2,1)S(1)}, bf16[512,1024]{1,0:T(8,128)(2,1)}, u32[]{:S(2)}) copy-start(bf16[512,1024]{1,0:T(8,128)(2,1)} %get-tuple-element.51.attn_ref) | copy-start | bytes 3145732
  566.5 10.0 %copy-start.10 = (bf16[4,128,2048]{2,1,0:T(8,128)(2,1)S(1)}, bf16[4,128,2048]{2,1,0:T(8,128)(2,1)}, u32[]{:S(2)}) copy-start(bf16[4,128,2048]{2,1,0:T(8,128)(2,1)} %shard_map.278) | copy-start | bytes 6291460
  647.1 10.2 %slice-start = ((s8[5242880]{0:T(1024)(128)(4,1)}), s8[1048576]{0:T(1024)(128)(4,1)S(1)}, s32[]{:S(2)}) async-start(s8[5242880]{0:T(1024)(128)(4,1)} %bitcast.143), calls=%async_computation.7 | async-start | bytes 2097152
  650.0 7.4 copy-start.13
  650.0 7.4 slice-start.1
  661.5 73.0 %copy-start.26 = (f32[1,128]{1,0:T(1,128)S(1)}, f32[1,128]{1,0:T(1,128)}, u32[]{:S(2)}) copy-start(f32[1,128]{1,0:T(1,128)} %get-tuple-element.75) | copy-start | bytes 1540
  661.5 73.0 %copy-start.27 = (f32[1,128]{1,0:T(1,128)S(1)}, f32[1,128]{1,0:T(1,128)}, u32[]{:S(2)}) copy-start(f32[1,128]{1,0:T(1,128)} %get-tuple-element.76) | copy-start | bytes 1540
  732.8 6.5 copy-start.8
  732.8 6.5 copy-start.9
  735.6 19.8 %all-to-all-start.2 = ((f32[32,1,4352]{2,1,0:T(1,128)}), f32[32,1,4352]{2,1,0:T(1,128)}, u32[]{:S(2)}, u32[]{:S(2)}) async-start(f32[32,1,4352]{2,1,0:T(1,128)} %broadcast_in_dim.81), calls=%async_computation.2 | async-start | bytes 1114112 | tf_op jit(solution)/shard_map/all_to_all | solution.py:1509
  739.3 2.1 copy-start.14
  739.6 2.9 copy-start.18
  739.6 3.7 copy-start.12
  743.3 17.1 %copy-start.1 = (bf16[2048,32]{0,1:T(8,128)(2,1)S(1)}, bf16[2048,32]{0,1:T(8,128)(2,1)}, u32[]{:S(2)}) copy-start(bf16[2048,32]{0,1:T(8,128)(2,1)} %param.27) | copy-start | bytes 393220
Sparse Core Ops, SparseCore 0:
  10.1 108.1 all-gather.3
  122.9 127.3 all-gather.5
  566.6 96.5 reduce-scatter.1

commit v5 on v4

--- a/solution.py
+++ b/solution.py
@@ -1614,13 +1614,14 @@
     ).astype(jnp.int32)
     own_blocks = lax.dynamic_slice_in_dim(blocks_by_loc, 2 * me_ctx, 2, 0)
 
-    inputs_f = inputs.transpose(1, 0, 2).reshape(tokens, width).astype(f32)
+    inputs_low = inputs.transpose(1, 0, 2).reshape(tokens, width)
+    inputs_f = inputs_low.astype(f32)
     cot_flat = cotangent.transpose(1, 0, 2).reshape(tokens, width)
     normed_f, inverse_one = rms_forward(inputs_f, norm_gain)
     q_cols, kv_cols = query_weight.shape[1], key_weight.shape[1]
     heads_loc = q_cols // head_dim
     qkv_shard = jnp.concatenate([query_weight, key_weight, value_weight], axis=1)
-    normed_flat, qkv_full = gather([normed_f.astype(bf16), qkv_shard], [WSH_AXES, CTX_AXES], 1)
+    qkv_full, normed_flat = gather([qkv_shard, normed_f.astype(bf16)], [CTX_AXES, WSH_AXES], 1)
     normed_flat = normed_flat.reshape(group_tokens, width)
     qkv_full = qkv_full.reshape(width, q_cols + 2 * kv_cols)
     out_full = lax.all_gather(out_weight.T, "ctx", axis=0, tiled=True)
@@ -1684,7 +1685,7 @@
     chosen_cot = weight_dense * (
         weight_cot - jnp.sum(weight_dense * weight_cot, axis=-1, keepdims=True)
     )
-    out_parts, gate_grad, up_grad = lax.optimization_barrier((out_parts, gate_grad, up_grad))
+    out_parts, down_grad = lax.optimization_barrier((out_parts, down_grad))
     logit_cot = chosen_cot.astype(bf16)
     router_part = jnp.einsum("te,td->ed", logit_cot, moe_flat, preferred_element_type=f32)
     if own_kernels():
@@ -1733,44 +1734,51 @@
         wsh_count,
         seq_count,
     )
-    kv_sums, down_grad = lax.optimization_barrier((kv_sums, down_grad))
+    kv_sums, gate_grad, up_grad = lax.optimization_barrier((kv_sums, gate_grad, up_grad))
     (kv_cot,) = scatter([kv_sums], [CTX_AXES], 9)
     low, key_gain_grad = kv_back(
         projected, kv_cot, key_gain, cos2, sin2, low, heads_loc, wsh_count, seq_count
     )
     summed = jnp.einsum("tq,cq->tc", low, qkv_full, preferred_element_type=f32)
     qkv_grad = jnp.einsum("tc,tq->cq", normed_flat, low, preferred_element_type=f32).astype(bf16)
-    last_parts = [
-        summed.astype(bf16).reshape(wsh_count, tokens, width),
-        qkv_grad.reshape(ctx_count, width // ctx_count, q_cols + 2 * kv_cols),
-    ]
+    summed = summed.astype(bf16).reshape(wsh_count, tokens, width)
+    qkv_grad = qkv_grad.reshape(ctx_count, width // ctx_count, q_cols + 2 * kv_cols)
+    query_gain_grad = query_gain_grad.reshape(head_dim)
+    key_gain_grad = key_gain_grad.reshape(head_dim)
+    early = jnp.concatenate([moe_gain_grad, query_gain_grad, key_gain_grad])
     if own_kernels():
-        normed_cot, qkv_grad, router_all = transfer(
+        lanes = 128
+        early = early.reshape(-1, lanes)
+        many = router_sum.shape[0]
+        small = jnp.pad(
+            jnp.concatenate([router_sum, early]), ((0, -(many + early.shape[0]) % 16), (0, 0))
+        )
+        qkv_grad, normed_cot, small = transfer(
             ["scatter", "scatter", "gather"],
-            last_parts + [router_sum],
-            [WSH_AXES, CTX_AXES, ALL_AXES],
+            [qkv_grad, summed, small],
+            [CTX_AXES, WSH_AXES, ALL_AXES],
             10,
         )
-        router_grad = router_all.reshape(expert_count, width).T
+        router_grad = small[:, :many].reshape(expert_count, width).T
+        early = jnp.sum(small[:, many : many + early.shape[0]], axis=0).reshape(-1)
     else:
-        normed_cot, qkv_grad = scatter(last_parts, [WSH_AXES, CTX_AXES], 10)
+        qkv_grad, normed_cot = scatter([qkv_grad, summed], [CTX_AXES, WSH_AXES], 10)
+        early = jnp.sum(to_everyone(early, device_count), axis=0)
     input_norm_cot, norm_gain_grad = rms_backward(inputs_f, inverse_one, norm_gain, normed_cot)
-    input_grad = rows_first(residual_cot + input_norm_cot)
-    query_gain_grad = query_gain_grad.reshape(head_dim)
-    key_gain_grad = key_gain_grad.reshape(head_dim)
-    gains = jnp.concatenate([norm_gain_grad, moe_gain_grad, query_gain_grad, key_gain_grad])
-    gains = jnp.sum(to_everyone(gains, device_count), axis=0)
+    norm_gain_grad = jnp.sum(to_everyone(norm_gain_grad, device_count), axis=0)
+    input_grad = residual_cot + input_norm_cot
+    input_grad = rows_first(input_grad)
     return (
         outputs,
         input_grad,
-        gains[:width],
+        norm_gain_grad,
         qkv_grad[:, :q_cols],
         qkv_grad[:, q_cols : q_cols + kv_cols],
         qkv_grad[:, q_cols + kv_cols :],
-        gains[2 * width : 2 * width + head_dim],
-        gains[2 * width + head_dim :],
+        early[width : width + head_dim],
+        early[width + head_dim :],
         out_weight_grad,
-        gains[width : 2 * width],
+        early[:width],
         router_grad,
         gate_grad,
         up_grad,

time: 776 us -> 782 us (level)
  Pallas kernels: 660 us -> 672 us
  waiting for transfers between devices: 10.8 us -> 2.09 us
    pallas_call x8, Pallas kernels: 517 us -> 529 us  [transfer(): pl.pallas_call(functools.partial(transfer_kernel, kinds, axes_list), out_...]
    all_to_all x3, waiting for transfers between devices: 10.1 us -> 1.35 us  [exchange(): lax.all_to_all(pieces, ('ctx', 'wsh'), split_axis=0, concat_axis=0, tiled...]
  transfers between devices with their start and end apart: 6 -> 6, of which waited for: 1 -> 1; matrix products, arithmetic and copies ran while one was open for 7% -> 8% of each run, Pallas kernels for 58% -> 59%
where the time goes in v5:
time: 782 us; the launch traced here: 773 us
  Pallas kernels  672 us (86%)
  matrix products  39.2 us (5%)
  other arithmetic  19 us (2%)
  local copies, waits for them, and re-layouts  15.3 us (2%)
  between operations  14.8 us (2%)
  starting transfers between devices  10.3 us (1%)
    pallas_call x8, Pallas kernels, transfer(): pl.pallas_call(functools.partial(transfer_kernel, kinds, axes_list), out_...  529 us
    pallas_call x1, Pallas kernels, expert_pass(): pl.pallas_call(functools.partial(expert_kernel, capacity), grid=(devices...  53.3 us
    pallas_call x1, Pallas kernels, attend(): pl.pallas_call(functools.partial(attend_kernel, heads, pieces, seqs, hd *...  32 us
    pallas_call x1, Pallas kernels, attend_back(): pl.pallas_call(functools.partial(attend_back_kernel, heads, pieces, seqs,...  28 us
    pallas_call x2, Pallas kernels, column_products(): pl.pallas_call(product_kernel, grid=(k // block,), in_specs=[pl.BlockSpec...  25.1 us
  transfers between devices with their start and end apart: 6, of which 1 were waited for; matrix products, arithmetic and copies ran while one was open for 8% of the time, Pallas kernels for 59%

profile of v5, /device:TPU:0, one launch (start us, length us, event | category | flops | bytes accessed | tf_op | source)
XLA Modules:
  0.0 773.0 jit_solution(14434570962128704841)
XLA Ops:
  8.0 1.6 convert_bitcast_fusion
  11.1 1.8 copy.83
  13.0 1.0 pad_maximum_fusion.refs_0_
  14.0 0.9 fusion.2.refs_1_
  14.9 107.0 %shard_map.272 = (bf16[8,256,1280]{2,1,0:T(8,128)(2,1)}, bf16[4,128,2048]{2,1,0:T(8,128)(2,1)}) custom-call(bf16[256,1280]{1,0:T(8,128)(2,1)} %pad_maximum_fusion.refs_0_, bf16[128,2048]{1,0:T(8,128)(2,1)} %fusion.2.refs_1_), custom_call_target="tpu_custom_call" | custom-call | tf_op jit(solution)/shard_map/pallas_call | solution.py:493
  121.9 0.8 bitcast_convert_fusion
  123.6 0.8 pad_maximum_fusion.1.cos_ref
  124.4 0.8 pad_maximum_fusion.2.sin_ref
  125.1 7.5 fusion.28.proj_ref
  132.7 2.4 kv_prep.1.refs_0_
  135.1 51.2 %shard_map.273.kv_ref = bf16[8,512,256]{2,1,0:T(8,128)(2,1)} custom-call(bf16[512,256]{1,0:T(8,128)(2,1)} %kv_prep.1.refs_0_), custom_call_target="tpu_custom_call" | custom-call | tf_op jit(solution)/shard_map/pallas_call | solution.py:493
  187.8 32.0 %attend.1 = (bf16[512,1024]{1,0:T(8,128)(2,1)}, f32[4,1,1024]{2,1,0:T(1,128)}, bf16[4,1024,128]{2,1,0:T(8,128)(2,1)}) custom-call(s32[16]{0:T(128)} %select_reduce_fusion.3.loc_ref, s32[2]{0:T(128)} %dynamic_slice.6.own_ref, f32[512,1280]{1,0:T(8,128)} %fusion.28.proj_ref, bf16[8,512,256]{2,1,0:T(8,128)(2,1)} %shard_map.273.kv_ref, f32[1,128]{1,0:T(1,128)} %bitcast.142, ...), custom_call_target="tpu_custom_call" | custom-call | tf_op jit(solution)/shard_map/attend/pallas_call | solution.py:1164
  220.0 6.2 convolution_convert_fusion.2
  226.2 17.9 %shard_map.274 = f32[128,2048]{1,0:T(8,128)} custom-call(bf16[4,128,2048]{2,1,0:T(8,128)(2,1)} %bitcast.127), custom_call_target="tpu_custom_call" | custom-call | tf_op jit(solution)/shard_map/pallas_call | solution.py:493
  244.2 1.5 multiply_reduce_fusion.2
  245.6 1.0 copy-done.2
  247.8 2.7 all-to-all-start
  250.5 72.6 %shard_map.275.x_ref = bf16[32,128,2048]{2,1,0:T(8,128)(2,1)} custom-call(bf16[128,2048]{1,0:T(8,128)(2,1)} %copy-done.6), custom_call_target="tpu_custom_call" | custom-call | tf_op jit(solution)/shard_map/pallas_call | solution.py:493
  323.7 53.3 %expert_pass.1 = (bf16[1536,2048]{1,0:T(8,128)(2,1)}, bf16[1536,2048]{1,0:T(8,128)(2,1)}, bf16[1536,768]{1,0:T(8,128)(2,1)}, bf16[1536,768]{1,0:T(8,128)(2,1)}, ...) custom-call(s32[32,1,128]{2,1,0:T(1,128)} %get-tuple-element.178.slo, ...), custom_call_target="tpu_custom_call" | custom-call | tf_op jit(solution)/shard_map/expert_pass/pallas_call | solution.py:1425
  377.0 3.9 all-to-all-start.1
  381.0 9.9 %shard_map.276 = f32[1,768,2048]{2,1,0:T(8,128)} custom-call(bf16[1536,768]{1,0:T(8,128)(2,1)} %get-tuple-element.55.a_ref, bf16[1536,2048]{1,0:T(8,128)(2,1)} %get-tuple-element.56.refs_0_), custom_call_target="tpu_custom_call" | custom-call | tf_op jit(solution)/shard_map/pallas_call | solution.py:1473
  391.2 0.8 copy.91
  392.0 140.3 %shard_map.277 = (f32[128,2048]{1,0:T(8,128)}, f32[128,2048]{1,0:T(8,128)}, f32[16,128]{1,0:T(8,128)}) custom-call(bf16[32,128,2048]{2,1,0:T(8,128)(2,1)} %get-tuple-element.53.refs_0_, bf16[32,128,2048]{2,1,0:T(8,128)(2,1)} %get-tuple-element.57.refs_1_, f32[32,16,128]{2,1,0:T(8,128)} %bitcast.130), custom_call_target="tpu_custom_call" | custom-call | tf_op jit(solution)/shard_map/pallas_call | solution.py:493
  532.3 1.9 multiply_reduce_fusion
  534.2 1.8 fusion.25
  536.0 19.2 %shard_map.278 = bf16[4,128,2048]{2,1,0:T(8,128)(2,1)} custom-call(bf16[128,2048]{1,0:T(8,128)(2,1)} %get-tuple-element.170.refs_0_), custom_call_target="tpu_custom_call" | custom-call | tf_op jit(solution)/shard_map/pallas_call | solution.py:493
  555.2 6.0 convolution_convert_fusion.1
  561.3 15.1 %shard_map.279 = (f32[1,2048,768]{2,1,0:T(8,128)}, f32[1,2048,768]{2,1,0:T(8,128)}) custom-call(bf16[1536,2048]{1,0:T(8,128)(2,1)} %get-tuple-element.65.a_ref, bf16[1536,768]{1,0:T(8,128)(2,1)} %get-tuple-element.66.refs_0_, bf16[1536,768]{1,0:T(8,128)(2,1)} %get-tuple-element.67.refs_1_), custom_call_target="tpu_custom_call" | custom-call | tf_op jit(solution)/shard_map/pallas_call | solution.py:1473
  576.4 5.5 convolution_convert_fusion.4.cot_ref
  581.9 28.0 %attend_back.1 = (bf16[512,1280]{1,0:T(8,128)(2,1)}, bf16[8,512,256]{2,1,0:T(8,128)(2,1)}, f32[1,128]{1,0:T(1,128)}) custom-call(s32[16]{0:T(128)} %select_reduce_fusion.3.loc_ref, s32[2]{0:T(128)} %dynamic_slice.6.own_ref, f32[512,1280]{1,0:T(8,128)} %fusion.28.proj_ref, bf16[8,512,256]{2,1,0:T(8,128)(2,1)} %shard_map.273.kv_ref, ...), custom_call_target="tpu_custom_call" | custom-call | tf_op jit(solution)/shard_map/attend_back/pallas_call | solution.py:1319
  610.0 49.6 %shard_map.280.cot_ref = f32[512,256]{1,0:T(8,128)} custom-call(bf16[8,512,256]{2,1,0:T(8,128)(2,1)} %get-tuple-element.70.refs_0_), custom_call_target="tpu_custom_call" | custom-call | tf_op jit(solution)/shard_map/pallas_call | solution.py:493
  659.7 2.8 kv_back.1
  663.8 7.3 convolution_convert_fusion
  671.1 4.2 convolution_convert_fusion.3
  675.3 70.8 %shard_map.281 = (f32[256,1280]{1,0:T(8,128)}, f32[128,2048]{1,0:T(8,128)}, f32[32,48,128]{2,1,0:T(8,128)}) custom-call(bf16[8,256,1280]{2,1,0:T(8,128)(2,1)} %bitcast.120, bf16[4,128,2048]{2,1,0:T(8,128)(2,1)} %bitcast.128, f32[48,128]{1,0:T(8,128)} %select_maximum_fusion.refs_2_), custom_call_target="tpu_custom_call" | custom-call | tf_op jit(solution)/shard_map/pallas_call | solution.py:493
  746.2 1.7 fusion.8
  747.8 0.8 broadcast_in_dim.81
  748.7 3.5 all-to-all-start.2
  752.2 1.0 slice_reduce_fusion
  754.1 1.0 slice.51
  755.1 1.8 copy.97
  756.9 1.1 slice.41
  758.0 0.8 copy.99
  758.8 1.3 copy.98
  761.4 1.3 all-to-all-done.2
  762.8 0.8 reduce_sum.128
  763.6 1.1 convert_bitcast_fusion.1
  764.7 1.3 copy.89
  (114 shorter events, 10.2 us)
Async XLA Ops:
  7.2 239.6 %copy-start = (bf16[2048,32]{0,1:T(8,128)(2,1)S(1)}, bf16[2048,32]{0,1:T(8,128)(2,1)}, u32[]{:S(2)}) copy-start(bf16[2048,32]{0,1:T(8,128)(2,1)} %param.27) | copy-start | bytes 393220
  7.2 3.1 copy-start.11
  7.2 212.8 %all-gather.4.cloned.1.call-start = ((), (), s32[]{:S(2)}) async-start(), calls=%async_computation.4 | async-start | bytes 4718592 | tf_op jit(solution)/shard_map/all_gather | solution.py:1627
  7.9 315.8 %all-gather.6.cloned.1.call-start = ((), (), s32[]{:S(2)}) async-start(), calls=%async_computation.6 | async-start | bytes 17301504 | tf_op jit(solution)/shard_map/all_gather | solution.py:1629
  9.6 3.3 copy-start.17
  9.6 3.3 copy-start.20
  9.6 3.3 copy-start.21
  10.3 3.7 copy-start.19
  13.0 109.8 %copy-start.4 = (f32[2,64,2048]{2,1,0:T(8,128)}, f32[2,64,2048]{2,1,0:T(8,128)S(1)}, u32[]{:S(2)}) copy-start(f32[2,64,2048]{2,1,0:T(8,128)S(1)} %copy.83) | copy-start | bytes 3145732
  13.9 108.9 %copy-start.25 = (s32[8]{0:T(128)S(1)}, s32[8]{0:T(128)}, u32[]{:S(2)}) copy-start(s32[8]{0:T(128)} %param.18) | copy-start | bytes 100
  132.7 53.8 %copy-start.22 = (s32[64,2,8]{0,2,1:T(8,128)S(1)}, s32[64,2,8]{0,2,1:T(8,128)}, u32[]{:S(2)}) copy-start(s32[64,2,8]{0,2,1:T(8,128)} %param.31) | copy-start | bytes 12292
  132.7 53.9 %copy-start.23 = (s32[64,2,8]{0,2,1:T(8,128)S(1)}, s32[64,2,8]{0,2,1:T(8,128)}, u32[]{:S(2)}) copy-start(s32[64,2,8]{0,2,1:T(8,128)} %param.32) | copy-start | bytes 12292
  244.2 2.4 copy-start.18
  245.6 1.0 copy-start.2
  246.8 3.7 copy-start.6
  247.8 75.3 %all-to-all-start = ((f32[32,2,128]{2,1,0:T(2,128)}), f32[32,2,128]{2,1,0:T(2,128)S(1)}, u32[]{:S(2)}, u32[]{:S(2)}) async-start(f32[32,2,128]{2,1,0:T(2,128)} %pad_maximum_fusion.3), calls=%async_computation | async-start | bytes 65536 | tf_op jit(solution)/shard_map/all_to_all | solution.py:1509
  377.0 13.9 %all-to-all-start.1 = ((f32[32,1,128]{2,1,0:T(1,128)}), f32[32,1,128]{2,1,0:T(1,128)S(1)}, u32[]{:S(2)}, u32[]{:S(2)}) async-start(f32[32,1,128]{2,1,0:T(1,128)} %get-tuple-element.58), calls=%async_computation.1 | async-start | bytes 32768 | tf_op jit(solution)/shard_map/all_to_all | solution.py:1509
  381.0 382.6 %reduce-scatter.2.cloned.1.call-start = ((), (), s32[]{:S(2)}) async-start(), calls=%async_computation.5 | async-start | bytes 4718592 | tf_op jit(solution)/shard_map/reduce_scatter | solution.py:1715
  381.0 10.0 %copy-start.7 = (bf16[128,2048]{1,0:T(8,128)(2,1)S(1)}, bf16[128,2048]{1,0:T(8,128)(2,1)}, u32[]{:S(2)}) copy-start(bf16[128,2048]{1,0:T(8,128)(2,1)} %copy-done.6) | copy-start | bytes 1572868
  392.0 140.3 %copy-start.3 = (f32[128,2048]{1,0:T(8,128)S(1)}, f32[128,2048]{1,0:T(8,128)}, u32[]{:S(2)}) copy-start(f32[128,2048]{1,0:T(8,128)} %copy-done.2) | copy-start | bytes 3145732
  532.3 1.9 copy-start.5
  532.3 1.9 copy-start.16
  536.0 19.2 %copy-start.15 = (bf16[512,1024]{1,0:T(8,128)(2,1)S(1)}, bf16[512,1024]{1,0:T(8,128)(2,1)}, u32[]{:S(2)}) copy-start(bf16[512,1024]{1,0:T(8,128)(2,1)} %get-tuple-element.51.attn_ref) | copy-start | bytes 3145732
  561.3 15.1 %copy-start.10 = (bf16[4,128,2048]{2,1,0:T(8,128)(2,1)S(1)}, bf16[4,128,2048]{2,1,0:T(8,128)(2,1)}, u32[]{:S(2)}) copy-start(bf16[4,128,2048]{2,1,0:T(8,128)(2,1)} %shard_map.278) | copy-start | bytes 6291460
  659.6 2.9 copy-start.26
  659.6 3.5 copy-start.24
  659.7 11.5 %slice-start = ((s8[5242880]{0:T(1024)(128)(4,1)}), s8[1048576]{0:T(1024)(128)(4,1)S(1)}, s32[]{:S(2)}) async-start(s8[5242880]{0:T(1024)(128)(4,1)} %bitcast.151), calls=%async_computation.7 | async-start | bytes 2097152
  663.8 7.3 copy-start.13
  663.8 7.3 slice-start.1
  746.1 7.1 copy-start.8
  746.2 7.1 copy-start.9
  748.7 14.1 %all-to-all-start.2 = ((f32[32,1,2048]{2,1,0:T(1,128)}), f32[32,1,2048]{2,1,0:T(1,128)S(1)}, u32[]{:S(2)}, u32[]{:S(2)}) async-start(f32[32,1,2048]{2,1,0:T(1,128)} %broadcast_in_dim.81), calls=%async_computation.2 | async-start | bytes 524288 | tf_op jit(solution)/shard_map/all_to_all | solution.py:1509
  753.6 3.3 copy-start.14
  755.1 3.7 copy-start.12
  758.8 7.2 copy-start.1
Sparse Core Ops, SparseCore 0:
  10.1 108.1 all-gather.3
  122.9 127.3 all-gather.5
  561.4 101.6 reduce-scatter.1
